TPU v7x, 128 devices: a whole 4x4x4 slice. The times are simulated.
128 devices in a mesh: fsdp: 8 (over z_hi, y), tp: 16 (over z_lo, x, core).
Axes of the slice: x: 4, y: 4, z: 4 (z_hi: 2, z_lo: 2; z = z_hi * 2 + z_lo), core: 2. Of those that a mesh axis runs over, the one named last changes fastest.
Arguments:
- tokens: bfloat16 [2048, 8192], P('fsdp', 'tp'), may hold values from -6 to 6
- out_grad: bfloat16 [2048, 8192], P('fsdp', 'tp'), may hold values from -6 to 6
- gate_weight: bfloat16 [8192, 2048], P('fsdp', 'tp'), may hold values from -0.0625 to 0.0625
- up_weight: bfloat16 [8192, 2048], P('fsdp', 'tp'), may hold values from -0.0625 to 0.0625
- down_weight: bfloat16 [2048, 8192], P('tp', 'fsdp'), may hold values from -0.125 to 0.125
Outputs:
- input_grad: bfloat16 [2048, 8192], P('fsdp', 'tp')
- gate_grad: float32 [8192, 2048], P('fsdp', 'tp')
- up_grad: float32 [8192, 2048], P('fsdp', 'tp')
- down_grad: float32 [2048, 8192], P('tp', 'fsdp')
All inputs are finite; a program needn't handle non-finite values.
Results may differ from a plain program's by a relative error of at most 0.0023.
Values may be sent and summed in bfloat16 or wider, within the bound.
A program may use at most 128 MiB of HBM per device.

v0:
```python
import functools
import math

import jax
import jax.numpy as jnp
from jax import lax
from jax.sharding import PartitionSpec as P
from jax.experimental import pallas as pl
from jax.experimental.pallas import tpu as pltpu

MESH = pl.DeviceIdType.MESH
F32 = jnp.float32
BF16 = jnp.bfloat16
VMEM_LIMIT = 60 * 1024 * 1024
CHUNKS = 4
AHEAD = 2
TILE = 512


def place(nf, nt):
    return lax.axis_index("fsdp"), lax.axis_index("tp")


def enter(nf, nt):
    f, t = place(nf, nt)
    barrier = pltpu.get_barrier_semaphore()
    for j in range(1, nf):
        pl.semaphore_signal(
            barrier, inc=1, device_id=(lax.rem(f + j, nf), t), device_id_type=MESH
        )
    for j in range(1, nt):
        pl.semaphore_signal(
            barrier, inc=1, device_id=(f, lax.rem(t + j, nt)), device_id_type=MESH
        )
    pl.semaphore_wait(barrier, nf + nt - 2)


def remote(src, dst, send, recv, device):
    return pltpu.make_async_remote_copy(
        src_ref=src,
        dst_ref=dst,
        send_sem=send,
        recv_sem=recv,
        device_id=device,
        device_id_type=MESH,
    )


def line_steps(stage, mats, nz, f, t, up_send, down_send, recv, arrived):
    z = t // 2

    def up(m, b):
        return remote(
            stage.at[m, b], stage.at[m, b], up_send.at[m, b], recv.at[m, b], (f, t + 2)
        )

    def down(m, b):
        return remote(
            stage.at[m, b], stage.at[m, b], down_send.at[m, b], recv.at[m, b], (f, t - 2)
        )

    for s in range(nz):
        for m in range(mats):
            for direction in (0, 1) if s else (0,):
                b = z - s if direction == 0 else z + s

                @pl.when((b >= 0) & (b < nz))
                def _(m=m, b=b, s=s, direction=direction):
                    if s:
                        up(m, b).wait_recv()
                    if s == 0 or direction == 0:

                        @pl.when(z < nz - 1)
                        def _():
                            up(m, b).start()

                    if s == 0 or direction == 1:

                        @pl.when(z > 0)
                        def _():
                            down(m, b).start()

                    arrived(m, b)

    def finish():
        for b in range(nz):
            for m in range(mats):

                @pl.when((z < nz - 1) & (b <= z))
                def _(m=m, b=b):
                    up(m, b).wait_send()

                @pl.when((z > 0) & (b >= z))
                def _(m=m, b=b):
                    down(m, b).wait_send()

    return finish


def spread_kernel(
    nf,
    nt,
    tokens,
    grads,
    x_out,
    g_out,
    stage,
    local_sem,
    up_send,
    down_send,
    line_recv,
    plane_send,
    plane_recv,
    pair_send,
    pair_recv,
):
    f, t = place(nf, nt)
    nz = nt // 2
    z, k = t // 2, lax.rem(t, 2)
    rows, width = tokens.shape
    size = rows // CHUNKS
    outs = (x_out, g_out)
    loads = []
    for m, ref in enumerate((tokens, grads)):
        load = pltpu.make_async_copy(ref, stage.at[m, z], local_sem.at[m])
        load.start()
        loads.append(load)
    enter(nf, nt)
    for load in loads:
        load.wait()

    half = pl.ds(pl.multiple_of(k * width, width), width)

    def held(m, b, c):
        return stage.at[m, b, pl.ds(c * size, size)]

    def spot(m, g, c):
        return outs[m].at[pl.ds(pl.multiple_of(g * rows + c * size, size), size), half]

    def up(m, b, c):
        here = held(m, b, c)
        return remote(here, here, up_send.at[m, b, c], line_recv.at[m, b, c], (f, t + 2))

    def down(m, b, c):
        here = held(m, b, c)
        return remote(here, here, down_send.at[m, b, c], line_recv.at[m, b, c], (f, t - 2))

    def plane(m, b, c):
        return remote(
            held(m, b, c), spot(m, f, c), plane_send.at[m, b, c], plane_recv.at[m, f, c], (b, t)
        )

    def plane_in(m, g, c):
        return remote(
            held(m, 0, c), spot(m, g, c), plane_send.at[m, 0, c], plane_recv.at[m, g, c], (f, t)
        )

    def keep(m, c):
        return pltpu.make_async_copy(held(m, f, c), spot(m, f, c), plane_recv.at[m, f, c])

    def arrived(m, b, c):
        @pl.when(b != f)
        def _():
            plane(m, b, c).start()

        @pl.when(b == f)
        def _():
            keep(m, c).start()

    def send_own(c):
        for m in range(2):

            @pl.when(z < nz - 1)
            def _(m=m):
                up(m, z, c).start()

            @pl.when(z > 0)
            def _(m=m):
                down(m, z, c).start()

    def pair(m, g, c):
        here = spot(m, g, c)
        return remote(
            here, here, pair_send.at[m, g, c], pair_recv.at[m, g, c], (f, t + 1 - 2 * k)
        )

    def swap(c):
        for m in range(2):
            for j in range(nf):
                g = lax.rem(f + j, nf)
                if j == 0:
                    keep(m, c).wait()
                else:
                    plane_in(m, g, c).wait_recv()
                pair(m, g, c).start()

    edge = (z == 0) | (z == nz - 1)
    for c in range(CHUNKS):
        if c < AHEAD:
            send_own(c)
        else:

            @pl.when(edge)
            def _(c=c):
                send_own(c)

    for c in range(CHUNKS):
        for m in range(2):
            arrived(m, z, c)
        for s in range(1, nz):
            for direction in (0, 1):
                b = z - s if direction == 0 else z + s

                @pl.when((b >= 0) & (b < nz))
                def _(b=b, direction=direction):
                    for m in range(2):
                        up(m, b, c).wait_recv()
                        if direction == 0:

                            @pl.when(z < nz - 1)
                            def _():
                                up(m, b, c).start()

                        else:

                            @pl.when(z > 0)
                            def _():
                                down(m, b, c).start()

                        arrived(m, b, c)

        if c + AHEAD < CHUNKS:

            @pl.when(jnp.logical_not(edge))
            def _(c=c):
                send_own(c + AHEAD)

        if c >= 2:
            swap(c - 2)
    for c in range(max(CHUNKS - 2, 0), CHUNKS):
        swap(c)
    for c in range(CHUNKS):
        for m in range(2):
            for b in range(nz):

                @pl.when((z < nz - 1) & (b <= z))
                def _(m=m, b=b):
                    up(m, b, c).wait_send()

                @pl.when((z > 0) & (b >= z))
                def _(m=m, b=b):
                    down(m, b, c).wait_send()

                @pl.when(b != f)
                def _(m=m, b=b):
                    plane(m, b, c).wait_send()

            for g in range(nf):
                pair(m, g, c).wait()


def middle_kernel(
    nf,
    nt,
    factor,
    whole,
    grads,
    gate_weight,
    up_weight,
    down_weight,
    all_out,
    w_out,
    gate_out,
    up_out,
    down_out,
    partial,
    hidden_out,
    landing,
    stage,
    hidden_own,
    sum_send,
    sum_recv,
    up_send,
    down_send,
    line_recv,
    plane_send,
    plane_recv,
    pair_send,
    pair_recv,
    h_send,
    h_recv,
    local_sem,
    w_send,
    w_recv,
):
    f, t = place(nf, nt)
    nz = nt // 2
    z, k = t // 2, lax.rem(t, 2)
    rows = landing.shape[1]
    width = hidden_own.shape[1]

    def block(g):
        return pl.ds(pl.multiple_of(g * rows, rows), rows)

    part = w_out.shape[0]
    ups = (gate_weight, up_weight)

    def into(u, i):
        return w_out.at[:, pl.ds(pl.multiple_of((2 * u + i) * width, width), width)]

    def w_own(i):
        return pltpu.make_async_copy(
            ups[i].at[pl.ds(t * part, part)], into(t, i), local_sem.at[1 + i]
        )

    def multiply(g):
        x = whole[block(g), :]
        partial[block(g), :width] = jnp.dot(x, gate_weight[...], preferred_element_type=F32)
        partial[block(g), width : 2 * width] = jnp.dot(
            x, up_weight[...], preferred_element_type=F32
        )
        partial[block(g), 2 * width :] = lax.dot_general(
            grads[block(g), :],
            down_weight[...],
            (((1,), (1,)), ((), ())),
            preferred_element_type=F32,
        )

    for i in range(2):
        w_own(i).start()
    enter(nf, nt)

    def share(g):
        return remote(
            partial.at[block(g)], landing.at[f], sum_send.at[g], sum_recv.at[f], (g, t)
        )

    def share_in(g):
        return remote(
            partial.at[block(g)], landing.at[g], sum_send.at[g], sum_recv.at[g], (g, t)
        )

    def w_copy(u, i):
        return remote(
            ups[i].at[pl.ds(u * part, part)], into(t, i), w_send.at[u, i], w_recv.at[t, i], (f, u)
        )

    def w_in(u, i):
        return remote(
            ups[i].at[pl.ds(0, part)], into(u, i), w_send.at[u, i], w_recv.at[u, i], (f, u)
        )

    for j in range(1, nt):
        for i in range(2):
            w_copy(lax.rem(t + j, nt), i).start()

    @pl.loop(1, nf + 1)
    def _(j):
        multiply(lax.rem(f + j, nf))

        @pl.when(j > 1)
        def _():
            share(lax.rem(f + j - 1, nf)).start()

    for j in range(1, nf):
        share_in(lax.rem(f + j, nf)).wait_recv()
    total = partial[block(f), :]
    for j in range(1, nf):
        total = total + landing[lax.rem(f + j, nf)]
    gate = total[:, :width]
    up = total[:, width : 2 * width]
    hidden_grad = total[:, 2 * width :]
    squashed = jax.nn.sigmoid(gate)
    activated = gate * squashed
    slope = squashed * (1.0 + gate * (1.0 - squashed))
    stage[0, z, :, :width] = (hidden_grad * up * slope).astype(BF16)
    stage[0, z, :, width:] = (hidden_grad * activated).astype(BF16)
    hidden_own[...] = (activated * up).astype(BF16)

    def h_copy(g):
        return remote(
            hidden_own, hidden_out.at[block(f)], h_send.at[g], h_recv.at[f], (g, t)
        )

    def h_in(g):
        return remote(
            hidden_own, hidden_out.at[block(g)], h_send.at[g], h_recv.at[g], (g, t)
        )

    def spot(g, b):
        at = pl.multiple_of((2 * b + k) * 2 * width, 2 * width)
        return all_out.at[block(g), pl.ds(at, 2 * width)]

    def plane(b, g):
        return remote(
            stage.at[0, b], spot(f, b), plane_send.at[b, g], plane_recv.at[b, f], (g, t)
        )

    def plane_in(b, g):
        return remote(
            stage.at[0, b], spot(g, b), plane_send.at[b, g], plane_recv.at[b, g], (g, t)
        )

    def keep(b):
        return pltpu.make_async_copy(stage.at[0, b], spot(f, b), plane_recv.at[b, f])

    def arrived(m, b):
        for j in range(1, nf):
            plane(b, lax.rem(f + j, nf)).start()
        keep(b).start()

    finish = line_steps(stage, 1, nz, f, t, up_send, down_send, line_recv, arrived)
    for j in range(1, nf):
        h_copy(lax.rem(f + j, nf)).start()
    h_keep = pltpu.make_async_copy(hidden_own, hidden_out.at[block(f)], local_sem.at[0])
    h_keep.start()

    def pair(b, g):
        return remote(
            spot(g, b), spot(g, b), pair_send.at[b, g], pair_recv.at[b, g], (f, t + 1 - 2 * k)
        )

    def pair_in(b, g):
        at = pl.multiple_of((2 * b + 1 - k) * 2 * width, 2 * width)
        here = all_out.at[block(g), pl.ds(at, 2 * width)]
        return remote(
            here, here, pair_send.at[b, g], pair_recv.at[b, g], (f, t + 1 - 2 * k)
        )

    def pass_on(b):
        for j in range(nf):
            g = lax.rem(f + j, nf)
            if j == 0:
                keep(b).wait()
            else:
                plane_in(b, g).wait_recv()
            pair(b, g).start()

    h_keep.wait()
    for j in range(1, nf):
        h_in(lax.rem(f + j, nf)).wait_recv()
    pass_on(z)
    own = pl.ds(pl.multiple_of(t * 2 * width, 2 * width), 2 * width)
    tile = min(TILE, whole.shape[1])
    contract = (((0,), (0,)), ((), ()))

    @pl.loop(0, whole.shape[1] // tile)
    def _(i):
        cols = pl.ds(pl.multiple_of(i * tile, tile), tile)
        term = factor * lax.dot_general(
            whole[:, cols], all_out[:, own], contract, preferred_element_type=F32
        )
        gate_out[cols, :] = term[:, :width]
        up_out[cols, :] = term[:, width:]
        down_out[:, cols] = factor * lax.dot_general(
            hidden_out[...], grads[:, cols], contract, preferred_element_type=F32
        )

    for b in range(nz):

        @pl.when(b != z)
        def _(b=b):
            pass_on(b)

    finish()
    for j in range(1, nf):
        g = lax.rem(f + j, nf)
        share(g).wait_send()
        h_copy(g).wait_send()
        for b in range(nz):
            plane(b, g).wait_send()
    for b in range(nz):
        for g in range(nf):
            pair(b, g).wait_send()
            pair_in(b, g).wait_recv()
    for i in range(2):
        w_own(i).wait()
        for j in range(1, nt):
            u = lax.rem(t + j, nt)
            w_copy(u, i).wait_send()
            w_in(u, i).wait_recv()


def return_kernel(nf, nt, deltas, turned, out, result, landing, send, recv, send2, recv2, local_sem):
    f, t = place(nf, nt)
    rows = landing.shape[1]

    def block(g):
        return pl.ds(pl.multiple_of(g * rows, rows), rows)

    keep = pltpu.make_async_copy(result.at[block(f)], landing.at[f], local_sem.at[0])
    enter(nf, nt)

    def first(g):
        return remote(result.at[block(g)], landing.at[f], send.at[g], recv.at[f], (g, t))

    def first_in(g):
        return remote(result.at[block(g)], landing.at[g], send.at[g], recv.at[g], (g, t))

    @pl.loop(1, nf + 1)
    def _(j):
        g = lax.rem(f + j, nf)
        result[block(g), :] = lax.dot_general(
            deltas[block(g), :],
            turned[...],
            (((1,), (1,)), ((), ())),
            preferred_element_type=F32,
        ).astype(BF16)

        @pl.when(j > 1)
        def _():
            first(lax.rem(f + j - 1, nf)).start()

    keep.start()
    keep.wait()
    lane = lax.rem(t, nf)

    def second(g):
        return remote(
            landing.at[g], out.at[lane], send2.at[g], recv2.at[lane], (f, 2 * g + t // nf)
        )

    def own(g):
        return pltpu.make_async_copy(landing.at[g], out.at[lane], recv2.at[lane])

    def second_in(i):
        return remote(
            landing.at[0], out.at[i], send2.at[0], recv2.at[i], (f, t)
        )

    for j in range(nf):
        g = lax.rem(f + j, nf)
        if j:
            first_in(g).wait_recv()

        @pl.when(2 * g + t // nf != t)
        def _(g=g):
            second(g).start()

        @pl.when(2 * g + t // nf == t)
        def _(g=g):
            own(g).start()

    source = lax.rem(t, 2) * nf
    for i in range(nf):

        @pl.when(source + i != t)
        def _(i=i):
            second_in(i).wait_recv()

        @pl.when(source + i == t)
        def _(i=i):
            own(0).wait()

    for j in range(nf):
        g = lax.rem(f + j, nf)
        if j:
            first(g).wait_send()

        @pl.when(2 * g + t // nf != t)
        def _(g=g):
            second(g).wait_send()


def params(number):
    return pltpu.CompilerParams(
        collective_id=number, has_side_effects=True, vmem_limit_bytes=VMEM_LIMIT
    )


ANY = pl.BlockSpec(memory_space=pl.ANY)
VMEM = pl.BlockSpec(memory_space=pltpu.VMEM)
DMA = pltpu.SemaphoreType.DMA


def body(tokens, out_grad, gate_weight, up_weight, down_weight):
    nf, nt = lax.axis_size("fsdp"), lax.axis_size("tp")
    nz = nt // 2
    rows, shard = tokens.shape
    depth, width = gate_weight.shape
    count = rows * nf
    factor = 1.0 / math.sqrt(count)
    assert nt == 2 * nf and depth == 2 * shard

    part = depth // nt
    whole, grads = pl.pallas_call(
        functools.partial(spread_kernel, nf, nt),
        out_shape=(
            jax.ShapeDtypeStruct((count, depth), BF16),
            jax.ShapeDtypeStruct((count, depth), BF16),
        ),
        in_specs=[VMEM, VMEM],
        out_specs=(VMEM, VMEM),
        scratch_shapes=[
            pltpu.VMEM((2, nz, rows, shard), BF16),
            DMA((2,)),
            DMA((2, nz, CHUNKS)),
            DMA((2, nz, CHUNKS)),
            DMA((2, nz, CHUNKS)),
            DMA((2, nz, CHUNKS)),
            DMA((2, nf, CHUNKS)),
            DMA((2, nf, CHUNKS)),
            DMA((2, nf, CHUNKS)),
        ],
        compiler_params=params(0),
        name="spread",
    )(tokens, out_grad)

    deltas, turned, gate_grad, up_grad, down_grad = pl.pallas_call(
        functools.partial(middle_kernel, nf, nt, factor),
        out_shape=(
            jax.ShapeDtypeStruct((count, nt * 2 * width), BF16),
            jax.ShapeDtypeStruct((part, nt * 2 * width), BF16),
            jax.ShapeDtypeStruct((depth, width), F32),
            jax.ShapeDtypeStruct((depth, width), F32),
            jax.ShapeDtypeStruct((width, depth), F32),
        ),
        in_specs=[VMEM] * 5,
        out_specs=(VMEM,) * 5,
        scratch_shapes=[
            pltpu.VMEM((count, 3 * width), F32),
            pltpu.VMEM((count, width), BF16),
            pltpu.VMEM((nf, rows, 3 * width), F32),
            pltpu.VMEM((1, nz, rows, 2 * width), BF16),
            pltpu.VMEM((rows, width), BF16),
            DMA((nf,)),
            DMA((nf,)),
            DMA((1, nz)),
            DMA((1, nz)),
            DMA((1, nz)),
            DMA((nz, nf)),
            DMA((nz, nf)),
            DMA((nz, nf)),
            DMA((nz, nf)),
            DMA((nf,)),
            DMA((nf,)),
            DMA((3,)),
            DMA((nt, 2)),
            DMA((nt, 2)),
        ],
        compiler_params=params(1),
        name="middle",
    )(whole, grads, gate_weight, up_weight, down_weight)

    input_grad = pl.pallas_call(
        functools.partial(return_kernel, nf, nt),
        out_shape=jax.ShapeDtypeStruct((nf, rows, part), BF16),
        in_specs=[VMEM, VMEM],
        out_specs=VMEM,
        scratch_shapes=[
            pltpu.VMEM((count, part), BF16),
            pltpu.VMEM((nf, rows, part), BF16),
            DMA((nf,)),
            DMA((nf,)),
            DMA((nf,)),
            DMA((nf,)),
            DMA((1,)),
        ],
        compiler_params=params(2),
        name="back",
    )(deltas, turned)
    input_grad = input_grad.transpose(1, 0, 2).reshape(rows, shard)

    return (input_grad, gate_grad, up_grad, down_grad)


def solution(mesh):
    return jax.shard_map(
        body,
        mesh=mesh,
        in_specs=(
            P("fsdp", "tp"),
            P("fsdp", "tp"),
            P("fsdp", "tp"),
            P("fsdp", "tp"),
            P("tp", "fsdp"),
        ),
        out_specs=(P("fsdp", "tp"), P("fsdp", "tp"), P("fsdp", "tp"), P("tp", "fsdp")),
        check_vma=False,
    )
```

profile of v0, /device:TPU:32, one launch (start us, length us, event | category | flops | bytes accessed | tf_op | source)
XLA Modules:
  0.0 354.3 jit_solution(12270597336916250367)
XLA Ops:
  0.6 115.3 %spread.1 = (bf16[2048,1024]{1,0:T(8,128)(2,1)}, bf16[2048,1024]{1,0:T(8,128)(2,1)}) custom-call(bf16[256,512]{1,0:T(8,128)(2,1)} %tokens.1, bf16[256,512]{1,0:T(8,128)(2,1)} %grads.1), custom_call_target="tpu_custom_call" | custom-call | tf_op jit(solution)/shard_map/spread/pallas_call | solution.py:586
  115.9 194.3 %middle.1 = (bf16[2048,4096]{1,0:T(8,128)(2,1)}, bf16[64,4096]{1,0:T(8,128)(2,1)}, f32[1024,128]{1,0:T(8,128)}, f32[1024,128]{1,0:T(8,128)}, f32[128,1024]{1,0:T(8,128)}) custom-call(bf16[2048,1024]{1,0:T(8,128)(2,1)} %get-tuple-element.11.whole, bf16[2048,1024]{1,0:T(8,128)(2,1)} %get-tuple-element.12.grads, bf16[1024,128]{1,0:T(8,128)(2,1)} %gate_weight.1, ...), custom_call_target="tpu_custom_call" | custom-call | tf_op jit(solution)/shard_map/middle/pallas_call | solution.py:609
  310.3 0.0 copy-start.2
  310.3 0.0 copy-start.1
  310.3 0.0 copy-start
  310.3 39.5 %back.1 = bf16[8,256,64]{2,1,0:T(8,128)(2,1)} custom-call(bf16[2048,4096]{1,0:T(8,128)(2,1)} %get-tuple-element.13.deltas, bf16[64,4096]{1,0:T(8,128)(2,1)} %get-tuple-element.14.turned), custom_call_target="tpu_custom_call" | custom-call | tf_op jit(solution)/shard_map/back/pallas_call | solution.py:645
  349.8 1.2 copy.9
  351.0 0.8 copy.10
  351.9 0.0 copy-done.2
  351.9 0.8 copy.14
  352.7 0.0 copy-done.1
  352.7 0.8 copy.15
  353.5 0.0 copy-done
  353.5 0.8 copy.16
Async XLA Ops:
  310.3 41.6 %copy-start.2 = (f32[1024,128]{1,0:T(8,128)S(1)}, f32[1024,128]{1,0:T(8,128)}, u32[]{:S(2)}) copy-start(f32[1024,128]{1,0:T(8,128)} %get-tuple-element.27) | copy-start | bytes 1572868
  310.3 42.4 %copy-start.1 = (f32[1024,128]{1,0:T(8,128)S(1)}, f32[1024,128]{1,0:T(8,128)}, u32[]{:S(2)}) copy-start(f32[1024,128]{1,0:T(8,128)} %get-tuple-element.28) | copy-start | bytes 1572868
  310.3 43.2 %copy-start = (f32[128,1024]{1,0:T(8,128)S(1)}, f32[128,1024]{1,0:T(8,128)}, u32[]{:S(2)}) copy-start(f32[128,1024]{1,0:T(8,128)} %get-tuple-element.29) | copy-start | bytes 1572868
where the time goes:
time: 359 us; the launch traced here: 354 us
  Pallas kernels  349 us (97%)
  local copies, waits for them, and re-layouts  4.46 us (1%)
    pallas_call x1, Pallas kernels, body(): pl.pallas_call(functools.partial(middle_kernel, nf, nt, factor), out_shap...  194 us
    pallas_call x1, Pallas kernels, body(): pl.pallas_call(functools.partial(spread_kernel, nf, nt), out_shape=(jax.S...  115 us
    pallas_call x1, Pallas kernels, body(): pl.pallas_call(functools.partial(return_kernel, nf, nt), out_shape=jax.Sh...  39.5 us

commit v1 on v0

v1 whole, which is shorter than its diff:
```python
import functools
import math

import jax
import jax.numpy as jnp
from jax import lax
from jax.sharding import PartitionSpec as P
from jax.experimental import pallas as pl
from jax.experimental.pallas import tpu as pltpu

MESH = pl.DeviceIdType.MESH
F32 = jnp.float32
BF16 = jnp.bfloat16
VMEM_LIMIT = 60 * 1024 * 1024
ROWS = ((0,), (0,))
COLS = ((1,), (1,))


def kernel(
    factor,
    tokens,
    grads,
    gate_weight,
    up_weight,
    down_weight,
    result,
    gate_out,
    up_out,
    down_out,
    xg,
    wf,
    df,
    sa,
    zra,
    zla,
    sb,
    zrb,
    zlb,
    acts,
    hidden,
    dg,
    tw,
    dpart,
    gpart,
    dtwo,
    gtwo,
    done,
    gone,
    dmid,
    gmid,
    dland,
    gland,
    gown,
    total,
    rounded,
    z_send,
    z_recv,
    x_send,
    x_recv,
    p_send,
    p_recv,
    y_send,
    y_recv,
    a_send,
    a_recv,
    b_send,
    b_recv,
    t_send,
    t_recv,
    l_send,
    l_recv,
    dx_send,
    dx_recv,
    dp_send,
    dp_recv,
    two_send,
    two_recv,
    one_send,
    one_recv,
    r_send,
    r_recv,
):
    f, t = lax.axis_index("fsdp"), lax.axis_index("tp")
    h, y = lax.div(f, 4), lax.rem(f, 4)
    l, x, k = lax.div(t, 8), lax.rem(lax.div(t, 2), 4), lax.rem(t, 2)
    z = 2 * h + l
    outer = h == l
    inner = h != l
    rows, shard = tokens.shape
    deep, width = gate_weight.shape
    part = rows // 2
    wide = 2 * width

    def at(xx, yy, hh, ll, kk):
        return (hh * 4 + yy, ll * 8 + xx * 2 + kk)

    def at_z(zz):
        return at(x, y, lax.div(zz, 2), lax.rem(zz, 2), k)

    xs = (lax.rem(x + 3, 4), lax.rem(x + 1, 4), lax.rem(x + 2, 4))
    ys = (lax.rem(y + 3, 4), lax.rem(y + 1, 4), lax.rem(y + 2, 4))
    right, left = at(xs[1], y, h, l, k), at(xs[0], y, h, l, k)
    north, south = at(x, ys[1], h, l, k), at(x, ys[0], h, l, k)
    mate = at(x, y, h, l, 1 - k)
    flip = at(x, y, h, 1 - l, k)
    across = at(x, y, 1 - h, 1 - l, k)
    step = 1 - 2 * k
    ahead = at_z(lax.rem(z + step + 4, 4))

    def remote(src, dst, send, recv, device):
        return pltpu.make_async_remote_copy(
            src_ref=src,
            dst_ref=dst,
            send_sem=send,
            recv_sem=recv,
            device_id=device,
            device_id_type=MESH,
        )

    barrier = pltpu.get_barrier_semaphore()
    for j in range(1, 16):
        pl.semaphore_signal(
            barrier, inc=1, device_id=(f, lax.rem(t + j, 16)), device_id_type=MESH
        )
    for peer in (north, south, at(x, y, 1 - h, l, k), across):
        pl.semaphore_signal(barrier, inc=1, device_id=peer, device_id_type=MESH)
    pl.semaphore_wait(barrier, 19)

    ups = (gate_weight, up_weight, down_weight)

    def w_own(w, q):
        size = ups[w].shape[0] // 2
        return ups[w].at[pl.ds(q * size, size)]

    def w_spot(o, w, q):
        if w == 2:
            return df.at[o, pl.ds(q * (width // 2), width // 2)]
        return wf.at[o, w, pl.ds(q * (deep // 2), deep // 2)]

    def w_out(way, w, q):
        return remote(
            w_own(w, q),
            w_spot(y, w, q),
            y_send.at[way, w, q],
            y_recv.at[way, w, q],
            (north, south)[way],
        )

    def w_on(w, q):
        here = w_spot(ys[q], w, q)
        return remote(here, here, y_send.at[2, w, q], y_recv.at[2, w, q], (north, south)[q])

    def w_in(d, w, q):
        here = w_spot(ys[d], w, q)
        return remote(here, here, y_send.at[2, w, q], y_recv.at[d, w, q], north)

    def w_start(w):
        for way, q in ((0, 0), (1, 1), (0, 1), (1, 0)):
            w_out(way, w, q).start()

    def w_forward(w):
        for q in range(2):
            w_in(q, w, q).wait_recv()
            w_on(w, q).start()

    def w_rest(w):
        for q in range(2):
            w_in(1 - q, w, q).wait_recv()
            w_in(2, w, q).wait_recv()

    own = (tokens, grads)
    slot = (h, 1 - h)

    def x_own(m, q):
        return own[m].at[pl.ds(q * part, part)]

    def x_spot(p, o, j, m, q):
        return xg.at[p * 4 + o, m, slot[j], pl.ds(q * part, part)]

    def z_out(m, q, device, j):
        spot = xg.at[k * 4 + x, m, h, pl.ds(q * part, part)]
        return remote(x_own(m, q), spot, z_send.at[0, m, q], z_recv.at[j, m, q], device)

    def z_on(m, q):
        here = x_spot(k, x, 1, m, q)
        return remote(here, here, z_send.at[1, m, q], z_recv.at[1, m, q], flip)

    def z_in(j, m, q):
        here = x_spot(k, x, j, m, q)
        return remote(here, here, z_send.at[0, m, q], z_recv.at[j, m, q], flip)

    def x_out(way, src, j, m, q):
        return remote(
            src,
            x_spot(k, x, j, m, q),
            x_send.at[way, j, m, q],
            x_recv.at[way, j, m, q],
            (right, left)[way],
        )

    def x_on(j, m, q):
        here = x_spot(k, xs[q], j, m, q)
        return remote(
            here, here, x_send.at[2, j, m, q], x_recv.at[2, j, m, q], (right, left)[q]
        )

    def x_in(d, j, m, q):
        here = x_spot(k, xs[d], j, m, q)
        return remote(here, here, x_send.at[2, j, m, q], x_recv.at[d, j, m, q], right)

    places = (*xs, x)

    def p_out(d, src, j, m, q):
        return remote(
            src,
            x_spot(k, places[d], j, m, q),
            p_send.at[d, j, m, q],
            p_recv.at[d, j, m, q],
            mate,
        )

    def p_in(d, j, m, q):
        here = x_spot(1 - k, places[d], j, m, q)
        return remote(here, here, p_send.at[d, j, m, q], p_recv.at[d, j, m, q], mate)

    def spread(src, j, m, q):
        for way in (0, 1) if q == 0 else (1, 0):
            x_out(way, src, j, m, q).start()
        p_out(3, src, j, m, q).start()

    def passed(d, j, m, q):
        x_in(d, j, m, q).wait_recv()
        if d == q:
            x_on(j, m, q).start()
        p_out(d, x_spot(k, places[d], j, m, q), j, m, q).start()

    def z_forward(m, q):
        @pl.when(inner)
        def _():
            z_in(1, m, q).wait_recv()
            z_on(m, q).start()

    def z_spread(m, q, own_too):
        @pl.when(inner)
        def _():
            z_in(0, m, q).wait_recv()
            spread(x_spot(k, x, 0, m, q), 0, m, q)

        @pl.when(outer)
        def _():
            if own_too:
                spread(x_own(m, q), 0, m, q)
            z_in(1, m, q).wait_recv()

        spread(x_spot(k, x, 1, m, q), 1, m, q)

    @pl.when(outer)
    def _():
        for m in range(2):
            for q in range(2):
                z_out(m, q, flip, 0).start()
            if m == 0:
                for q in range(2):
                    spread(x_own(0, q), 0, 0, q)

    @pl.when(inner)
    def _():
        for m in range(2):
            for q in range(2):
                z_out(m, q, across, 1).start()

    w_start(0)
    w_start(1)

    @pl.when(outer)
    def _():
        for m in range(2):
            xg[k * 4 + x, m, h] = own[m][...]

    wf[y, 0] = gate_weight[...]
    wf[y, 1] = up_weight[...]
    df[y] = down_weight[...]

    for q in range(2):
        z_forward(0, q)
        z_spread(0, q, False)
    for j in range(2):
        passed(0, j, 0, 0)
        passed(1, j, 0, 0)
    z_forward(1, 0)
    w_forward(0)
    for j in range(2):
        passed(1, j, 0, 1)
        passed(0, j, 0, 1)
    z_forward(1, 1)
    w_forward(1)
    w_start(2)
    for q in range(2):
        z_spread(1, q, True)
    for q in range(2):
        for j in range(2):
            passed(2, j, 0, q)
    w_rest(0)
    w_rest(1)
    for d in (3, 0, 1, 2):
        for j in range(2):
            for q in range(2):
                p_in(d, j, 0, q).wait_recv()

    tall = 2 * rows

    def block(m, o):
        return jnp.concatenate(
            [xg[p * 4 + o, m].reshape(tall, shard) for p in range(2)], axis=1
        )

    sa[...] = jnp.zeros_like(sa)

    @pl.loop(0, 4)
    def _(o):
        weights = jnp.concatenate([wf[o, 0], wf[o, 1]], axis=1)
        sa[...] += jnp.dot(block(0, o), weights, preferred_element_type=F32)

    def swap(src, mid, dst, send, recv):
        def first(c):
            at_c = pl.ds(c * rows, rows)
            return remote(src.at[at_c], mid.at[at_c], send.at[0, c], recv.at[0, c], ahead)

        def second(c):
            at_c = pl.ds(c * rows, rows)
            return remote(mid.at[at_c], dst.at[at_c], send.at[1, c], recv.at[1, c], ahead)

        return first, second

    a_first, a_second = swap(sa, zra, zla, a_send, a_recv)
    b_first, b_second = swap(sb, zrb, zlb, b_send, b_recv)

    for j in range(2):
        passed(0, j, 1, 0)
        passed(1, j, 1, 0)
        if j == 0:
            for c in range(2):
                a_first(c).start()
    w_forward(2)
    for j in range(2):
        passed(1, j, 1, 1)
        passed(0, j, 1, 1)
        a_first(j).wait_recv()
        a_second(j).start()

    def t_spot(u):
        return pl.ds(lax.rem(u, 2) * shard + lax.div(u, 8) * wide, wide)

    def t_out(j):
        u = lax.rem(t + j, 16)
        return remote(
            wf.at[lax.rem(lax.div(u, 2), 4), :, t_spot(u)],
            tw.at[t],
            t_send.at[j],
            t_recv.at[j],
            (f, u),
        )

    def t_in(j):
        u = lax.rem(t + 16 - j, 16)
        return remote(tw.at[u], tw.at[u], t_send.at[j], t_recv.at[j], (f, u))

    @pl.loop(1, 16)
    def _(j):
        t_out(j).start()

    tw[t] = wf[x, :, t_spot(t)]

    for c in range(2):
        a_second(c).wait_recv()
    sums = sa[...] + zla[...]
    gate, up = sums[:, :width], sums[:, width:]
    squashed = jax.nn.sigmoid(gate)
    activated = gate * squashed
    slope = squashed * (1.0 + gate * (1.0 - squashed))
    acts[:, :width] = up * slope
    acts[:, width:] = activated
    hidden[...] = (activated * up).astype(BF16)

    for q in range(2):
        for j in range(2):
            passed(2, j, 1, q)
    w_rest(2)
    for d in (3, 0, 1, 2):
        for j in range(2):
            for q in range(2):
                p_in(d, j, 1, q).wait_recv()

    sb[...] = jnp.zeros_like(sb)

    @pl.loop(0, 4)
    def _(o):
        sb[...] += lax.dot_general(
            block(1, o), df[o], (COLS, ((), ())), preferred_element_type=F32
        )

    def down_part(o):
        return lax.dot_general(
            hidden[...], block(1, o), (ROWS, ((), ())), preferred_element_type=F32
        )

    def gate_part(o):
        return lax.dot_general(
            block(0, o), dg[t], (ROWS, ((), ())), preferred_element_type=F32
        )

    twos, mids, parts, ones, lands = (
        (dtwo, gtwo),
        (dmid, gmid),
        (dpart, gpart),
        (done, gone),
        (dland, gland),
    )

    def halves(i, q):
        size = twos[i].shape[0] // 2
        return pl.ds(q * size, size)

    def two_out(i, q):
        return remote(
            twos[i].at[halves(i, q)],
            mids[i].at[q],
            two_send.at[i, q],
            two_recv.at[i, q],
            (north, south)[q],
        )

    def one_out(i, way, q):
        return remote(
            ones[i].at[way, halves(i, q)],
            lands[i].at[way, halves(i, q)],
            one_send.at[i, way, q],
            one_recv.at[i, way, q],
            (north, south)[way],
        )

    def one_parts(i, fn):
        for way in range(2):
            q = way
            term = fn(ys[1 - way])
            size = term.shape[0] // 2
            parts[i][way] = term[q * size : (q + 1) * size]
            ones[i][way, halves(i, 1 - q)] = term[(1 - q) * size : (2 - q) * size].astype(BF16)

    def one_merge(i):
        for way in range(2):
            two_out(i, way).wait_recv()
            ones[i][way, halves(i, way)] = (
                parts[i][way] + mids[i][way].astype(F32)
            ).astype(BF16)

    def finals(i):
        for way in range(2):
            for q in range(2):
                one_out(i, way, q).wait_recv()
        return lands[i][0].astype(F32) + lands[i][1].astype(F32)

    dtwo[...] = down_part(ys[2]).astype(BF16)
    for c in range(2):
        b_first(c).start()
    one_parts(0, down_part)
    for q in range(2):
        two_out(0, q).start()
    for way in range(2):
        one_out(0, way, 1 - way).start()
    for c in range(2):
        b_first(c).wait_recv()
        b_second(c).start()
    down_out[...] = down_part(y)
    one_merge(0)

    for c in range(2):
        b_second(c).wait_recv()
    for way in range(2):
        one_out(0, way, way).start()

    hidden_grad = sb[...] + zlb[...]
    dg[t, :, :width] = (hidden_grad * acts[:, :width]).astype(BF16)
    dg[t, :, width:] = (hidden_grad * acts[:, width:]).astype(BF16)
    gtwo[...] = gate_part(ys[2]).astype(BF16)

    sides = (l, 1 - l)

    def d_spot(c, o, j, q):
        return dg.at[sides[j] * 8 + o * 2 + c, pl.ds(q * rows, rows)]

    def l_out(q):
        here = d_spot(k, x, 0, q)
        return remote(here, here, l_send.at[q], l_recv.at[q], flip)

    def l_in(q):
        here = d_spot(k, x, 1, q)
        return remote(here, here, l_send.at[q], l_recv.at[q], flip)

    def dx_out(way, j, q):
        here = d_spot(k, x, j, q)
        return remote(
            here, here, dx_send.at[way, j, q], dx_recv.at[way, j, q], (right, left)[way]
        )

    def dx_on(j, q):
        here = d_spot(k, xs[q], j, q)
        return remote(here, here, dx_send.at[2, j, q], dx_recv.at[2, j, q], (right, left)[q])

    def dx_in(d, j, q):
        here = d_spot(k, xs[d], j, q)
        return remote(here, here, dx_send.at[2, j, q], dx_recv.at[d, j, q], right)

    def dp_out(d, j, q):
        here = d_spot(k, places[d], j, q)
        return remote(here, here, dp_send.at[d, j, q], dp_recv.at[d, j, q], mate)

    def dp_in(d, j, q):
        here = d_spot(1 - k, places[d], j, q)
        return remote(here, here, dp_send.at[d, j, q], dp_recv.at[d, j, q], mate)

    def d_spread(j, q):
        for way in (0, 1) if q == 0 else (1, 0):
            dx_out(way, j, q).start()
        dp_out(3, j, q).start()

    def d_passed(d, j, q):
        dx_in(d, j, q).wait_recv()
        if d == q:
            dx_on(j, q).start()
        dp_out(d, j, q).start()

    for q in range(2):
        l_out(q).start()
        d_spread(0, q)
    one_parts(1, gate_part)
    for q in range(2):
        two_out(1, q).start()
    for way in range(2):
        one_out(1, way, 1 - way).start()
    gown[...] = gate_part(y)
    for q in range(2):
        l_in(q).wait_recv()
        d_spread(1, q)
    down_out[...] = factor * (down_out[...] + finals(0))
    one_merge(1)
    for q in range(2):
        d_passed(q, 0, q)
    for way in range(2):
        one_out(1, way, way).start()
    for q in range(2):
        d_passed(q, 1, q)
    for j in range(2):
        for q in range(2):
            d_passed(1 - q, j, q)

    @pl.loop(1, 16)
    def _(j):
        t_in(j).wait_recv()

    total[...] = jnp.zeros_like(total)

    def gather(o, j):
        base = sides[j] * 8 + o * 2
        left_side = jnp.concatenate([dg[base], dg[base + 1]], axis=1)
        right_side = jnp.concatenate(
            [tw[base, 0], tw[base, 1], tw[base + 1, 0], tw[base + 1, 1]], axis=1
        )
        total[...] += lax.dot_general(
            left_side, right_side, (COLS, ((), ())), preferred_element_type=F32
        )

    for d in (3, 0, 1, 2):
        for j in range(2):
            for q in range(2):
                if d == 2:
                    d_passed(2, j, q)
            for q in range(2):
                dp_in(d, j, q).wait_recv()
            gather(places[d], j)
    rounded[...] = total[...].astype(BF16)

    def r_out(s):
        return remote(
            rounded.at[pl.ds(s * rows, rows)],
            result.at[:, pl.ds(pl.multiple_of(l * wide, wide), wide)],
            r_send.at[s],
            r_recv.at[l],
            at(x, y, s, h, k),
        )

    def r_in(e):
        spot = result.at[:, pl.ds(e * wide, wide)]
        return remote(spot, spot, r_send.at[0], r_recv.at[e], flip)

    both = factor * (gown[...] + finals(1))
    for s in range(2):

        @pl.when((s == h) & outer)
        def _(s=s):
            result[:, s * wide : (s + 1) * wide] = rounded[s * rows : (s + 1) * rows, :]

        @pl.when(jnp.logical_not((s == h) & outer))
        def _(s=s):
            r_out(s).start()

    gate_out[...] = both[:, :width]
    up_out[...] = both[:, width:]

    for m in range(2):
        for q in range(2):
            z_in(0, m, q).wait_send()

            @pl.when(inner)
            def _(m=m, q=q):
                z_on(m, q).wait_send()

            for j in range(2):
                for way in range(2):
                    x_out(way, x_own(m, q), j, m, q).wait_send()
                x_on(j, m, q).wait_send()
                for d in range(4):
                    p_out(d, x_own(m, q), j, m, q).wait_send()
    for w in range(3):
        for q in range(2):
            for way in range(2):
                w_out(way, w, q).wait_send()
            w_on(w, q).wait_send()
    for c in range(2):
        for copy in (a_first(c), a_second(c), b_first(c), b_second(c), l_out(c)):
            copy.wait_send()
        for i in range(2):
            two_out(i, c).wait_send()
            for q in range(2):
                one_out(i, c, q).wait_send()
        for j in range(2):
            for way in range(2):
                dx_out(way, j, c).wait_send()
            dx_on(j, c).wait_send()
            for d in range(4):
                dp_out(d, j, c).wait_send()

    @pl.loop(1, 16)
    def _(j):
        t_out(j).wait_send()

    for s in range(2):

        @pl.when(jnp.logical_not((s == h) & outer))
        def _(s=s):
            r_out(s).wait_send()

        @pl.when(jnp.logical_not((s == l) & outer))
        def _(s=s):
            r_in(s).wait_recv()


VMEM = pl.BlockSpec(memory_space=pltpu.VMEM)
DMA = pltpu.SemaphoreType.DMA


def body(tokens, out_grad, gate_weight, up_weight, down_weight):
    nf, nt = lax.axis_size("fsdp"), lax.axis_size("tp")
    rows, shard = tokens.shape
    deep, width = gate_weight.shape
    assert nf == 8 and nt == 16 and deep == 2 * shard
    factor = 1.0 / math.sqrt(rows * nf)
    tall = 2 * rows
    wide = 2 * width

    return tuple(
        pl.pallas_call(
            functools.partial(kernel, factor),
            out_shape=(
                jax.ShapeDtypeStruct((rows, shard), BF16),
                jax.ShapeDtypeStruct((deep, width), F32),
                jax.ShapeDtypeStruct((deep, width), F32),
                jax.ShapeDtypeStruct((width, deep), F32),
            ),
            in_specs=[VMEM] * 5,
            out_specs=(VMEM,) * 4,
            scratch_shapes=[
                pltpu.VMEM((8, 2, 2, rows, shard), BF16),
                pltpu.VMEM((4, 2, deep, width), BF16),
                pltpu.VMEM((4, width, deep), BF16),
                pltpu.VMEM((tall, wide), F32),
                pltpu.VMEM((tall, wide), F32),
                pltpu.VMEM((tall, wide), F32),
                pltpu.VMEM((tall, width), F32),
                pltpu.VMEM((tall, width), F32),
                pltpu.VMEM((tall, width), F32),
                pltpu.VMEM((tall, wide), F32),
                pltpu.VMEM((tall, width), BF16),
                pltpu.VMEM((nt, tall, wide), BF16),
                pltpu.VMEM((nt, 2, wide, width), BF16),
                pltpu.VMEM((2, width // 2, deep), F32),
                pltpu.VMEM((2, deep // 2, wide), F32),
                pltpu.VMEM((width, deep), BF16),
                pltpu.VMEM((deep, wide), BF16),
                pltpu.VMEM((2, width, deep), BF16),
                pltpu.VMEM((2, deep, wide), BF16),
                pltpu.VMEM((2, width // 2, deep), BF16),
                pltpu.VMEM((2, deep // 2, wide), BF16),
                pltpu.VMEM((2, width, deep), BF16),
                pltpu.VMEM((2, deep, wide), BF16),
                pltpu.VMEM((deep, wide), F32),
                pltpu.VMEM((tall, wide), F32),
                pltpu.VMEM((tall, wide), BF16),
                DMA((2, 2, 2)),
                DMA((2, 2, 2)),
                DMA((3, 2, 2, 2)),
                DMA((3, 2, 2, 2)),
                DMA((4, 2, 2, 2)),
                DMA((4, 2, 2, 2)),
                DMA((3, 3, 2)),
                DMA((3, 3, 2)),
                DMA((2, 2)),
                DMA((2, 2)),
                DMA((2, 2)),
                DMA((2, 2)),
                DMA((16,)),
                DMA((16,)),
                DMA((2,)),
                DMA((2,)),
                DMA((3, 2, 2)),
                DMA((3, 2, 2)),
                DMA((4, 2, 2)),
                DMA((4, 2, 2)),
                DMA((2, 2)),
                DMA((2, 2)),
                DMA((2, 2, 2)),
                DMA((2, 2, 2)),
                DMA((2,)),
                DMA((2,)),
            ],
            compiler_params=pltpu.CompilerParams(
                collective_id=0, has_side_effects=True, vmem_limit_bytes=VMEM_LIMIT
            ),
            name="block",
        )(tokens, out_grad, gate_weight, up_weight, down_weight)
    )


def solution(mesh):
    return jax.shard_map(
        body,
        mesh=mesh,
        in_specs=(
            P("fsdp", "tp"),
            P("fsdp", "tp"),
            P("fsdp", "tp"),
            P("fsdp", "tp"),
            P("tp", "fsdp"),
        ),
        out_specs=(P("fsdp", "tp"), P("fsdp", "tp"), P("fsdp", "tp"), P("tp", "fsdp")),
        check_vma=False,
    )
```

time: 359 us -> 119 us (0.33); the launches traced: 354 us -> 118 us
  Pallas kernels: 349 us -> 113 us
    pallas_call x3 -> x1, Pallas kernels: 349 us -> 113 us  [body(): pl.pallas_call(functools.partial(kernel, factor), out_shape=(jax.ShapeDty...]
where the time goes in v1:
time: 119 us; the launch traced here: 118 us
  Pallas kernels  113 us (95%)
  local copies, waits for them, and re-layouts  4.98 us (4%)
    pallas_call x1, Pallas kernels, body(): pl.pallas_call(functools.partial(kernel, factor), out_shape=(jax.ShapeDty...  113 us
    unnamed x10, local copies, waits for them, and re-layouts  4.98 us

profile of v1, /device:TPU:32, one launch (start us, length us, event | category | flops | bytes accessed | tf_op | source)
XLA Modules:
  0.0 118.4 jit_solution(9020132986979679425)
XLA Ops:
  0.6 112.7 %block.1 = (bf16[256,512]{1,0:T(8,128)(2,1)}, f32[1024,128]{1,0:T(8,128)}, f32[1024,128]{1,0:T(8,128)}, f32[128,1024]{1,0:T(8,128)}) custom-call(bf16[256,512]{1,0:T(8,128)(2,1)} %tokens.1, bf16[256,512]{1,0:T(8,128)(2,1)} %grads.1, bf16[1024,128]{1,0:T(8,128)(2,1)} %gate_weight.1, bf16[1024,128]{1,0:T(8,128)(2,1)} %up_weight.1, bf16[128,1024]{1,0:T(8,128)(2,1)} %down_weight.1), custom_call_target="tpu_custom_call" | custom-call | tf_op jit(solution)/shard_map/block/pallas_call | solution.py:672
  113.4 0.0 copy-start.2
  113.4 1.7 %copy.13 = bf16[256,512]{1,0:T(8,128)(2,1)} copy(bf16[256,512]{1,0:T(8,128)(2,1)} %get-tuple-element.8) | data formatting | bytes 524288
  115.1 0.0 copy-done.2
  115.1 0.0 copy-start.1
  115.1 0.8 copy.14
  115.9 0.4 copy-done.1
  116.3 0.0 copy-start
  116.3 0.8 copy.15
  117.1 0.4 copy-done
  117.6 0.8 copy.16
Async XLA Ops:
  113.4 1.7 %copy-start.2 = (f32[1024,128]{1,0:T(8,128)S(1)}, f32[1024,128]{1,0:T(8,128)}, u32[]{:S(2)}) copy-start(f32[1024,128]{1,0:T(8,128)} %get-tuple-element.9) | copy-start | bytes 1572868
  115.1 1.2 %copy-start.1 = (f32[1024,128]{1,0:T(8,128)S(1)}, f32[1024,128]{1,0:T(8,128)}, u32[]{:S(2)}) copy-start(f32[1024,128]{1,0:T(8,128)} %get-tuple-element.10) | copy-start | bytes 1572868
  116.3 1.2 %copy-start = (f32[128,1024]{1,0:T(8,128)S(1)}, f32[128,1024]{1,0:T(8,128)}, u32[]{:S(2)}) copy-start(f32[128,1024]{1,0:T(8,128)} %get-tuple-element.11) | copy-start | bytes 1572868

commit v2 on v1

--- a/solution.py
+++ b/solution.py
@@ -31,10 +31,8 @@
     wf,
     df,
     sa,
-    zra,
     zla,
     sb,
-    zrb,
     zlb,
     acts,
     hidden,
@@ -52,6 +50,7 @@
     gland,
     gown,
     total,
+    near,
     rounded,
     z_send,
     z_recv,
@@ -67,8 +66,8 @@
     b_recv,
     t_send,
     t_recv,
-    l_send,
-    l_recv,
+    f_send,
+    f_recv,
     dx_send,
     dx_recv,
     dp_send,
@@ -83,7 +82,6 @@
     f, t = lax.axis_index("fsdp"), lax.axis_index("tp")
     h, y = lax.div(f, 4), lax.rem(f, 4)
     l, x, k = lax.div(t, 8), lax.rem(lax.div(t, 2), 4), lax.rem(t, 2)
-    z = 2 * h + l
     outer = h == l
     inner = h != l
     rows, shard = tokens.shape
@@ -93,9 +91,6 @@
 
     def at(xx, yy, hh, ll, kk):
         return (hh * 4 + yy, ll * 8 + xx * 2 + kk)
-
-    def at_z(zz):
-        return at(x, y, lax.div(zz, 2), lax.rem(zz, 2), k)
 
     xs = (lax.rem(x + 3, 4), lax.rem(x + 1, 4), lax.rem(x + 2, 4))
     ys = (lax.rem(y + 3, 4), lax.rem(y + 1, 4), lax.rem(y + 2, 4))
@@ -104,8 +99,8 @@
     mate = at(x, y, h, l, 1 - k)
     flip = at(x, y, h, 1 - l, k)
     across = at(x, y, 1 - h, 1 - l, k)
-    step = 1 - 2 * k
-    ahead = at_z(lax.rem(z + step + 4, 4))
+    opposite = at(x, y, 1 - h, l, k)
+    me = 2 * x + k
 
     def remote(src, dst, send, recv, device):
         return pltpu.make_async_remote_copy(
@@ -122,7 +117,7 @@
         pl.semaphore_signal(
             barrier, inc=1, device_id=(f, lax.rem(t + j, 16)), device_id_type=MESH
         )
-    for peer in (north, south, at(x, y, 1 - h, l, k), across):
+    for peer in (north, south, opposite, across):
         pl.semaphore_signal(barrier, inc=1, device_id=peer, device_id_type=MESH)
     pl.semaphore_wait(barrier, 19)
 
@@ -297,16 +292,6 @@
     w_start(2)
     for q in range(2):
         z_spread(1, q, True)
-    for q in range(2):
-        for j in range(2):
-            passed(2, j, 0, q)
-    w_rest(0)
-    w_rest(1)
-    for d in (3, 0, 1, 2):
-        for j in range(2):
-            for q in range(2):
-                p_in(d, j, 0, q).wait_recv()
-
     tall = 2 * rows
 
     def block(m, o):
@@ -314,65 +299,73 @@
             [xg[p * 4 + o, m].reshape(tall, shard) for p in range(2)], axis=1
         )
 
-    sa[...] = jnp.zeros_like(sa)
-
-    @pl.loop(0, 4)
-    def _(o):
+    def pair_in(d, m):
+        for q in range(2):
+            for j in range(2):
+                p_in(d, j, m, q).wait_recv()
+
+    def gate_up(d):
+        o = places[d]
         weights = jnp.concatenate([wf[o, 0], wf[o, 1]], axis=1)
-        sa[...] += jnp.dot(block(0, o), weights, preferred_element_type=F32)
-
-    def swap(src, mid, dst, send, recv):
-        def first(c):
+        term = jnp.dot(block(0, o), weights, preferred_element_type=F32)
+        sa[...] = term if d == 3 else sa[...] + term
+
+    w_rest(0)
+    w_rest(1)
+    for d in (3, 0, 1):
+        pair_in(d, 0)
+        gate_up(d)
+    for q in range(2):
+        for j in range(2):
+            passed(2, j, 0, q)
+    pair_in(2, 0)
+    gate_up(2)
+    def swap(src, dst, send, recv):
+        def copy(c):
             at_c = pl.ds(c * rows, rows)
-            return remote(src.at[at_c], mid.at[at_c], send.at[0, c], recv.at[0, c], ahead)
-
-        def second(c):
-            at_c = pl.ds(c * rows, rows)
-            return remote(mid.at[at_c], dst.at[at_c], send.at[1, c], recv.at[1, c], ahead)
-
-        return first, second
-
-    a_first, a_second = swap(sa, zra, zla, a_send, a_recv)
-    b_first, b_second = swap(sb, zrb, zlb, b_send, b_recv)
+            return remote(src.at[at_c], dst.at[at_c], send.at[c], recv.at[c], opposite)
+
+        return copy
+
+    a_swap = swap(sa, zla, a_send, a_recv)
+    b_swap = swap(sb, zlb, b_send, b_recv)
 
     for j in range(2):
         passed(0, j, 1, 0)
         passed(1, j, 1, 0)
         if j == 0:
             for c in range(2):
-                a_first(c).start()
+                a_swap(c).start()
     w_forward(2)
     for j in range(2):
         passed(1, j, 1, 1)
         passed(0, j, 1, 1)
-        a_first(j).wait_recv()
-        a_second(j).start()
-
-    def t_spot(u):
-        return pl.ds(lax.rem(u, 2) * shard + lax.div(u, 8) * wide, wide)
+
+    def t_rows(u):
+        return pl.ds(lax.rem(u, 2) * shard, shard)
 
     def t_out(j):
-        u = lax.rem(t + j, 16)
+        u = lax.rem(me + j, 8)
         return remote(
-            wf.at[lax.rem(lax.div(u, 2), 4), :, t_spot(u)],
-            tw.at[t],
+            wf.at[lax.div(u, 2), :, t_rows(u)],
+            tw.at[me],
             t_send.at[j],
             t_recv.at[j],
-            (f, u),
+            (f, l * 8 + u),
         )
 
     def t_in(j):
-        u = lax.rem(t + 16 - j, 16)
-        return remote(tw.at[u], tw.at[u], t_send.at[j], t_recv.at[j], (f, u))
-
-    @pl.loop(1, 16)
+        u = lax.rem(me + 8 - j, 8)
+        return remote(tw.at[u], tw.at[u], t_send.at[j], t_recv.at[j], (f, l * 8 + u))
+
+    @pl.loop(1, 8)
     def _(j):
         t_out(j).start()
 
-    tw[t] = wf[x, :, t_spot(t)]
+    tw[me] = wf[x, :, t_rows(me)]
 
     for c in range(2):
-        a_second(c).wait_recv()
+        a_swap(c).wait_recv()
     sums = sa[...] + zla[...]
     gate, up = sums[:, :width], sums[:, width:]
     squashed = jax.nn.sigmoid(gate)
@@ -382,23 +375,22 @@
     acts[:, width:] = activated
     hidden[...] = (activated * up).astype(BF16)
 
+    def grad_in(d):
+        o = places[d]
+        term = lax.dot_general(
+            block(1, o), df[o], (COLS, ((), ())), preferred_element_type=F32
+        )
+        sb[...] = term if d == 3 else sb[...] + term
+
+    w_rest(2)
+    for d in (3, 0, 1):
+        pair_in(d, 1)
+        grad_in(d)
     for q in range(2):
         for j in range(2):
             passed(2, j, 1, q)
-    w_rest(2)
-    for d in (3, 0, 1, 2):
-        for j in range(2):
-            for q in range(2):
-                p_in(d, j, 1, q).wait_recv()
-
-    sb[...] = jnp.zeros_like(sb)
-
-    @pl.loop(0, 4)
-    def _(o):
-        sb[...] += lax.dot_general(
-            block(1, o), df[o], (COLS, ((), ())), preferred_element_type=F32
-        )
-
+    pair_in(2, 1)
+    grad_in(2)
     def down_part(o):
         return lax.dot_general(
             hidden[...], block(1, o), (ROWS, ((), ())), preferred_element_type=F32
@@ -406,7 +398,7 @@
 
     def gate_part(o):
         return lax.dot_general(
-            block(0, o), dg[t], (ROWS, ((), ())), preferred_element_type=F32
+            block(0, o), dg[me], (ROWS, ((), ())), preferred_element_type=F32
         )
 
     twos, mids, parts, ones, lands = (
@@ -462,77 +454,59 @@
 
     dtwo[...] = down_part(ys[2]).astype(BF16)
     for c in range(2):
-        b_first(c).start()
+        b_swap(c).start()
     one_parts(0, down_part)
     for q in range(2):
         two_out(0, q).start()
     for way in range(2):
         one_out(0, way, 1 - way).start()
-    for c in range(2):
-        b_first(c).wait_recv()
-        b_second(c).start()
     down_out[...] = down_part(y)
     one_merge(0)
 
     for c in range(2):
-        b_second(c).wait_recv()
+        b_swap(c).wait_recv()
     for way in range(2):
         one_out(0, way, way).start()
 
     hidden_grad = sb[...] + zlb[...]
-    dg[t, :, :width] = (hidden_grad * acts[:, :width]).astype(BF16)
-    dg[t, :, width:] = (hidden_grad * acts[:, width:]).astype(BF16)
+    dg[me, :, :width] = (hidden_grad * acts[:, :width]).astype(BF16)
+    dg[me, :, width:] = (hidden_grad * acts[:, width:]).astype(BF16)
     gtwo[...] = gate_part(ys[2]).astype(BF16)
 
-    sides = (l, 1 - l)
-
-    def d_spot(c, o, j, q):
-        return dg.at[sides[j] * 8 + o * 2 + c, pl.ds(q * rows, rows)]
-
-    def l_out(q):
-        here = d_spot(k, x, 0, q)
-        return remote(here, here, l_send.at[q], l_recv.at[q], flip)
-
-    def l_in(q):
-        here = d_spot(k, x, 1, q)
-        return remote(here, here, l_send.at[q], l_recv.at[q], flip)
-
-    def dx_out(way, j, q):
-        here = d_spot(k, x, j, q)
-        return remote(
-            here, here, dx_send.at[way, j, q], dx_recv.at[way, j, q], (right, left)[way]
-        )
-
-    def dx_on(j, q):
-        here = d_spot(k, xs[q], j, q)
-        return remote(here, here, dx_send.at[2, j, q], dx_recv.at[2, j, q], (right, left)[q])
-
-    def dx_in(d, j, q):
-        here = d_spot(k, xs[d], j, q)
-        return remote(here, here, dx_send.at[2, j, q], dx_recv.at[d, j, q], right)
-
-    def dp_out(d, j, q):
-        here = d_spot(k, places[d], j, q)
-        return remote(here, here, dp_send.at[d, j, q], dp_recv.at[d, j, q], mate)
-
-    def dp_in(d, j, q):
-        here = d_spot(1 - k, places[d], j, q)
-        return remote(here, here, dp_send.at[d, j, q], dp_recv.at[d, j, q], mate)
-
-    def d_spread(j, q):
+    def d_spot(c, o, q):
+        return dg.at[o * 2 + c, pl.ds(q * rows, rows)]
+
+    def dx_out(way, q):
+        here = d_spot(k, x, q)
+        return remote(here, here, dx_send.at[way, q], dx_recv.at[way, q], (right, left)[way])
+
+    def dx_on(q):
+        here = d_spot(k, xs[q], q)
+        return remote(here, here, dx_send.at[2, q], dx_recv.at[2, q], (right, left)[q])
+
+    def dx_in(d, q):
+        here = d_spot(k, xs[d], q)
+        return remote(here, here, dx_send.at[2, q], dx_recv.at[d, q], right)
+
+    def dp_out(d, q):
+        here = d_spot(k, places[d], q)
+        return remote(here, here, dp_send.at[d, q], dp_recv.at[d, q], mate)
+
+    def dp_in(d, q):
+        here = d_spot(1 - k, places[d], q)
+        return remote(here, here, dp_send.at[d, q], dp_recv.at[d, q], mate)
+
+    def d_passed(d, q):
+        dx_in(d, q).wait_recv()
+        if d == q:
+            dx_on(q).start()
+        dp_out(d, q).start()
+
+    for q in range(2):
         for way in (0, 1) if q == 0 else (1, 0):
-            dx_out(way, j, q).start()
-        dp_out(3, j, q).start()
-
-    def d_passed(d, j, q):
-        dx_in(d, j, q).wait_recv()
-        if d == q:
-            dx_on(j, q).start()
-        dp_out(d, j, q).start()
-
-    for q in range(2):
-        l_out(q).start()
-        d_spread(0, q)
+            dx_out(way, q).start()
+    for q in range(2):
+        dp_out(3, q).start()
     one_parts(1, gate_part)
     for q in range(2):
         two_out(1, q).start()
@@ -540,72 +514,72 @@
         one_out(1, way, 1 - way).start()
     gown[...] = gate_part(y)
     for q in range(2):
-        l_in(q).wait_recv()
-        d_spread(1, q)
+        d_passed(q, q)
+    for q in range(2):
+        d_passed(1 - q, q)
     down_out[...] = factor * (down_out[...] + finals(0))
     one_merge(1)
-    for q in range(2):
-        d_passed(q, 0, q)
     for way in range(2):
         one_out(1, way, way).start()
-    for q in range(2):
-        d_passed(q, 1, q)
-    for j in range(2):
-        for q in range(2):
-            d_passed(1 - q, j, q)
-
-    @pl.loop(1, 16)
+    @pl.loop(1, 8)
     def _(j):
         t_in(j).wait_recv()
 
-    total[...] = jnp.zeros_like(total)
-
-    def gather(o, j):
-        base = sides[j] * 8 + o * 2
-        left_side = jnp.concatenate([dg[base], dg[base + 1]], axis=1)
+    def gather(d, at_s):
+        base = places[d] * 2
+        left_side = jnp.concatenate([dg[base, at_s], dg[base + 1, at_s]], axis=1)
         right_side = jnp.concatenate(
             [tw[base, 0], tw[base, 1], tw[base + 1, 0], tw[base + 1, 1]], axis=1
         )
-        total[...] += lax.dot_general(
+        term = lax.dot_general(
             left_side, right_side, (COLS, ((), ())), preferred_element_type=F32
         )
-
-    for d in (3, 0, 1, 2):
-        for j in range(2):
-            for q in range(2):
-                if d == 2:
-                    d_passed(2, j, q)
-            for q in range(2):
-                dp_in(d, j, q).wait_recv()
-            gather(places[d], j)
-    rounded[...] = total[...].astype(BF16)
-
-    def r_out(s):
+        total[at_s] = term if d == 3 else total[at_s] + term
+
+    for d in (3, 0, 1):
+        for q in range(2):
+            dp_in(d, q).wait_recv()
+        gather(d, pl.ds(0, tall))
+    for q in range(2):
+        d_passed(2, q)
+    for q in range(2):
+        dp_in(2, q).wait_recv()
+    mine, other = pl.ds(l * rows, rows), pl.ds((1 - l) * rows, rows)
+    gather(2, other)
+    gather(2, mine)
+
+    def f_out(c):
         return remote(
-            rounded.at[pl.ds(s * rows, rows)],
-            result.at[:, pl.ds(pl.multiple_of(l * wide, wide), wide)],
-            r_send.at[s],
-            r_recv.at[l],
-            at(x, y, s, h, k),
-        )
-
-    def r_in(e):
-        spot = result.at[:, pl.ds(e * wide, wide)]
-        return remote(spot, spot, r_send.at[0], r_recv.at[e], flip)
-
+            total.at[pl.ds((1 - l) * rows + c * part, part)],
+            near.at[pl.ds(c * part, part)],
+            f_send.at[c],
+            f_recv.at[c],
+            flip,
+        )
+
+    for c in range(2):
+        f_out(c).start()
     both = factor * (gown[...] + finals(1))
-    for s in range(2):
-
-        @pl.when((s == h) & outer)
-        def _(s=s):
-            result[:, s * wide : (s + 1) * wide] = rounded[s * rows : (s + 1) * rows, :]
-
-        @pl.when(jnp.logical_not((s == h) & outer))
-        def _(s=s):
-            r_out(s).start()
-
     gate_out[...] = both[:, :width]
     up_out[...] = both[:, width:]
+
+    def r_out(c):
+        at_c = pl.ds(c * part, part)
+        return remote(rounded.at[at_c], result.at[at_c], r_send.at[c], r_recv.at[c], across)
+
+    for c in range(2):
+        f_out(c).wait_recv()
+        rounded[c * part : (c + 1) * part] = (
+            total[pl.ds(l * rows + c * part, part)] + near[c * part : (c + 1) * part]
+        ).astype(BF16)
+    @pl.when(inner)
+    def _():
+        for c in range(2):
+            r_out(c).start()
+
+    @pl.when(outer)
+    def _():
+        result[...] = rounded[...]
 
     for m in range(2):
         for q in range(2):
@@ -627,32 +601,26 @@
                 w_out(way, w, q).wait_send()
             w_on(w, q).wait_send()
     for c in range(2):
-        for copy in (a_first(c), a_second(c), b_first(c), b_second(c), l_out(c)):
+        for copy in (a_swap(c), b_swap(c), f_out(c)):
             copy.wait_send()
         for i in range(2):
             two_out(i, c).wait_send()
             for q in range(2):
                 one_out(i, c, q).wait_send()
-        for j in range(2):
-            for way in range(2):
-                dx_out(way, j, c).wait_send()
-            dx_on(j, c).wait_send()
-            for d in range(4):
-                dp_out(d, j, c).wait_send()
-
-    @pl.loop(1, 16)
+        for way in range(2):
+            dx_out(way, c).wait_send()
+        dx_on(c).wait_send()
+        for d in range(4):
+            dp_out(d, c).wait_send()
+
+    @pl.loop(1, 8)
     def _(j):
         t_out(j).wait_send()
 
-    for s in range(2):
-
-        @pl.when(jnp.logical_not((s == h) & outer))
-        def _(s=s):
-            r_out(s).wait_send()
-
-        @pl.when(jnp.logical_not((s == l) & outer))
-        def _(s=s):
-            r_in(s).wait_recv()
+    @pl.when(inner)
+    def _():
+        for c in range(2):
+            r_out(c).wait()
 
 
 VMEM = pl.BlockSpec(memory_space=pltpu.VMEM)
@@ -685,14 +653,12 @@
                 pltpu.VMEM((4, width, deep), BF16),
                 pltpu.VMEM((tall, wide), F32),
                 pltpu.VMEM((tall, wide), F32),
-                pltpu.VMEM((tall, wide), F32),
-                pltpu.VMEM((tall, width), F32),
                 pltpu.VMEM((tall, width), F32),
                 pltpu.VMEM((tall, width), F32),
                 pltpu.VMEM((tall, wide), F32),
                 pltpu.VMEM((tall, width), BF16),
-                pltpu.VMEM((nt, tall, wide), BF16),
-                pltpu.VMEM((nt, 2, wide, width), BF16),
+                pltpu.VMEM((8, tall, wide), BF16),
+                pltpu.VMEM((8, 2, shard, width), BF16),
                 pltpu.VMEM((2, width // 2, deep), F32),
                 pltpu.VMEM((2, deep // 2, wide), F32),
                 pltpu.VMEM((width, deep), BF16),
@@ -704,8 +670,9 @@
                 pltpu.VMEM((2, width, deep), BF16),
                 pltpu.VMEM((2, deep, wide), BF16),
                 pltpu.VMEM((deep, wide), F32),
-                pltpu.VMEM((tall, wide), F32),
-                pltpu.VMEM((tall, wide), BF16),
+                pltpu.VMEM((tall, shard), F32),
+                pltpu.VMEM((rows, shard), F32),
+                pltpu.VMEM((rows, shard), BF16),
                 DMA((2, 2, 2)),
                 DMA((2, 2, 2)),
                 DMA((3, 2, 2, 2)),
@@ -714,18 +681,18 @@
                 DMA((4, 2, 2, 2)),
                 DMA((3, 3, 2)),
                 DMA((3, 3, 2)),
-                DMA((2, 2)),
-                DMA((2, 2)),
-                DMA((2, 2)),
-                DMA((2, 2)),
-                DMA((16,)),
-                DMA((16,)),
                 DMA((2,)),
                 DMA((2,)),
-                DMA((3, 2, 2)),
-                DMA((3, 2, 2)),
-                DMA((4, 2, 2)),
-                DMA((4, 2, 2)),
+                DMA((2,)),
+                DMA((2,)),
+                DMA((8,)),
+                DMA((8,)),
+                DMA((2,)),
+                DMA((2,)),
+                DMA((3, 2)),
+                DMA((3, 2)),
+                DMA((4, 2)),
+                DMA((4, 2)),
                 DMA((2, 2)),
                 DMA((2, 2)),
                 DMA((2, 2, 2)),

time: 119 us -> 114 us (0.958)
  Pallas kernels: 113 us -> 107 us
    pallas_call x1, Pallas kernels: 113 us -> 107 us  [body(): pl.pallas_call(functools.partial(kernel, factor), out_shape=(jax.ShapeDty...]
where the time goes in v2:
time: 114 us; the launch traced here: 113 us
  Pallas kernels  107 us (94%)
  local copies, waits for them, and re-layouts  4.98 us (4%)
    pallas_call x1, Pallas kernels, body(): pl.pallas_call(functools.partial(kernel, factor), out_shape=(jax.ShapeDty...  107 us
    unnamed x10, local copies, waits for them, and re-layouts  4.98 us

profile of v2, /device:TPU:32, one launch (start us, length us, event | category | flops | bytes accessed | tf_op | source)
XLA Modules:
  0.0 112.9 jit_solution(11676326057289226418)
XLA Ops:
  0.6 107.3 %block.1 = (bf16[256,512]{1,0:T(8,128)(2,1)}, f32[1024,128]{1,0:T(8,128)}, f32[1024,128]{1,0:T(8,128)}, f32[128,1024]{1,0:T(8,128)}) custom-call(bf16[256,512]{1,0:T(8,128)(2,1)} %tokens.1, bf16[256,512]{1,0:T(8,128)(2,1)} %grads.1, bf16[1024,128]{1,0:T(8,128)(2,1)} %gate_weight.1, bf16[1024,128]{1,0:T(8,128)(2,1)} %up_weight.1, bf16[128,1024]{1,0:T(8,128)(2,1)} %down_weight.1), custom_call_target="tpu_custom_call" | custom-call | tf_op jit(solution)/shard_map/block/pallas_call | solution.py:640
  107.9 0.0 copy-start.2
  108.0 1.7 %copy.13 = bf16[256,512]{1,0:T(8,128)(2,1)} copy(bf16[256,512]{1,0:T(8,128)(2,1)} %get-tuple-element.8) | data formatting | bytes 524288
  109.7 0.0 copy-done.2
  109.7 0.0 copy-start.1
  109.7 0.8 copy.14
  110.5 0.4 copy-done.1
  110.9 0.0 copy-start
  110.9 0.8 copy.15
  111.7 0.4 copy-done
  112.1 0.8 copy.16
Async XLA Ops:
  107.9 1.7 %copy-start.2 = (f32[1024,128]{1,0:T(8,128)S(1)}, f32[1024,128]{1,0:T(8,128)}, u32[]{:S(2)}) copy-start(f32[1024,128]{1,0:T(8,128)} %get-tuple-element.9) | copy-start | bytes 1572868
  109.7 1.2 %copy-start.1 = (f32[1024,128]{1,0:T(8,128)S(1)}, f32[1024,128]{1,0:T(8,128)}, u32[]{:S(2)}) copy-start(f32[1024,128]{1,0:T(8,128)} %get-tuple-element.10) | copy-start | bytes 1572868
  110.9 1.2 %copy-start = (f32[128,1024]{1,0:T(8,128)S(1)}, f32[128,1024]{1,0:T(8,128)}, u32[]{:S(2)}) copy-start(f32[128,1024]{1,0:T(8,128)} %get-tuple-element.11) | copy-start | bytes 1572868

commit v3 on v2

--- a/solution.py
+++ b/solution.py
@@ -11,7 +11,7 @@
 MESH = pl.DeviceIdType.MESH
 F32 = jnp.float32
 BF16 = jnp.bfloat16
-VMEM_LIMIT = 60 * 1024 * 1024
+VMEM_LIMIT = 40 * 1024 * 1024
 ROWS = ((0,), (0,))
 COLS = ((1,), (1,))
 
@@ -66,6 +66,8 @@
     b_recv,
     t_send,
     t_recv,
+    u_send,
+    u_recv,
     f_send,
     f_recv,
     dx_send,
@@ -312,6 +314,46 @@
 
     w_rest(0)
     w_rest(1)
+    quarter = shard // 4
+
+    def t_rows(u):
+        return pl.ds(lax.rem(u, 2) * shard + y * quarter, quarter)
+
+    def t_out(j):
+        u = lax.rem(me + j, 8)
+        return remote(
+            wf.at[lax.div(u, 2), :, t_rows(u)],
+            tw.at[me, :, pl.ds(y * quarter, quarter)],
+            t_send.at[j],
+            t_recv.at[j],
+            (f, l * 8 + u),
+        )
+
+    def t_in(j):
+        u = lax.rem(me + 8 - j, 8)
+        spot = tw.at[u, :, pl.ds(y * quarter, quarter)]
+        return remote(spot, spot, t_send.at[j], t_recv.at[j], (f, l * 8 + u))
+
+    def u_spot(o, q):
+        return tw.at[pl.ds(q * 4, 4), :, pl.ds(o * quarter, quarter)]
+
+    def u_out(way, q):
+        here = u_spot(y, q)
+        return remote(here, here, u_send.at[way, q], u_recv.at[way, q], (north, south)[way])
+
+    def u_on(q):
+        here = u_spot(ys[q], q)
+        return remote(here, here, u_send.at[2, q], u_recv.at[2, q], (north, south)[q])
+
+    def u_in(d, q):
+        here = u_spot(ys[d], q)
+        return remote(here, here, u_send.at[2, q], u_recv.at[d, q], north)
+
+    @pl.loop(1, 8)
+    def _(j):
+        t_out(j).start()
+
+    tw[me, :, pl.ds(y * quarter, quarter)] = wf[x, :, t_rows(me)]
     for d in (3, 0, 1):
         pair_in(d, 0)
         gate_up(d)
@@ -341,29 +383,12 @@
         passed(1, j, 1, 1)
         passed(0, j, 1, 1)
 
-    def t_rows(u):
-        return pl.ds(lax.rem(u, 2) * shard, shard)
-
-    def t_out(j):
-        u = lax.rem(me + j, 8)
-        return remote(
-            wf.at[lax.div(u, 2), :, t_rows(u)],
-            tw.at[me],
-            t_send.at[j],
-            t_recv.at[j],
-            (f, l * 8 + u),
-        )
-
-    def t_in(j):
-        u = lax.rem(me + 8 - j, 8)
-        return remote(tw.at[u], tw.at[u], t_send.at[j], t_recv.at[j], (f, l * 8 + u))
-
     @pl.loop(1, 8)
     def _(j):
-        t_out(j).start()
-
-    tw[me] = wf[x, :, t_rows(me)]
-
+        t_in(j).wait_recv()
+
+    for way, q in ((0, 0), (1, 1), (0, 1), (1, 0)):
+        u_out(way, q).start()
     for c in range(2):
         a_swap(c).wait_recv()
     sums = sa[...] + zla[...]
@@ -460,6 +485,9 @@
         two_out(0, q).start()
     for way in range(2):
         one_out(0, way, 1 - way).start()
+    for q in range(2):
+        u_in(q, q).wait_recv()
+        u_on(q).start()
     down_out[...] = down_part(y)
     one_merge(0)
 
@@ -473,109 +501,124 @@
     dg[me, :, width:] = (hidden_grad * acts[:, width:]).astype(BF16)
     gtwo[...] = gate_part(ys[2]).astype(BF16)
 
-    def d_spot(c, o, q):
-        return dg.at[o * 2 + c, pl.ds(q * rows, rows)]
-
-    def dx_out(way, q):
-        here = d_spot(k, x, q)
-        return remote(here, here, dx_send.at[way, q], dx_recv.at[way, q], (right, left)[way])
-
-    def dx_on(q):
-        here = d_spot(k, xs[q], q)
-        return remote(here, here, dx_send.at[2, q], dx_recv.at[2, q], (right, left)[q])
-
-    def dx_in(d, q):
-        here = d_spot(k, xs[d], q)
-        return remote(here, here, dx_send.at[2, q], dx_recv.at[d, q], right)
-
-    def dp_out(d, q):
-        here = d_spot(k, places[d], q)
-        return remote(here, here, dp_send.at[d, q], dp_recv.at[d, q], mate)
-
-    def dp_in(d, q):
-        here = d_spot(1 - k, places[d], q)
-        return remote(here, here, dp_send.at[d, q], dp_recv.at[d, q], mate)
-
-    def d_passed(d, q):
-        dx_in(d, q).wait_recv()
+    turn = (1 - l, l)
+
+    def d_spot(c, o, e, q):
+        return dg.at[o * 2 + c, pl.ds(turn[e] * rows + q * part, part)]
+
+    def dx_out(way, e, q):
+        here = d_spot(k, x, e, q)
+        return remote(
+            here, here, dx_send.at[way, e, q], dx_recv.at[way, e, q], (right, left)[way]
+        )
+
+    def dx_on(e, q):
+        here = d_spot(k, xs[q], e, q)
+        return remote(here, here, dx_send.at[2, e, q], dx_recv.at[2, e, q], (right, left)[q])
+
+    def dx_in(d, e, q):
+        here = d_spot(k, xs[d], e, q)
+        return remote(here, here, dx_send.at[2, e, q], dx_recv.at[d, e, q], right)
+
+    def dp_out(d, e, q):
+        here = d_spot(k, places[d], e, q)
+        return remote(here, here, dp_send.at[d, e, q], dp_recv.at[d, e, q], mate)
+
+    def dp_in(d, e, q):
+        here = d_spot(1 - k, places[d], e, q)
+        return remote(here, here, dp_send.at[d, e, q], dp_recv.at[d, e, q], mate)
+
+    def d_start(e):
+        for q in range(2):
+            for way in (0, 1) if q == 0 else (1, 0):
+                dx_out(way, e, q).start()
+            dp_out(3, e, q).start()
+
+    def d_passed(d, e, q):
+        dx_in(d, e, q).wait_recv()
         if d == q:
-            dx_on(q).start()
-        dp_out(d, q).start()
-
-    for q in range(2):
-        for way in (0, 1) if q == 0 else (1, 0):
-            dx_out(way, q).start()
-    for q in range(2):
-        dp_out(3, q).start()
+            dx_on(e, q).start()
+        dp_out(d, e, q).start()
+
+    def d_near(e):
+        for q in range(2):
+            d_passed(q, e, q)
+        for q in range(2):
+            d_passed(1 - q, e, q)
+
+    def gather(d, e):
+        base = places[d] * 2
+        at_s = pl.ds(turn[e] * rows, rows)
+        left_side = jnp.concatenate([dg[base, at_s], dg[base + 1, at_s]], axis=1)
+        right_side = jnp.concatenate(
+            [tw[base, 0], tw[base, 1], tw[base + 1, 0], tw[base + 1, 1]], axis=1
+        )
+        term = lax.dot_general(
+            left_side, right_side, (COLS, ((), ())), preferred_element_type=F32
+        )
+        total[e] = term if d == 3 else total[e] + term
+
+    def gathers(e, ds):
+        for d in ds:
+            for q in range(2):
+                dp_in(d, e, q).wait_recv()
+            gather(d, e)
+
+    piece = rows // 4
+
+    def f_out(c):
+        at_c = pl.ds(c * piece, piece)
+        return remote(total.at[0, at_c], near.at[at_c], f_send.at[c], f_recv.at[c], flip)
+
+    def r_out(c):
+        at_c = pl.ds(c * piece, piece)
+        return remote(rounded.at[at_c], result.at[at_c], r_send.at[c], r_recv.at[c], across)
+
+    d_start(0)
     one_parts(1, gate_part)
     for q in range(2):
         two_out(1, q).start()
     for way in range(2):
         one_out(1, way, 1 - way).start()
     gown[...] = gate_part(y)
-    for q in range(2):
-        d_passed(q, q)
-    for q in range(2):
-        d_passed(1 - q, q)
-    down_out[...] = factor * (down_out[...] + finals(0))
+    d_near(0)
+    d_start(1)
+    for q in range(2):
+        u_in(1 - q, q).wait_recv()
+        u_in(2, q).wait_recv()
+    gathers(0, (3, 0, 1))
+    for q in range(2):
+        d_passed(2, 0, q)
+    gathers(0, (2,))
+    d_near(1)
+    for c in range(4):
+        f_out(c).start()
     one_merge(1)
+    gathers(1, (3,))
     for way in range(2):
         one_out(1, way, way).start()
-    @pl.loop(1, 8)
-    def _(j):
-        t_in(j).wait_recv()
-
-    def gather(d, at_s):
-        base = places[d] * 2
-        left_side = jnp.concatenate([dg[base, at_s], dg[base + 1, at_s]], axis=1)
-        right_side = jnp.concatenate(
-            [tw[base, 0], tw[base, 1], tw[base + 1, 0], tw[base + 1, 1]], axis=1
-        )
-        term = lax.dot_general(
-            left_side, right_side, (COLS, ((), ())), preferred_element_type=F32
-        )
-        total[at_s] = term if d == 3 else total[at_s] + term
-
-    for d in (3, 0, 1):
-        for q in range(2):
-            dp_in(d, q).wait_recv()
-        gather(d, pl.ds(0, tall))
-    for q in range(2):
-        d_passed(2, q)
-    for q in range(2):
-        dp_in(2, q).wait_recv()
-    mine, other = pl.ds(l * rows, rows), pl.ds((1 - l) * rows, rows)
-    gather(2, other)
-    gather(2, mine)
-
-    def f_out(c):
-        return remote(
-            total.at[pl.ds((1 - l) * rows + c * part, part)],
-            near.at[pl.ds(c * part, part)],
-            f_send.at[c],
-            f_recv.at[c],
-            flip,
-        )
-
-    for c in range(2):
-        f_out(c).start()
+    gathers(1, (0, 1))
+    for q in range(2):
+        d_passed(2, 1, q)
+    gathers(1, (2,))
+    down_out[...] = factor * (down_out[...] + finals(0))
+    for c in range(4):
+        f_out(c).wait_recv()
+        at_c = pl.ds(c * piece, piece)
+        rounded[at_c] = (total[1, at_c] + near[at_c]).astype(BF16)
+
+        if c:
+
+            @pl.when(inner)
+            def _(c=c):
+                r_out(c - 1).start()
+
     both = factor * (gown[...] + finals(1))
     gate_out[...] = both[:, :width]
     up_out[...] = both[:, width:]
-
-    def r_out(c):
-        at_c = pl.ds(c * part, part)
-        return remote(rounded.at[at_c], result.at[at_c], r_send.at[c], r_recv.at[c], across)
-
-    for c in range(2):
-        f_out(c).wait_recv()
-        rounded[c * part : (c + 1) * part] = (
-            total[pl.ds(l * rows + c * part, part)] + near[c * part : (c + 1) * part]
-        ).astype(BF16)
     @pl.when(inner)
     def _():
-        for c in range(2):
-            r_out(c).start()
+        r_out(3).start()
 
     @pl.when(outer)
     def _():
@@ -601,17 +644,21 @@
                 w_out(way, w, q).wait_send()
             w_on(w, q).wait_send()
     for c in range(2):
-        for copy in (a_swap(c), b_swap(c), f_out(c)):
+        for copy in (a_swap(c), b_swap(c), f_out(c), f_out(2 + c)):
             copy.wait_send()
         for i in range(2):
             two_out(i, c).wait_send()
             for q in range(2):
                 one_out(i, c, q).wait_send()
         for way in range(2):
-            dx_out(way, c).wait_send()
-        dx_on(c).wait_send()
-        for d in range(4):
-            dp_out(d, c).wait_send()
+            u_out(way, c).wait_send()
+        u_on(c).wait_send()
+        for e in range(2):
+            for way in range(2):
+                dx_out(way, e, c).wait_send()
+            dx_on(e, c).wait_send()
+            for d in range(4):
+                dp_out(d, e, c).wait_send()
 
     @pl.loop(1, 8)
     def _(j):
@@ -619,7 +666,7 @@
 
     @pl.when(inner)
     def _():
-        for c in range(2):
+        for c in range(4):
             r_out(c).wait()
 
 
@@ -670,7 +717,7 @@
                 pltpu.VMEM((2, width, deep), BF16),
                 pltpu.VMEM((2, deep, wide), BF16),
                 pltpu.VMEM((deep, wide), F32),
-                pltpu.VMEM((tall, shard), F32),
+                pltpu.VMEM((2, rows, shard), F32),
                 pltpu.VMEM((rows, shard), F32),
                 pltpu.VMEM((rows, shard), BF16),
                 DMA((2, 2, 2)),
@@ -687,18 +734,20 @@
                 DMA((2,)),
                 DMA((8,)),
                 DMA((8,)),
-                DMA((2,)),
-                DMA((2,)),
                 DMA((3, 2)),
                 DMA((3, 2)),
-                DMA((4, 2)),
-                DMA((4, 2)),
+                DMA((4,)),
+                DMA((4,)),
+                DMA((3, 2, 2)),
+                DMA((3, 2, 2)),
+                DMA((4, 2, 2)),
+                DMA((4, 2, 2)),
                 DMA((2, 2)),
                 DMA((2, 2)),
                 DMA((2, 2, 2)),
                 DMA((2, 2, 2)),
-                DMA((2,)),
-                DMA((2,)),
+                DMA((4,)),
+                DMA((4,)),
             ],
             compiler_params=pltpu.CompilerParams(
                 collective_id=0, has_side_effects=True, vmem_limit_bytes=VMEM_LIMIT

time: 114 us -> 107 us (0.939)
  Pallas kernels: 107 us -> 97.8 us
  local copies, waits for them, and re-layouts: 4.98 us -> 7.82 us
    pallas_call x1, Pallas kernels: 107 us -> 97.8 us  [body(): pl.pallas_call(functools.partial(kernel, factor), out_shape=(jax.ShapeDty...]
    unnamed x10 -> x14, local copies, waits for them, and re-layouts: 4.98 us -> 7.82 us
where the time goes in v3:
time: 107 us; the launch traced here: 106 us
  Pallas kernels  97.8 us (91%)
  local copies, waits for them, and re-layouts  7.82 us (7%)
    pallas_call x1, Pallas kernels, body(): pl.pallas_call(functools.partial(kernel, factor), out_shape=(jax.ShapeDty...  97.8 us
    unnamed x14, local copies, waits for them, and re-layouts  7.82 us

profile of v3, /device:TPU:32, one launch (start us, length us, event | category | flops | bytes accessed | tf_op | source)
XLA Modules:
  0.0 106.3 jit_solution(748361195700944340)
XLA Ops:
  0.6 0.0 copy-start
  0.6 0.9 copy-done
  1.6 0.0 copy-start.1
  1.6 0.9 copy-done.1
  2.5 0.0 copy-start.2
  2.5 0.9 copy-done.2
  3.5 0.0 copy-start.3
  3.5 0.9 copy-done.3
  4.4 0.0 copy-start.4
  4.4 0.9 copy-done.4
  5.4 97.8 %block.1 = (bf16[256,512]{1,0:T(8,128)(2,1)S(1)}, f32[1024,128]{1,0:T(8,128)S(1)}, f32[1024,128]{1,0:T(8,128)S(1)}, f32[128,1024]{1,0:T(8,128)S(1)}) custom-call(bf16[256,512]{1,0:T(8,128)(2,1)S(1)} %copy-done, bf16[256,512]{1,0:T(8,128)(2,1)S(1)} %copy-done.1, bf16[1024,128]{1,0:T(8,128)(2,1)S(1)} %copy-done.2, bf16[1024,128]{1,0:T(8,128)(2,1)S(1)} %copy-done.3, ...), custom_call_target="tpu_custom_call" | custom-call | tf_op jit(solution)/shard_map/block/pallas_call | solution.py:687
  103.2 0.7 copy.13
  103.9 0.8 copy.14
  104.7 0.8 copy.15
  105.5 0.8 copy.16
Async XLA Ops:
  0.6 1.0 copy-start
  1.6 0.9 copy-start.1
  2.5 0.9 copy-start.2
  3.5 0.9 copy-start.3
  4.4 0.9 copy-start.4

commit v4 on v3

--- a/solution.py
+++ b/solution.py
@@ -11,7 +11,7 @@
 MESH = pl.DeviceIdType.MESH
 F32 = jnp.float32
 BF16 = jnp.bfloat16
-VMEM_LIMIT = 40 * 1024 * 1024
+VMEM_LIMIT = 60 * 1024 * 1024
 ROWS = ((0,), (0,))
 COLS = ((1,), (1,))
 
@@ -27,6 +27,10 @@
     gate_out,
     up_out,
     down_out,
+    gate_own,
+    up_own,
+    down_own,
+    held,
     xg,
     wf,
     df,
@@ -52,6 +56,8 @@
     total,
     near,
     rounded,
+    load,
+    keep,
     z_send,
     z_recv,
     x_send,
@@ -114,6 +120,30 @@
             device_id_type=MESH,
         )
 
+    copies = [
+        pltpu.make_async_copy(ref, spot, load.at[i])
+        for i, (ref, spot) in enumerate(
+            (
+                (tokens, held.at[0]),
+                (gate_weight, wf.at[y, 0]),
+                (up_weight, wf.at[y, 1]),
+                (grads, held.at[1]),
+                (down_weight, df.at[y]),
+            )
+        )
+    ]
+    kept = [
+        pltpu.make_async_copy(ref, xg.at[k * 4 + x, m, h], load.at[5 + m])
+        for m, ref in enumerate((tokens, grads))
+    ]
+    for copy in copies:
+        copy.start()
+
+    @pl.when(outer)
+    def _():
+        for copy in kept:
+            copy.start()
+
     barrier = pltpu.get_barrier_semaphore()
     for j in range(1, 16):
         pl.semaphore_signal(
@@ -123,11 +153,13 @@
         pl.semaphore_signal(barrier, inc=1, device_id=peer, device_id_type=MESH)
     pl.semaphore_wait(barrier, 19)
 
-    ups = (gate_weight, up_weight, down_weight)
-
-    def w_own(w, q):
-        size = ups[w].shape[0] // 2
-        return ups[w].at[pl.ds(q * size, size)]
+    for copy in copies:
+        copy.wait()
+
+    @pl.when(outer)
+    def _():
+        for copy in kept:
+            copy.wait()
 
     def w_spot(o, w, q):
         if w == 2:
@@ -136,7 +168,7 @@
 
     def w_out(way, w, q):
         return remote(
-            w_own(w, q),
+            w_spot(y, w, q),
             w_spot(y, w, q),
             y_send.at[way, w, q],
             y_recv.at[way, w, q],
@@ -165,11 +197,10 @@
             w_in(1 - q, w, q).wait_recv()
             w_in(2, w, q).wait_recv()
 
-    own = (tokens, grads)
     slot = (h, 1 - h)
 
     def x_own(m, q):
-        return own[m].at[pl.ds(q * part, part)]
+        return held.at[m, pl.ds(q * part, part)]
 
     def x_spot(p, o, j, m, q):
         return xg.at[p * 4 + o, m, slot[j], pl.ds(q * part, part)]
@@ -269,49 +300,20 @@
     w_start(0)
     w_start(1)
 
-    @pl.when(outer)
-    def _():
-        for m in range(2):
-            xg[k * 4 + x, m, h] = own[m][...]
-
-    wf[y, 0] = gate_weight[...]
-    wf[y, 1] = up_weight[...]
-    df[y] = down_weight[...]
-
     for q in range(2):
         z_forward(0, q)
         z_spread(0, q, False)
+    w_forward(0)
     for j in range(2):
         passed(0, j, 0, 0)
         passed(1, j, 0, 0)
     z_forward(1, 0)
-    w_forward(0)
+    w_forward(1)
+    w_start(2)
     for j in range(2):
         passed(1, j, 0, 1)
         passed(0, j, 0, 1)
     z_forward(1, 1)
-    w_forward(1)
-    w_start(2)
-    for q in range(2):
-        z_spread(1, q, True)
-    tall = 2 * rows
-
-    def block(m, o):
-        return jnp.concatenate(
-            [xg[p * 4 + o, m].reshape(tall, shard) for p in range(2)], axis=1
-        )
-
-    def pair_in(d, m):
-        for q in range(2):
-            for j in range(2):
-                p_in(d, j, m, q).wait_recv()
-
-    def gate_up(d):
-        o = places[d]
-        weights = jnp.concatenate([wf[o, 0], wf[o, 1]], axis=1)
-        term = jnp.dot(block(0, o), weights, preferred_element_type=F32)
-        sa[...] = term if d == 3 else sa[...] + term
-
     w_rest(0)
     w_rest(1)
     quarter = shard // 4
@@ -354,6 +356,26 @@
         t_out(j).start()
 
     tw[me, :, pl.ds(y * quarter, quarter)] = wf[x, :, t_rows(me)]
+    for q in range(2):
+        z_spread(1, q, True)
+    tall = 2 * rows
+
+    def block(m, o):
+        return jnp.concatenate(
+            [xg[p * 4 + o, m].reshape(tall, shard) for p in range(2)], axis=1
+        )
+
+    def pair_in(d, m):
+        for q in range(2):
+            for j in range(2):
+                p_in(d, j, m, q).wait_recv()
+
+    def gate_up(d):
+        o = places[d]
+        weights = jnp.concatenate([wf[o, 0], wf[o, 1]], axis=1)
+        term = jnp.dot(block(0, o), weights, preferred_element_type=F32)
+        sa[...] = term if d == 3 else sa[...] + term
+
     for d in (3, 0, 1):
         pair_in(d, 0)
         gate_up(d)
@@ -488,13 +510,10 @@
     for q in range(2):
         u_in(q, q).wait_recv()
         u_on(q).start()
-    down_out[...] = down_part(y)
-    one_merge(0)
+    down_own[...] = down_part(y)
 
     for c in range(2):
         b_swap(c).wait_recv()
-    for way in range(2):
-        one_out(0, way, way).start()
 
     hidden_grad = sb[...] + zlb[...]
     dg[me, :, :width] = (hidden_grad * acts[:, :width]).astype(BF16)
@@ -583,9 +602,12 @@
     gown[...] = gate_part(y)
     d_near(0)
     d_start(1)
+    one_merge(0)
     for q in range(2):
         u_in(1 - q, q).wait_recv()
         u_in(2, q).wait_recv()
+    for way in range(2):
+        one_out(0, way, way).start()
     gathers(0, (3, 0, 1))
     for q in range(2):
         d_passed(2, 0, q)
@@ -601,7 +623,14 @@
     for q in range(2):
         d_passed(2, 1, q)
     gathers(1, (2,))
-    down_out[...] = factor * (down_out[...] + finals(0))
+    down_own[...] = factor * (down_own[...] + finals(0))
+    keeps = [
+        pltpu.make_async_copy(src, dst, keep.at[i])
+        for i, (src, dst) in enumerate(
+            ((down_own, down_out), (gate_own, gate_out), (up_own, up_out), (rounded, result))
+        )
+    ]
+    keeps[0].start()
     for c in range(4):
         f_out(c).wait_recv()
         at_c = pl.ds(c * piece, piece)
@@ -614,15 +643,18 @@
                 r_out(c - 1).start()
 
     both = factor * (gown[...] + finals(1))
-    gate_out[...] = both[:, :width]
-    up_out[...] = both[:, width:]
+    gate_own[...] = both[:, :width]
+    up_own[...] = both[:, width:]
     @pl.when(inner)
     def _():
         r_out(3).start()
 
     @pl.when(outer)
     def _():
-        result[...] = rounded[...]
+        keeps[3].start()
+
+    for copy in keeps[1:3]:
+        copy.start()
 
     for m in range(2):
         for q in range(2):
@@ -669,8 +701,28 @@
         for c in range(4):
             r_out(c).wait()
 
-
-VMEM = pl.BlockSpec(memory_space=pltpu.VMEM)
+    @pl.when(outer)
+    def _():
+        keeps[3].wait()
+
+    for copy in keeps[:3]:
+        copy.wait()
+
+
+def store_kernel(*refs):
+    found, kept, held, sem = refs[:4], refs[4:8], refs[8:12], refs[12]
+    loads = [pltpu.make_async_copy(found[i], held[i], sem.at[0, i]) for i in range(4)]
+    stores = [pltpu.make_async_copy(held[i], kept[i], sem.at[1, i]) for i in range(4)]
+    for copy in loads:
+        copy.start()
+    for i in range(4):
+        loads[i].wait()
+        stores[i].start()
+    for copy in stores:
+        copy.wait()
+
+
+HBM = pl.BlockSpec(memory_space=pltpu.HBM)
 DMA = pltpu.SemaphoreType.DMA
 
 
@@ -683,18 +735,23 @@
     tall = 2 * rows
     wide = 2 * width
 
-    return tuple(
+    shapes = (
+        jax.ShapeDtypeStruct((rows, shard), BF16),
+        jax.ShapeDtypeStruct((deep, width), F32),
+        jax.ShapeDtypeStruct((deep, width), F32),
+        jax.ShapeDtypeStruct((width, deep), F32),
+    )
+    found = tuple(
         pl.pallas_call(
             functools.partial(kernel, factor),
-            out_shape=(
-                jax.ShapeDtypeStruct((rows, shard), BF16),
-                jax.ShapeDtypeStruct((deep, width), F32),
-                jax.ShapeDtypeStruct((deep, width), F32),
-                jax.ShapeDtypeStruct((width, deep), F32),
-            ),
-            in_specs=[VMEM] * 5,
-            out_specs=(VMEM,) * 4,
+            out_shape=shapes,
+            in_specs=[HBM] * 5,
+            out_specs=(HBM,) * 4,
             scratch_shapes=[
+                pltpu.VMEM((deep, width), F32),
+                pltpu.VMEM((deep, width), F32),
+                pltpu.VMEM((width, deep), F32),
+                pltpu.VMEM((2, rows, shard), BF16),
                 pltpu.VMEM((8, 2, 2, rows, shard), BF16),
                 pltpu.VMEM((4, 2, deep, width), BF16),
                 pltpu.VMEM((4, width, deep), BF16),
@@ -720,6 +777,8 @@
                 pltpu.VMEM((2, rows, shard), F32),
                 pltpu.VMEM((rows, shard), F32),
                 pltpu.VMEM((rows, shard), BF16),
+                DMA((7,)),
+                DMA((4,)),
                 DMA((2, 2, 2)),
                 DMA((2, 2, 2)),
                 DMA((3, 2, 2, 2)),
@@ -755,6 +814,17 @@
             name="block",
         )(tokens, out_grad, gate_weight, up_weight, down_weight)
     )
+    return tuple(
+        pl.pallas_call(
+            store_kernel,
+            out_shape=shapes,
+            in_specs=[HBM] * 4,
+            out_specs=(HBM,) * 4,
+            scratch_shapes=[pltpu.VMEM(s.shape, s.dtype) for s in shapes] + [DMA((2, 4))],
+            compiler_params=pltpu.CompilerParams(vmem_limit_bytes=VMEM_LIMIT),
+            name="store",
+        )(*found)
+    )
 
 
 def solution(mesh):

time: 107 us -> 98.5 us (0.921)
  local copies, waits for them, and re-layouts: 7.82 us -> 0 us
    unnamed x14 -> x0, local copies, waits for them, and re-layouts: 7.82 us -> none
    pallas_call x1 -> x2, Pallas kernels: 97.8 us -> 97.7 us  [the longest x1 95.4 us: body(): pl.pallas_call(functools.partial(kernel, factor), out_shape=shapes, in_sp...]
where the time goes in v4:
time: 98.5 us; the launch traced here: 98.4 us
  Pallas kernels  97.7 us (99%)
    pallas_call x1, Pallas kernels, body(): pl.pallas_call(functools.partial(kernel, factor), out_shape=shapes, in_sp...  95.4 us
    pallas_call x1, Pallas kernels, body(): pl.pallas_call(store_kernel, out_shape=shapes, in_specs=[HBM] * 4, out_sp...  2.33 us

profile of v4, /device:TPU:32, one launch (start us, length us, event | category | flops | bytes accessed | tf_op | source)
XLA Modules:
  0.0 98.4 jit_solution(13501010582972737514)
XLA Ops:
  0.6 95.4 %block.1 = (bf16[256,512]{1,0:T(8,128)(2,1)}, f32[1024,128]{1,0:T(8,128)}, f32[1024,128]{1,0:T(8,128)}, f32[128,1024]{1,0:T(8,128)}) custom-call(bf16[256,512]{1,0:T(8,128)(2,1)} %tokens.1, bf16[256,512]{1,0:T(8,128)(2,1)} %grads.1, bf16[1024,128]{1,0:T(8,128)(2,1)} %gate_weight.1, bf16[1024,128]{1,0:T(8,128)(2,1)} %up_weight.1, bf16[128,1024]{1,0:T(8,128)(2,1)} %down_weight.1), custom_call_target="tpu_custom_call" | custom-call | tf_op jit(solution)/shard_map/block/pallas_call | solution.py:745
  96.0 2.3 %store.1 = (bf16[256,512]{1,0:T(8,128)(2,1)}, f32[1024,128]{1,0:T(8,128)}, f32[1024,128]{1,0:T(8,128)}, f32[128,1024]{1,0:T(8,128)}) custom-call(bf16[256,512]{1,0:T(8,128)(2,1)} %get-tuple-element.8.refs_0_, f32[1024,128]{1,0:T(8,128)} %get-tuple-element.9.refs_1_, f32[1024,128]{1,0:T(8,128)} %get-tuple-element.10.refs_2_, ...), custom_call_target="tpu_custom_call" | custom-call | tf_op jit(solution)/shard_map/store/pallas_call | solution.py:818

commit v5 on v4

--- a/solution.py
+++ b/solution.py
@@ -12,6 +12,7 @@
 F32 = jnp.float32
 BF16 = jnp.bfloat16
 VMEM_LIMIT = 60 * 1024 * 1024
+XFIRST = 64
 ROWS = ((0,), (0,))
 COLS = ((1,), (1,))
 
@@ -30,7 +31,6 @@
     gate_own,
     up_own,
     down_own,
-    held,
     xg,
     wf,
     df,
@@ -64,6 +64,12 @@
     x_recv,
     p_send,
     p_recv,
+    v_send,
+    v_recv,
+    zx_send,
+    zx_recv,
+    px_send,
+    px_recv,
     y_send,
     y_recv,
     a_send,
@@ -95,6 +101,10 @@
     rows, shard = tokens.shape
     deep, width = gate_weight.shape
     part = rows // 2
+    zpart = (rows - XFIRST) // 2
+    xpart = XFIRST // 2
+    odd = (h - l) * (h - l)
+    home = h * (1 - odd) + 2 * odd
     wide = 2 * width
 
     def at(xx, yy, hh, ll, kk):
@@ -124,25 +134,16 @@
         pltpu.make_async_copy(ref, spot, load.at[i])
         for i, (ref, spot) in enumerate(
             (
-                (tokens, held.at[0]),
+                (tokens, xg.at[k * 4 + x, 0, home]),
                 (gate_weight, wf.at[y, 0]),
                 (up_weight, wf.at[y, 1]),
-                (grads, held.at[1]),
+                (grads, xg.at[k * 4 + x, 1, home]),
                 (down_weight, df.at[y]),
             )
         )
-    ]
-    kept = [
-        pltpu.make_async_copy(ref, xg.at[k * 4 + x, m, h], load.at[5 + m])
-        for m, ref in enumerate((tokens, grads))
     ]
     for copy in copies:
         copy.start()
-
-    @pl.when(outer)
-    def _():
-        for copy in kept:
-            copy.start()
 
     barrier = pltpu.get_barrier_semaphore()
     for j in range(1, 16):
@@ -155,11 +156,6 @@
 
     for copy in copies:
         copy.wait()
-
-    @pl.when(outer)
-    def _():
-        for copy in kept:
-            copy.wait()
 
     def w_spot(o, w, q):
         if w == 2:
@@ -200,13 +196,13 @@
     slot = (h, 1 - h)
 
     def x_own(m, q):
-        return held.at[m, pl.ds(q * part, part)]
+        return xg.at[k * 4 + x, m, home, pl.ds(q * zpart, zpart)]
 
     def x_spot(p, o, j, m, q):
-        return xg.at[p * 4 + o, m, slot[j], pl.ds(q * part, part)]
+        return xg.at[p * 4 + o, m, slot[j], pl.ds(q * zpart, zpart)]
 
     def z_out(m, q, device, j):
-        spot = xg.at[k * 4 + x, m, h, pl.ds(q * part, part)]
+        spot = xg.at[k * 4 + x, m, h, pl.ds(q * zpart, zpart)]
         return remote(x_own(m, q), spot, z_send.at[0, m, q], z_recv.at[j, m, q], device)
 
     def z_on(m, q):
@@ -282,37 +278,145 @@
 
         spread(x_spot(k, x, 1, m, q), 1, m, q)
 
+    def v_spot(o, m, q):
+        return xg.at[k * 4 + o, m, home, pl.ds(2 * zpart + q * xpart, xpart)]
+
+    def v_out(way, m, q):
+        here = v_spot(x, m, q)
+        return remote(
+            here, here, v_send.at[way, m, q], v_recv.at[way, m, q], (right, left)[way]
+        )
+
+    def v_on(m, q):
+        here = v_spot(xs[q], m, q)
+        return remote(here, here, v_send.at[2, m, q], v_recv.at[2, m, q], (right, left)[q])
+
+    def v_in(d, m, q):
+        here = v_spot(xs[d], m, q)
+        return remote(here, here, v_send.at[2, m, q], v_recv.at[d, m, q], right)
+
+    def zx_spot(p, d, m, at_s):
+        return xg.at[p * 4 + places[d], m, at_s, pl.ds(2 * zpart, XFIRST)]
+
+    def zx_out(d, m, device, j):
+        return remote(
+            zx_spot(k, d, m, home),
+            zx_spot(k, d, m, h),
+            zx_send.at[0, d, m],
+            zx_recv.at[j, d, m],
+            device,
+        )
+
+    def zx_on(d, m):
+        here = zx_spot(k, d, m, 1 - h)
+        return remote(here, here, zx_send.at[1, d, m], zx_recv.at[1, d, m], flip)
+
+    def zx_in(j, d, m):
+        here = zx_spot(k, d, m, slot[j])
+        return remote(here, here, zx_send.at[0, d, m], zx_recv.at[j, d, m], flip)
+
+    def px_out(d, j, m):
+        here = zx_spot(k, d, m, slot[j])
+        return remote(here, here, px_send.at[d, j, m], px_recv.at[d, j, m], mate)
+
+    def px_in(d, j, m):
+        here = zx_spot(1 - k, d, m, slot[j])
+        return remote(here, here, px_send.at[d, j, m], px_recv.at[d, j, m], mate)
+
+    def v_start(m):
+        for q in range(2):
+            for way in (0, 1) if q == 0 else (1, 0):
+                v_out(way, m, q).start()
+
+    def v_near(m):
+        for q in range(2):
+            v_in(q, m, q).wait_recv()
+            v_on(m, q).start()
+        for q in range(2):
+            v_in(1 - q, m, q).wait_recv()
+
+    def v_far(m):
+        for q in range(2):
+            v_in(2, m, q).wait_recv()
+
+    def zx_start(m, ds):
+        for d in ds:
+
+            @pl.when(outer)
+            def _(d=d):
+                zx_out(d, m, flip, 0).start()
+                px_out(d, 0, m).start()
+
+            @pl.when(inner)
+            def _(d=d):
+                zx_out(d, m, across, 1).start()
+
+    def zx_take(m, ds):
+        for d in ds:
+
+            @pl.when(inner)
+            def _(d=d):
+                zx_in(1, d, m).wait_recv()
+                zx_on(d, m).start()
+                px_out(d, 1, m).start()
+                zx_in(0, d, m).wait_recv()
+                px_out(d, 0, m).start()
+
+            @pl.when(outer)
+            def _(d=d):
+                zx_in(1, d, m).wait_recv()
+                px_out(d, 1, m).start()
+
+    def z_start(m):
+        @pl.when(outer)
+        def _():
+            for q in range(2):
+                z_out(m, q, flip, 0).start()
+
+        @pl.when(inner)
+        def _():
+            for q in range(2):
+                z_out(m, q, across, 1).start()
+
+    v_start(0)
+    z_start(0)
+
     @pl.when(outer)
     def _():
-        for m in range(2):
-            for q in range(2):
-                z_out(m, q, flip, 0).start()
-            if m == 0:
-                for q in range(2):
-                    spread(x_own(0, q), 0, 0, q)
-
-    @pl.when(inner)
-    def _():
-        for m in range(2):
-            for q in range(2):
-                z_out(m, q, across, 1).start()
-
+        for q in range(2):
+            spread(x_own(0, q), 0, 0, q)
+
+    zx_start(0, (3,))
     w_start(0)
     w_start(1)
 
-    for q in range(2):
-        z_forward(0, q)
-        z_spread(0, q, False)
+    v_near(0)
+    zx_start(0, (0, 1))
+    z_forward(0, 0)
+    z_spread(0, 0, False)
+    v_far(0)
+    zx_start(0, (2,))
+    z_start(1)
+    v_start(1)
+    zx_start(1, (3,))
+    z_forward(0, 1)
+    z_spread(0, 1, False)
     w_forward(0)
     for j in range(2):
         passed(0, j, 0, 0)
         passed(1, j, 0, 0)
+    zx_take(0, (3, 0, 1))
+    v_near(1)
+    zx_start(1, (0, 1))
     z_forward(1, 0)
     w_forward(1)
     w_start(2)
     for j in range(2):
         passed(1, j, 0, 1)
         passed(0, j, 0, 1)
+    zx_take(0, (2,))
+    v_far(1)
+    zx_start(1, (2,))
     z_forward(1, 1)
     w_rest(0)
     w_rest(1)
@@ -362,13 +466,15 @@
 
     def block(m, o):
         return jnp.concatenate(
-            [xg[p * 4 + o, m].reshape(tall, shard) for p in range(2)], axis=1
+            [xg[p * 4 + o, m, :2].reshape(tall, shard) for p in range(2)], axis=1
         )
 
     def pair_in(d, m):
         for q in range(2):
             for j in range(2):
                 p_in(d, j, m, q).wait_recv()
+        for j in range(2):
+            px_in(d, j, m).wait_recv()
 
     def gate_up(d):
         o = places[d]
@@ -400,6 +506,7 @@
         if j == 0:
             for c in range(2):
                 a_swap(c).start()
+    zx_take(1, (3, 0, 1, 2))
     w_forward(2)
     for j in range(2):
         passed(1, j, 1, 1)
@@ -657,7 +764,19 @@
         copy.start()
 
     for m in range(2):
-        for q in range(2):
+        for d in range(4):
+            zx_in(0, d, m).wait_send()
+            for j in range(2):
+                px_out(d, j, m).wait_send()
+
+            @pl.when(inner)
+            def _(d=d, m=m):
+                zx_on(d, m).wait_send()
+
+        for q in range(2):
+            for way in range(2):
+                v_out(way, m, q).wait_send()
+            v_on(m, q).wait_send()
             z_in(0, m, q).wait_send()
 
             @pl.when(inner)
@@ -751,8 +870,7 @@
                 pltpu.VMEM((deep, width), F32),
                 pltpu.VMEM((deep, width), F32),
                 pltpu.VMEM((width, deep), F32),
-                pltpu.VMEM((2, rows, shard), BF16),
-                pltpu.VMEM((8, 2, 2, rows, shard), BF16),
+                pltpu.VMEM((8, 2, 3, rows, shard), BF16),
                 pltpu.VMEM((4, 2, deep, width), BF16),
                 pltpu.VMEM((4, width, deep), BF16),
                 pltpu.VMEM((tall, wide), F32),
@@ -777,7 +895,7 @@
                 pltpu.VMEM((2, rows, shard), F32),
                 pltpu.VMEM((rows, shard), F32),
                 pltpu.VMEM((rows, shard), BF16),
-                DMA((7,)),
+                DMA((5,)),
                 DMA((4,)),
                 DMA((2, 2, 2)),
                 DMA((2, 2, 2)),
@@ -785,6 +903,12 @@
                 DMA((3, 2, 2, 2)),
                 DMA((4, 2, 2, 2)),
                 DMA((4, 2, 2, 2)),
+                DMA((3, 2, 2)),
+                DMA((3, 2, 2)),
+                DMA((2, 4, 2)),
+                DMA((2, 4, 2)),
+                DMA((4, 2, 2)),
+                DMA((4, 2, 2)),
                 DMA((3, 3, 2)),
                 DMA((3, 3, 2)),
                 DMA((2,)),

time: 98.5 us -> 108 us (1.096)
  the two profiles are of different devices: /device:TPU:32 before, /device:TPU:39 now
where the time goes in v5:
time: 108 us; the launch traced here: 107 us
  Pallas kernels  107 us (99%)
    pallas_call x1, Pallas kernels, body(): pl.pallas_call(functools.partial(kernel, factor), out_shape=shapes, in_sp...  105 us
    pallas_call x1, Pallas kernels, body(): pl.pallas_call(store_kernel, out_shape=shapes, in_specs=[HBM] * 4, out_sp...  2.33 us

profile of v5, /device:TPU:39, one launch (start us, length us, event | category | flops | bytes accessed | tf_op | source)
XLA Modules:
  0.0 107.5 jit_solution(620169778395343978)
XLA Ops:
  0.6 104.5 %block.1 = (bf16[256,512]{1,0:T(8,128)(2,1)}, f32[1024,128]{1,0:T(8,128)}, f32[1024,128]{1,0:T(8,128)}, f32[128,1024]{1,0:T(8,128)}) custom-call(bf16[256,512]{1,0:T(8,128)(2,1)} %tokens.1, bf16[256,512]{1,0:T(8,128)(2,1)} %grads.1, bf16[1024,128]{1,0:T(8,128)(2,1)} %gate_weight.1, bf16[1024,128]{1,0:T(8,128)(2,1)} %up_weight.1, bf16[128,1024]{1,0:T(8,128)(2,1)} %down_weight.1), custom_call_target="tpu_custom_call" | custom-call | tf_op jit(solution)/shard_map/block/pallas_call | solution.py:864
  105.2 2.3 %store.1 = (bf16[256,512]{1,0:T(8,128)(2,1)}, f32[1024,128]{1,0:T(8,128)}, f32[1024,128]{1,0:T(8,128)}, f32[128,1024]{1,0:T(8,128)}) custom-call(bf16[256,512]{1,0:T(8,128)(2,1)} %get-tuple-element.8.refs_0_, f32[1024,128]{1,0:T(8,128)} %get-tuple-element.9.refs_1_, f32[1024,128]{1,0:T(8,128)} %get-tuple-element.10.refs_2_, ...), custom_call_target="tpu_custom_call" | custom-call | tf_op jit(solution)/shard_map/store/pallas_call | solution.py:942

commit v6 on v4

--- a/solution.py
+++ b/solution.py
@@ -12,6 +12,7 @@
 F32 = jnp.float32
 BF16 = jnp.bfloat16
 VMEM_LIMIT = 60 * 1024 * 1024
+XFIRST = 32
 ROWS = ((0,), (0,))
 COLS = ((1,), (1,))
 
@@ -30,7 +31,6 @@
     gate_own,
     up_own,
     down_own,
-    held,
     xg,
     wf,
     df,
@@ -64,6 +64,12 @@
     x_recv,
     p_send,
     p_recv,
+    v_send,
+    v_recv,
+    zx_send,
+    zx_recv,
+    px_send,
+    px_recv,
     y_send,
     y_recv,
     a_send,
@@ -74,6 +80,8 @@
     t_recv,
     u_send,
     u_recv,
+    g_send,
+    g_recv,
     f_send,
     f_recv,
     dx_send,
@@ -95,6 +103,11 @@
     rows, shard = tokens.shape
     deep, width = gate_weight.shape
     part = rows // 2
+    zparts = ((rows - XFIRST) // 2, part)
+    first = rows - XFIRST
+    xpart = XFIRST // 2
+    odd = (h - l) * (h - l)
+    home = h * (1 - odd) + 2 * odd
     wide = 2 * width
 
     def at(xx, yy, hh, ll, kk):
@@ -124,25 +137,16 @@
         pltpu.make_async_copy(ref, spot, load.at[i])
         for i, (ref, spot) in enumerate(
             (
-                (tokens, held.at[0]),
+                (tokens, xg.at[k * 4 + x, 0, home]),
                 (gate_weight, wf.at[y, 0]),
                 (up_weight, wf.at[y, 1]),
-                (grads, held.at[1]),
+                (grads, xg.at[k * 4 + x, 1, home]),
                 (down_weight, df.at[y]),
             )
         )
-    ]
-    kept = [
-        pltpu.make_async_copy(ref, xg.at[k * 4 + x, m, h], load.at[5 + m])
-        for m, ref in enumerate((tokens, grads))
     ]
     for copy in copies:
         copy.start()
-
-    @pl.when(outer)
-    def _():
-        for copy in kept:
-            copy.start()
 
     barrier = pltpu.get_barrier_semaphore()
     for j in range(1, 16):
@@ -155,11 +159,6 @@
 
     for copy in copies:
         copy.wait()
-
-    @pl.when(outer)
-    def _():
-        for copy in kept:
-            copy.wait()
 
     def w_spot(o, w, q):
         if w == 2:
@@ -200,13 +199,13 @@
     slot = (h, 1 - h)
 
     def x_own(m, q):
-        return held.at[m, pl.ds(q * part, part)]
+        return xg.at[k * 4 + x, m, home, pl.ds(q * zparts[m], zparts[m])]
 
     def x_spot(p, o, j, m, q):
-        return xg.at[p * 4 + o, m, slot[j], pl.ds(q * part, part)]
+        return xg.at[p * 4 + o, m, slot[j], pl.ds(q * zparts[m], zparts[m])]
 
     def z_out(m, q, device, j):
-        spot = xg.at[k * 4 + x, m, h, pl.ds(q * part, part)]
+        spot = xg.at[k * 4 + x, m, h, pl.ds(q * zparts[m], zparts[m])]
         return remote(x_own(m, q), spot, z_send.at[0, m, q], z_recv.at[j, m, q], device)
 
     def z_on(m, q):
@@ -268,107 +267,248 @@
             z_in(1, m, q).wait_recv()
             z_on(m, q).start()
 
-    def z_spread(m, q, own_too):
+    def z_near(m, q):
+        @pl.when(inner)
+        def _():
+            z_in(0, m, q).wait_recv()
+
+        spread(x_spot(k, x, 0, m, q), 0, m, q)
+
+    def z_far(m, q):
+        @pl.when(outer)
+        def _():
+            z_in(1, m, q).wait_recv()
+
+        spread(x_spot(k, x, 1, m, q), 1, m, q)
+
+    def z_near_inner(m, q):
         @pl.when(inner)
         def _():
             z_in(0, m, q).wait_recv()
             spread(x_spot(k, x, 0, m, q), 0, m, q)
 
+    quarter = shard // 4
+
+    def t_rows(u):
+        return pl.ds(lax.rem(u, 2) * shard + y * quarter, quarter)
+
+    def t_out(j):
+        u = lax.rem(me + j, 8)
+        return remote(
+            wf.at[lax.div(u, 2), 0, t_rows(u)],
+            tw.at[me, 0, pl.ds(y * quarter, quarter)],
+            t_send.at[j],
+            t_recv.at[j],
+            (f, l * 8 + u),
+        )
+
+    def t_in(j):
+        u = lax.rem(me + 8 - j, 8)
+        spot = tw.at[u, 0, pl.ds(y * quarter, quarter)]
+        return remote(spot, spot, t_send.at[j], t_recv.at[j], (f, l * 8 + u))
+
+    def g_rows(u):
+        return pl.ds(lax.rem(u, 2) * shard, shard)
+
+    def g_out(j):
+        u = lax.rem(me + j, 8)
+        return remote(
+            wf.at[lax.div(u, 2), 1, g_rows(u)],
+            tw.at[me, 1],
+            g_send.at[j],
+            g_recv.at[j],
+            (f, l * 8 + u),
+        )
+
+    def g_in(j):
+        u = lax.rem(me + 8 - j, 8)
+        spot = tw.at[u, 1]
+        return remote(spot, spot, g_send.at[j], g_recv.at[j], (f, l * 8 + u))
+
+    def u_spot(o, q):
+        return tw.at[pl.ds(q * 4, 4), 0, pl.ds(o * quarter, quarter)]
+
+    def u_out(way, q):
+        here = u_spot(y, q)
+        return remote(here, here, u_send.at[way, q], u_recv.at[way, q], (north, south)[way])
+
+    def u_on(q):
+        here = u_spot(ys[q], q)
+        return remote(here, here, u_send.at[2, q], u_recv.at[2, q], (north, south)[q])
+
+    def u_in(d, q):
+        here = u_spot(ys[d], q)
+        return remote(here, here, u_send.at[2, q], u_recv.at[d, q], north)
+
+    def v_spot(o, q):
+        return xg.at[k * 4 + o, 0, home, pl.ds(first + q * xpart, xpart)]
+
+    def v_out(way, q):
+        here = v_spot(x, q)
+        return remote(
+            here, here, v_send.at[way, q], v_recv.at[way, q], (right, left)[way]
+        )
+
+    def v_on(q):
+        here = v_spot(xs[q], q)
+        return remote(here, here, v_send.at[2, q], v_recv.at[2, q], (right, left)[q])
+
+    def v_in(d, q):
+        here = v_spot(xs[d], q)
+        return remote(here, here, v_send.at[2, q], v_recv.at[d, q], right)
+
+    def zx_spot(p, d, at_s):
+        return xg.at[p * 4 + places[d], 0, at_s, pl.ds(first, XFIRST)]
+
+    def zx_out(d, device, j):
+        return remote(
+            zx_spot(k, d, home),
+            zx_spot(k, d, h),
+            zx_send.at[0, d],
+            zx_recv.at[j, d],
+            device,
+        )
+
+    def zx_on(d):
+        here = zx_spot(k, d, 1 - h)
+        return remote(here, here, zx_send.at[1, d], zx_recv.at[1, d], flip)
+
+    def zx_in(j, d):
+        here = zx_spot(k, d, slot[j])
+        return remote(here, here, zx_send.at[0, d], zx_recv.at[j, d], flip)
+
+    def px_out(d, j):
+        here = zx_spot(k, d, slot[j])
+        return remote(here, here, px_send.at[d, j], px_recv.at[d, j], mate)
+
+    def px_in(d, j):
+        here = zx_spot(1 - k, d, slot[j])
+        return remote(here, here, px_send.at[d, j], px_recv.at[d, j], mate)
+
+    def v_start():
+        for q in range(2):
+            for way in (0, 1) if q == 0 else (1, 0):
+                v_out(way, q).start()
+
+    def v_near():
+        for q in range(2):
+            v_in(q, q).wait_recv()
+            v_on(q).start()
+        for q in range(2):
+            v_in(1 - q, q).wait_recv()
+
+    def v_far():
+        for q in range(2):
+            v_in(2, q).wait_recv()
+
+    def zx_start(ds):
+        for d in ds:
+
+            @pl.when(outer)
+            def _(d=d):
+                zx_out(d, flip, 0).start()
+                px_out(d, 0).start()
+
+            @pl.when(inner)
+            def _(d=d):
+                zx_out(d, across, 1).start()
+
+    def zx_pass(ds):
+        for d in ds:
+
+            @pl.when(inner)
+            def _(d=d):
+                zx_in(1, d).wait_recv()
+                zx_on(d).start()
+
+    def zx_take(ds):
+        for d in ds:
+
+            @pl.when(inner)
+            def _(d=d):
+                zx_in(0, d).wait_recv()
+                px_out(d, 0).start()
+
+            @pl.when(outer)
+            def _(d=d):
+                zx_in(1, d).wait_recv()
+
+            px_out(d, 1).start()
+
+    def z_start(m):
         @pl.when(outer)
         def _():
-            if own_too:
-                spread(x_own(m, q), 0, m, q)
-            z_in(1, m, q).wait_recv()
-
-        spread(x_spot(k, x, 1, m, q), 1, m, q)
+            for q in range(2):
+                z_out(m, q, flip, 0).start()
+
+        @pl.when(inner)
+        def _():
+            for q in range(2):
+                z_out(m, q, across, 1).start()
+
+    v_start()
+    z_start(0)
 
     @pl.when(outer)
     def _():
-        for m in range(2):
-            for q in range(2):
-                z_out(m, q, flip, 0).start()
-            if m == 0:
-                for q in range(2):
-                    spread(x_own(0, q), 0, 0, q)
-
-    @pl.when(inner)
-    def _():
-        for m in range(2):
-            for q in range(2):
-                z_out(m, q, across, 1).start()
-
+        for q in range(2):
+            spread(x_own(0, q), 0, 0, q)
+
+    zx_start((3,))
     w_start(0)
     w_start(1)
 
-    for q in range(2):
-        z_forward(0, q)
-        z_spread(0, q, False)
+    v_near()
+    zx_start((0, 1))
+    z_forward(0, 0)
+    z_near_inner(0, 0)
+    z_far(0, 0)
+    v_far()
+    zx_start((2,))
+    z_start(1)
+    z_forward(0, 1)
+    z_near_inner(0, 1)
+    z_far(0, 1)
     w_forward(0)
     for j in range(2):
         passed(0, j, 0, 0)
         passed(1, j, 0, 0)
-    z_forward(1, 0)
     w_forward(1)
     w_start(2)
     for j in range(2):
         passed(1, j, 0, 1)
         passed(0, j, 0, 1)
+    z_forward(1, 0)
+    zx_pass((3, 0, 1))
     z_forward(1, 1)
+    zx_pass((2,))
+    z_near(1, 0)
+    z_near(1, 1)
     w_rest(0)
     w_rest(1)
-    quarter = shard // 4
-
-    def t_rows(u):
-        return pl.ds(lax.rem(u, 2) * shard + y * quarter, quarter)
-
-    def t_out(j):
-        u = lax.rem(me + j, 8)
-        return remote(
-            wf.at[lax.div(u, 2), :, t_rows(u)],
-            tw.at[me, :, pl.ds(y * quarter, quarter)],
-            t_send.at[j],
-            t_recv.at[j],
-            (f, l * 8 + u),
-        )
-
-    def t_in(j):
-        u = lax.rem(me + 8 - j, 8)
-        spot = tw.at[u, :, pl.ds(y * quarter, quarter)]
-        return remote(spot, spot, t_send.at[j], t_recv.at[j], (f, l * 8 + u))
-
-    def u_spot(o, q):
-        return tw.at[pl.ds(q * 4, 4), :, pl.ds(o * quarter, quarter)]
-
-    def u_out(way, q):
-        here = u_spot(y, q)
-        return remote(here, here, u_send.at[way, q], u_recv.at[way, q], (north, south)[way])
-
-    def u_on(q):
-        here = u_spot(ys[q], q)
-        return remote(here, here, u_send.at[2, q], u_recv.at[2, q], (north, south)[q])
-
-    def u_in(d, q):
-        here = u_spot(ys[d], q)
-        return remote(here, here, u_send.at[2, q], u_recv.at[d, q], north)
 
     @pl.loop(1, 8)
     def _(j):
         t_out(j).start()
 
-    tw[me, :, pl.ds(y * quarter, quarter)] = wf[x, :, t_rows(me)]
-    for q in range(2):
-        z_spread(1, q, True)
+    z_far(1, 0)
+    z_far(1, 1)
+    w_forward(2)
+    zx_take((3, 0, 1, 2))
     tall = 2 * rows
 
     def block(m, o):
         return jnp.concatenate(
-            [xg[p * 4 + o, m].reshape(tall, shard) for p in range(2)], axis=1
+            [xg[p * 4 + o, m, :2].reshape(tall, shard) for p in range(2)], axis=1
         )
 
     def pair_in(d, m):
         for q in range(2):
             for j in range(2):
                 p_in(d, j, m, q).wait_recv()
+        if m == 0:
+            for j in range(2):
+                px_in(d, j).wait_recv()
 
     def gate_up(d):
         o = places[d]
@@ -384,9 +524,11 @@
             passed(2, j, 0, q)
     pair_in(2, 0)
     gate_up(2)
+    turn = (1 - l, l)
+
     def swap(src, dst, send, recv):
         def copy(c):
-            at_c = pl.ds(c * rows, rows)
+            at_c = pl.ds(turn[c] * rows, rows)
             return remote(src.at[at_c], dst.at[at_c], send.at[c], recv.at[c], opposite)
 
         return copy
@@ -394,23 +536,44 @@
     a_swap = swap(sa, zla, a_send, a_recv)
     b_swap = swap(sb, zlb, b_send, b_recv)
 
+    a_swap(0).start()
+    tw[me, 0, pl.ds(y * quarter, quarter)] = wf[x, 0, t_rows(me)]
+    tw[me, 1] = wf[x, 1, g_rows(me)]
+    a_swap(1).start()
+    @pl.loop(1, 8)
+    def _(j):
+        t_in(j).wait_recv()
+
+    for way, q in ((0, 0), (1, 1), (0, 1), (1, 0)):
+        u_out(way, q).start()
     for j in range(2):
         passed(0, j, 1, 0)
         passed(1, j, 1, 0)
-        if j == 0:
-            for c in range(2):
-                a_swap(c).start()
-    w_forward(2)
     for j in range(2):
         passed(1, j, 1, 1)
         passed(0, j, 1, 1)
 
+    for q in range(2):
+        u_in(q, q).wait_recv()
+        u_on(q).start()
+    def grad_in(d):
+        o = places[d]
+        term = lax.dot_general(
+            block(1, o), df[o], (COLS, ((), ())), preferred_element_type=F32
+        )
+        sb[...] = term if d == 3 else sb[...] + term
+
     @pl.loop(1, 8)
     def _(j):
-        t_in(j).wait_recv()
-
-    for way, q in ((0, 0), (1, 1), (0, 1), (1, 0)):
-        u_out(way, q).start()
+        g_out(j).start()
+
+    w_rest(2)
+    for d in (3, 0, 1):
+        pair_in(d, 1)
+        grad_in(d)
+    for q in range(2):
+        for j in range(2):
+            passed(2, j, 1, q)
     for c in range(2):
         a_swap(c).wait_recv()
     sums = sa[...] + zla[...]
@@ -422,22 +585,15 @@
     acts[:, width:] = activated
     hidden[...] = (activated * up).astype(BF16)
 
-    def grad_in(d):
-        o = places[d]
-        term = lax.dot_general(
-            block(1, o), df[o], (COLS, ((), ())), preferred_element_type=F32
-        )
-        sb[...] = term if d == 3 else sb[...] + term
-
-    w_rest(2)
-    for d in (3, 0, 1):
-        pair_in(d, 1)
-        grad_in(d)
-    for q in range(2):
-        for j in range(2):
-            passed(2, j, 1, q)
     pair_in(2, 1)
-    grad_in(2)
+    for c in range(2):
+        at_s = pl.ds(turn[c] * rows, rows)
+        last = jnp.concatenate([xg[p * 4 + xs[2], 1, turn[c]] for p in range(2)], axis=1)
+        sb[at_s] += lax.dot_general(
+            last, df[xs[2]], (COLS, ((), ())), preferred_element_type=F32
+        )
+        if c:
+            b_swap(0).start()
     def down_part(o):
         return lax.dot_general(
             hidden[...], block(1, o), (ROWS, ((), ())), preferred_element_type=F32
@@ -500,27 +656,12 @@
         return lands[i][0].astype(F32) + lands[i][1].astype(F32)
 
     dtwo[...] = down_part(ys[2]).astype(BF16)
-    for c in range(2):
-        b_swap(c).start()
+    b_swap(1).start()
     one_parts(0, down_part)
     for q in range(2):
         two_out(0, q).start()
     for way in range(2):
         one_out(0, way, 1 - way).start()
-    for q in range(2):
-        u_in(q, q).wait_recv()
-        u_on(q).start()
-    down_own[...] = down_part(y)
-
-    for c in range(2):
-        b_swap(c).wait_recv()
-
-    hidden_grad = sb[...] + zlb[...]
-    dg[me, :, :width] = (hidden_grad * acts[:, :width]).astype(BF16)
-    dg[me, :, width:] = (hidden_grad * acts[:, width:]).astype(BF16)
-    gtwo[...] = gate_part(ys[2]).astype(BF16)
-
-    turn = (1 - l, l)
 
     def d_spot(c, o, e, q):
         return dg.at[o * 2 + c, pl.ds(turn[e] * rows + q * part, part)]
@@ -593,7 +734,18 @@
         at_c = pl.ds(c * piece, piece)
         return remote(rounded.at[at_c], result.at[at_c], r_send.at[c], r_recv.at[c], across)
 
+    def delta(e):
+        b_swap(e).wait_recv()
+        at_s = pl.ds(turn[e] * rows, rows)
+        hidden_grad = sb[at_s] + zlb[at_s]
+        dg[me, at_s, :width] = (hidden_grad * acts[at_s, :width]).astype(BF16)
+        dg[me, at_s, width:] = (hidden_grad * acts[at_s, width:]).astype(BF16)
+
+    delta(0)
+    down_own[...] = down_part(y)
     d_start(0)
+    delta(1)
+    gtwo[...] = gate_part(ys[2]).astype(BF16)
     one_parts(1, gate_part)
     for q in range(2):
         two_out(1, q).start()
@@ -608,12 +760,18 @@
         u_in(2, q).wait_recv()
     for way in range(2):
         one_out(0, way, way).start()
+    @pl.loop(1, 8)
+    def _(j):
+        g_in(j).wait_recv()
+
     gathers(0, (3, 0, 1))
     for q in range(2):
         d_passed(2, 0, q)
     gathers(0, (2,))
+    for c in range(2):
+        f_out(c).start()
     d_near(1)
-    for c in range(4):
+    for c in range(2, 4):
         f_out(c).start()
     one_merge(1)
     gathers(1, (3,))
@@ -656,6 +814,19 @@
     for copy in keeps[1:3]:
         copy.start()
 
+    for d in range(4):
+        zx_in(0, d).wait_send()
+        for j in range(2):
+            px_out(d, j).wait_send()
+
+        @pl.when(inner)
+        def _(d=d):
+            zx_on(d).wait_send()
+
+    for q in range(2):
+        for way in range(2):
+            v_out(way, q).wait_send()
+        v_on(q).wait_send()
     for m in range(2):
         for q in range(2):
             z_in(0, m, q).wait_send()
@@ -695,6 +866,7 @@
     @pl.loop(1, 8)
     def _(j):
         t_out(j).wait_send()
+        g_out(j).wait_send()
 
     @pl.when(inner)
     def _():
@@ -751,8 +923,7 @@
                 pltpu.VMEM((deep, width), F32),
                 pltpu.VMEM((deep, width), F32),
                 pltpu.VMEM((width, deep), F32),
-                pltpu.VMEM((2, rows, shard), BF16),
-                pltpu.VMEM((8, 2, 2, rows, shard), BF16),
+                pltpu.VMEM((8, 2, 3, rows, shard), BF16),
                 pltpu.VMEM((4, 2, deep, width), BF16),
                 pltpu.VMEM((4, width, deep), BF16),
                 pltpu.VMEM((tall, wide), F32),
@@ -777,7 +948,7 @@
                 pltpu.VMEM((2, rows, shard), F32),
                 pltpu.VMEM((rows, shard), F32),
                 pltpu.VMEM((rows, shard), BF16),
-                DMA((7,)),
+                DMA((5,)),
                 DMA((4,)),
                 DMA((2, 2, 2)),
                 DMA((2, 2, 2)),
@@ -785,6 +956,12 @@
                 DMA((3, 2, 2, 2)),
                 DMA((4, 2, 2, 2)),
                 DMA((4, 2, 2, 2)),
+                DMA((3, 2)),
+                DMA((3, 2)),
+                DMA((2, 4)),
+                DMA((2, 4)),
+                DMA((4, 2)),
+                DMA((4, 2)),
                 DMA((3, 3, 2)),
                 DMA((3, 3, 2)),
                 DMA((2,)),
@@ -795,6 +972,8 @@
                 DMA((8,)),
                 DMA((3, 2)),
                 DMA((3, 2)),
+                DMA((8,)),
+                DMA((8,)),
                 DMA((4,)),
                 DMA((4,)),
                 DMA((3, 2, 2)),

time: 98.5 us -> 95.8 us (0.973); the launches traced: 98.4 us -> 94.6 us
  Pallas kernels: 97.7 us -> 94 us
    pallas_call x1, Pallas kernels: 95.4 us -> 91.6 us  [body(): pl.pallas_call(functools.partial(kernel, factor), out_shape=shapes, in_sp...]
where the time goes in v6:
time: 95.8 us; the launch traced here: 94.6 us
  Pallas kernels  94 us (98%)
    pallas_call x1, Pallas kernels, body(): pl.pallas_call(functools.partial(kernel, factor), out_shape=shapes, in_sp...  91.6 us
    pallas_call x1, Pallas kernels, body(): pl.pallas_call(store_kernel, out_shape=shapes, in_specs=[HBM] * 4, out_sp...  2.33 us

profile of v6, /device:TPU:32, one launch (start us, length us, event | category | flops | bytes accessed | tf_op | source)
XLA Modules:
  0.0 94.6 jit_solution(16795578945570242570)
XLA Ops:
  0.6 91.6 %block.1 = (bf16[256,512]{1,0:T(8,128)(2,1)}, f32[1024,128]{1,0:T(8,128)}, f32[1024,128]{1,0:T(8,128)}, f32[128,1024]{1,0:T(8,128)}) custom-call(bf16[256,512]{1,0:T(8,128)(2,1)} %tokens.1, bf16[256,512]{1,0:T(8,128)(2,1)} %grads.1, bf16[1024,128]{1,0:T(8,128)(2,1)} %gate_weight.1, bf16[1024,128]{1,0:T(8,128)(2,1)} %up_weight.1, bf16[128,1024]{1,0:T(8,128)(2,1)} %down_weight.1), custom_call_target="tpu_custom_call" | custom-call | tf_op jit(solution)/shard_map/block/pallas_call | solution.py:917
  92.3 2.3 %store.1 = (bf16[256,512]{1,0:T(8,128)(2,1)}, f32[1024,128]{1,0:T(8,128)}, f32[1024,128]{1,0:T(8,128)}, f32[128,1024]{1,0:T(8,128)}) custom-call(bf16[256,512]{1,0:T(8,128)(2,1)} %get-tuple-element.8.refs_0_, f32[1024,128]{1,0:T(8,128)} %get-tuple-element.9.refs_1_, f32[1024,128]{1,0:T(8,128)} %get-tuple-element.10.refs_2_, ...), custom_call_target="tpu_custom_call" | custom-call | tf_op jit(solution)/shard_map/store/pallas_call | solution.py:997

commit v7 on v6

--- a/solution.py
+++ b/solution.py
@@ -13,6 +13,7 @@
 BF16 = jnp.bfloat16
 VMEM_LIMIT = 60 * 1024 * 1024
 XFIRST = 32
+DIRECT = 256
 ROWS = ((0,), (0,))
 COLS = ((1,), (1,))
 
@@ -287,34 +288,35 @@
             z_in(0, m, q).wait_recv()
             spread(x_spot(k, x, 0, m, q), 0, m, q)
 
-    quarter = shard // 4
-
-    def t_rows(u):
-        return pl.ds(lax.rem(u, 2) * shard + y * quarter, quarter)
-
-    def t_out(j):
-        u = lax.rem(me + j, 8)
-        return remote(
-            wf.at[lax.div(u, 2), 0, t_rows(u)],
-            tw.at[me, 0, pl.ds(y * quarter, quarter)],
-            t_send.at[j],
-            t_recv.at[j],
+    fourths = (shard // 4, (shard - DIRECT) // 4)
+    bases = (0, DIRECT)
+
+    def t_copy(u, w, j):
+        return remote(
+            wf.at[
+                lax.div(u, 2),
+                w,
+                pl.ds(lax.rem(u, 2) * shard + bases[w] + y * fourths[w], fourths[w]),
+            ],
+            tw.at[me, w, pl.ds(bases[w] + y * fourths[w], fourths[w])],
+            t_send.at[w, j],
+            t_recv.at[w, j],
             (f, l * 8 + u),
         )
 
-    def t_in(j):
+    def t_out(w, j):
+        return t_copy(lax.rem(me + j, 8), w, j)
+
+    def t_in(w, j):
         u = lax.rem(me + 8 - j, 8)
-        spot = tw.at[u, 0, pl.ds(y * quarter, quarter)]
-        return remote(spot, spot, t_send.at[j], t_recv.at[j], (f, l * 8 + u))
-
-    def g_rows(u):
-        return pl.ds(lax.rem(u, 2) * shard, shard)
+        spot = tw.at[u, w, pl.ds(bases[w] + y * fourths[w], fourths[w])]
+        return remote(spot, spot, t_send.at[w, j], t_recv.at[w, j], (f, l * 8 + u))
 
     def g_out(j):
         u = lax.rem(me + j, 8)
         return remote(
-            wf.at[lax.div(u, 2), 1, g_rows(u)],
-            tw.at[me, 1],
+            wf.at[lax.div(u, 2), 1, pl.ds(lax.rem(u, 2) * shard, DIRECT)],
+            tw.at[me, 1, pl.ds(0, DIRECT)],
             g_send.at[j],
             g_recv.at[j],
             (f, l * 8 + u),
@@ -322,23 +324,25 @@
 
     def g_in(j):
         u = lax.rem(me + 8 - j, 8)
-        spot = tw.at[u, 1]
+        spot = tw.at[u, 1, pl.ds(0, DIRECT)]
         return remote(spot, spot, g_send.at[j], g_recv.at[j], (f, l * 8 + u))
 
-    def u_spot(o, q):
-        return tw.at[pl.ds(q * 4, 4), 0, pl.ds(o * quarter, quarter)]
-
-    def u_out(way, q):
-        here = u_spot(y, q)
-        return remote(here, here, u_send.at[way, q], u_recv.at[way, q], (north, south)[way])
-
-    def u_on(q):
-        here = u_spot(ys[q], q)
-        return remote(here, here, u_send.at[2, q], u_recv.at[2, q], (north, south)[q])
-
-    def u_in(d, q):
-        here = u_spot(ys[d], q)
-        return remote(here, here, u_send.at[2, q], u_recv.at[d, q], north)
+    def u_spot(o, w, q):
+        return tw.at[pl.ds(q * 4, 4), w, pl.ds(bases[w] + o * fourths[w], fourths[w])]
+
+    def u_out(way, w, q):
+        here = u_spot(y, w, q)
+        return remote(
+            here, here, u_send.at[way, w, q], u_recv.at[way, w, q], (north, south)[way]
+        )
+
+    def u_on(w, q):
+        here = u_spot(ys[q], w, q)
+        return remote(here, here, u_send.at[2, w, q], u_recv.at[2, w, q], (north, south)[q])
+
+    def u_in(d, w, q):
+        here = u_spot(ys[d], w, q)
+        return remote(here, here, u_send.at[2, w, q], u_recv.at[d, w, q], north)
 
     def v_spot(o, q):
         return xg.at[k * 4 + o, 0, home, pl.ds(first + q * xpart, xpart)]
@@ -489,7 +493,8 @@
 
     @pl.loop(1, 8)
     def _(j):
-        t_out(j).start()
+        for w in range(2):
+            t_out(w, j).start()
 
     z_far(1, 0)
     z_far(1, 1)
@@ -537,15 +542,19 @@
     b_swap = swap(sb, zlb, b_send, b_recv)
 
     a_swap(0).start()
-    tw[me, 0, pl.ds(y * quarter, quarter)] = wf[x, 0, t_rows(me)]
-    tw[me, 1] = wf[x, 1, g_rows(me)]
+    for w in range(2):
+        mine_w = pl.ds(bases[w] + y * fourths[w], fourths[w])
+        tw[me, w, mine_w] = wf[x, w, pl.ds(k * shard + bases[w] + y * fourths[w], fourths[w])]
+    tw[me, 1, :DIRECT] = wf[x, 1, pl.ds(k * shard, DIRECT)]
     a_swap(1).start()
     @pl.loop(1, 8)
     def _(j):
-        t_in(j).wait_recv()
-
-    for way, q in ((0, 0), (1, 1), (0, 1), (1, 0)):
-        u_out(way, q).start()
+        for w in range(2):
+            t_in(w, j).wait_recv()
+
+    for w in range(2):
+        for way, q in ((0, 0), (1, 1), (0, 1), (1, 0)):
+            u_out(way, w, q).start()
     for j in range(2):
         passed(0, j, 1, 0)
         passed(1, j, 1, 0)
@@ -553,19 +562,12 @@
         passed(1, j, 1, 1)
         passed(0, j, 1, 1)
 
-    for q in range(2):
-        u_in(q, q).wait_recv()
-        u_on(q).start()
     def grad_in(d):
         o = places[d]
         term = lax.dot_general(
             block(1, o), df[o], (COLS, ((), ())), preferred_element_type=F32
         )
         sb[...] = term if d == 3 else sb[...] + term
-
-    @pl.loop(1, 8)
-    def _(j):
-        g_out(j).start()
 
     w_rest(2)
     for d in (3, 0, 1):
@@ -574,6 +576,14 @@
     for q in range(2):
         for j in range(2):
             passed(2, j, 1, q)
+    @pl.loop(1, 8)
+    def _(j):
+        g_out(j).start()
+
+    for w in range(2):
+        for q in range(2):
+            u_in(q, w, q).wait_recv()
+            u_on(w, q).start()
     for c in range(2):
         a_swap(c).wait_recv()
     sums = sa[...] + zla[...]
@@ -745,21 +755,22 @@
     down_own[...] = down_part(y)
     d_start(0)
     delta(1)
+    one_merge(0)
     gtwo[...] = gate_part(ys[2]).astype(BF16)
-    one_parts(1, gate_part)
+    for way in range(2):
+        one_out(0, way, way).start()
+    d_near(0)
+    d_start(1)
     for q in range(2):
         two_out(1, q).start()
+    one_parts(1, gate_part)
     for way in range(2):
         one_out(1, way, 1 - way).start()
     gown[...] = gate_part(y)
-    d_near(0)
-    d_start(1)
-    one_merge(0)
     for q in range(2):
-        u_in(1 - q, q).wait_recv()
-        u_in(2, q).wait_recv()
-    for way in range(2):
-        one_out(0, way, way).start()
+        for w in range(2):
+            u_in(1 - q, w, q).wait_recv()
+            u_in(2, w, q).wait_recv()
     @pl.loop(1, 8)
     def _(j):
         g_in(j).wait_recv()
@@ -781,14 +792,12 @@
     for q in range(2):
         d_passed(2, 1, q)
     gathers(1, (2,))
-    down_own[...] = factor * (down_own[...] + finals(0))
     keeps = [
         pltpu.make_async_copy(src, dst, keep.at[i])
         for i, (src, dst) in enumerate(
             ((down_own, down_out), (gate_own, gate_out), (up_own, up_out), (rounded, result))
         )
     ]
-    keeps[0].start()
     for c in range(4):
         f_out(c).wait_recv()
         at_c = pl.ds(c * piece, piece)
@@ -800,18 +809,19 @@
             def _(c=c):
                 r_out(c - 1).start()
 
+    down_own[...] = factor * (down_own[...] + finals(0))
+    @pl.when(inner)
+    def _():
+        r_out(3).start()
+
+    @pl.when(outer)
+    def _():
+        keeps[3].start()
+
     both = factor * (gown[...] + finals(1))
     gate_own[...] = both[:, :width]
     up_own[...] = both[:, width:]
-    @pl.when(inner)
-    def _():
-        r_out(3).start()
-
-    @pl.when(outer)
-    def _():
-        keeps[3].start()
-
-    for copy in keeps[1:3]:
+    for copy in keeps[:3]:
         copy.start()
 
     for d in range(4):
@@ -853,9 +863,10 @@
             two_out(i, c).wait_send()
             for q in range(2):
                 one_out(i, c, q).wait_send()
-        for way in range(2):
-            u_out(way, c).wait_send()
-        u_on(c).wait_send()
+        for w in range(2):
+            for way in range(2):
+                u_out(way, w, c).wait_send()
+            u_on(w, c).wait_send()
         for e in range(2):
             for way in range(2):
                 dx_out(way, e, c).wait_send()
@@ -865,7 +876,8 @@
 
     @pl.loop(1, 8)
     def _(j):
-        t_out(j).wait_send()
+        for w in range(2):
+            t_out(w, j).wait_send()
         g_out(j).wait_send()
 
     @pl.when(inner)
@@ -968,10 +980,10 @@
                 DMA((2,)),
                 DMA((2,)),
                 DMA((2,)),
-                DMA((8,)),
-                DMA((8,)),
-                DMA((3, 2)),
-                DMA((3, 2)),
+                DMA((2, 8)),
+                DMA((2, 8)),
+                DMA((3, 2, 2)),
+                DMA((3, 2, 2)),
                 DMA((8,)),
                 DMA((8,)),
                 DMA((4,)),

time: 95.8 us -> 90.4 us (0.944)
  Pallas kernels: 94 us -> 89.2 us
    pallas_call x1, Pallas kernels: 91.6 us -> 86.8 us  [body(): pl.pallas_call(functools.partial(kernel, factor), out_shape=shapes, in_sp...]
where the time goes in v7:
time: 90.4 us; the launch traced here: 89.8 us
  Pallas kernels  89.2 us (99%)
    pallas_call x1, Pallas kernels, body(): pl.pallas_call(functools.partial(kernel, factor), out_shape=shapes, in_sp...  86.8 us
    pallas_call x1, Pallas kernels, body(): pl.pallas_call(store_kernel, out_shape=shapes, in_specs=[HBM] * 4, out_sp...  2.33 us

profile of v7, /device:TPU:32, one launch (start us, length us, event | category | flops | bytes accessed | tf_op | source)
XLA Modules:
  0.0 89.8 jit_solution(5115446837752089569)
XLA Ops:
  0.6 86.8 %block.1 = (bf16[256,512]{1,0:T(8,128)(2,1)}, f32[1024,128]{1,0:T(8,128)}, f32[1024,128]{1,0:T(8,128)}, f32[128,1024]{1,0:T(8,128)}) custom-call(bf16[256,512]{1,0:T(8,128)(2,1)} %tokens.1, bf16[256,512]{1,0:T(8,128)(2,1)} %grads.1, bf16[1024,128]{1,0:T(8,128)(2,1)} %gate_weight.1, bf16[1024,128]{1,0:T(8,128)(2,1)} %up_weight.1, bf16[128,1024]{1,0:T(8,128)(2,1)} %down_weight.1), custom_call_target="tpu_custom_call" | custom-call | tf_op jit(solution)/shard_map/block/pallas_call | solution.py:929
  87.5 2.3 %store.1 = (bf16[256,512]{1,0:T(8,128)(2,1)}, f32[1024,128]{1,0:T(8,128)}, f32[1024,128]{1,0:T(8,128)}, f32[128,1024]{1,0:T(8,128)}) custom-call(bf16[256,512]{1,0:T(8,128)(2,1)} %get-tuple-element.8.refs_0_, f32[1024,128]{1,0:T(8,128)} %get-tuple-element.9.refs_1_, f32[1024,128]{1,0:T(8,128)} %get-tuple-element.10.refs_2_, ...), custom_call_target="tpu_custom_call" | custom-call | tf_op jit(solution)/shard_map/store/pallas_call | solution.py:1009

commit v8 on v7

--- a/solution.py
+++ b/solution.py
@@ -13,7 +13,7 @@
 BF16 = jnp.bfloat16
 VMEM_LIMIT = 60 * 1024 * 1024
 XFIRST = 32
-DIRECT = 256
+DIRECT = 384
 ROWS = ((0,), (0,))
 COLS = ((1,), (1,))
 
@@ -69,8 +69,6 @@
     v_recv,
     zx_send,
     zx_recv,
-    px_send,
-    px_recv,
     y_send,
     y_recv,
     a_send,
@@ -135,15 +133,13 @@
         )
 
     copies = [
-        pltpu.make_async_copy(ref, spot, load.at[i])
-        for i, (ref, spot) in enumerate(
-            (
-                (tokens, xg.at[k * 4 + x, 0, home]),
-                (gate_weight, wf.at[y, 0]),
-                (up_weight, wf.at[y, 1]),
-                (grads, xg.at[k * 4 + x, 1, home]),
-                (down_weight, df.at[y]),
-            )
+        pltpu.make_async_copy(ref, spot, load)
+        for ref, spot in (
+            (tokens, xg.at[k * 4 + x, 0, home]),
+            (gate_weight, wf.at[y, 0]),
+            (up_weight, wf.at[y, 1]),
+            (grads, xg.at[k * 4 + x, 1, home]),
+            (down_weight, df.at[y]),
         )
     ]
     for copy in copies:
@@ -158,8 +154,8 @@
         pl.semaphore_signal(barrier, inc=1, device_id=peer, device_id_type=MESH)
     pl.semaphore_wait(barrier, 19)
 
-    for copy in copies:
-        copy.wait()
+    all_in = xg.at[pl.ds(0, 5), 0, 0]
+    pltpu.make_async_copy(all_in, all_in, load).wait()
 
     def w_spot(o, w, q):
         if w == 2:
@@ -170,18 +166,17 @@
         return remote(
             w_spot(y, w, q),
             w_spot(y, w, q),
-            y_send.at[way, w, q],
-            y_recv.at[way, w, q],
+            y_send,
+            y_recv.at[w, q if way == q else 2],
             (north, south)[way],
         )
 
     def w_on(w, q):
         here = w_spot(ys[q], w, q)
-        return remote(here, here, y_send.at[2, w, q], y_recv.at[2, w, q], (north, south)[q])
-
-    def w_in(d, w, q):
-        here = w_spot(ys[d], w, q)
-        return remote(here, here, y_send.at[2, w, q], y_recv.at[d, w, q], north)
+        return remote(here, here, y_send, y_recv.at[w, 2], (north, south)[q])
+
+    def w_wait(w, e, here):
+        remote(here, here, y_send, y_recv.at[w, e], north).wait_recv()
 
     def w_start(w):
         for way, q in ((0, 0), (1, 1), (0, 1), (1, 0)):
@@ -189,13 +184,11 @@
 
     def w_forward(w):
         for q in range(2):
-            w_in(q, w, q).wait_recv()
+            w_wait(w, q, w_spot(ys[q], w, q))
             w_on(w, q).start()
 
     def w_rest(w):
-        for q in range(2):
-            w_in(1 - q, w, q).wait_recv()
-            w_in(2, w, q).wait_recv()
+        w_wait(w, 2, df.at[pl.ds(0, 2)] if w == 2 else wf.at[pl.ds(0, 2), w])
 
     slot = (h, 1 - h)
 
@@ -207,34 +200,33 @@
 
     def z_out(m, q, device, j):
         spot = xg.at[k * 4 + x, m, h, pl.ds(q * zparts[m], zparts[m])]
-        return remote(x_own(m, q), spot, z_send.at[0, m, q], z_recv.at[j, m, q], device)
+        return remote(x_own(m, q), spot, z_send.at[0], z_recv.at[j, m, q], device)
 
     def z_on(m, q):
         here = x_spot(k, x, 1, m, q)
-        return remote(here, here, z_send.at[1, m, q], z_recv.at[1, m, q], flip)
+        return remote(here, here, z_send.at[1], z_recv.at[1, m, q], flip)
 
     def z_in(j, m, q):
         here = x_spot(k, x, j, m, q)
-        return remote(here, here, z_send.at[0, m, q], z_recv.at[j, m, q], flip)
+        return remote(here, here, z_send.at[0], z_recv.at[j, m, q], flip)
 
     def x_out(way, src, j, m, q):
         return remote(
             src,
             x_spot(k, x, j, m, q),
-            x_send.at[way, j, m, q],
-            x_recv.at[way, j, m, q],
+            x_send,
+            x_recv.at[m, q, 2 * way + j],
             (right, left)[way],
         )
 
     def x_on(j, m, q):
         here = x_spot(k, xs[q], j, m, q)
         return remote(
-            here, here, x_send.at[2, j, m, q], x_recv.at[2, j, m, q], (right, left)[q]
-        )
-
-    def x_in(d, j, m, q):
-        here = x_spot(k, xs[d], j, m, q)
-        return remote(here, here, x_send.at[2, j, m, q], x_recv.at[d, j, m, q], right)
+            here, here, x_send, x_recv.at[m, q, 4], (right, left)[q]
+        )
+
+    def x_wait(m, q, e, here):
+        remote(here, here, x_send, x_recv.at[m, q, e], right).wait_recv()
 
     places = (*xs, x)
 
@@ -242,14 +234,10 @@
         return remote(
             src,
             x_spot(k, places[d], j, m, q),
-            p_send.at[d, j, m, q],
-            p_recv.at[d, j, m, q],
+            p_send,
+            p_recv.at[d, m],
             mate,
         )
-
-    def p_in(d, j, m, q):
-        here = x_spot(1 - k, places[d], j, m, q)
-        return remote(here, here, p_send.at[d, j, m, q], p_recv.at[d, j, m, q], mate)
 
     def spread(src, j, m, q):
         for way in (0, 1) if q == 0 else (1, 0):
@@ -257,10 +245,17 @@
         p_out(3, src, j, m, q).start()
 
     def passed(d, j, m, q):
-        x_in(d, j, m, q).wait_recv()
+        x_wait(m, q, 2 * d + j, x_spot(k, xs[d], j, m, q))
         if d == q:
             x_on(j, m, q).start()
         p_out(d, x_spot(k, places[d], j, m, q), j, m, q).start()
+
+    def x_rest(m):
+        for q in range(2):
+            here = xg.at[k * 4 + xs[2], m, pl.ds(0, 2), pl.ds(q * zparts[m], zparts[m])]
+            x_wait(m, q, 4, here)
+            for j in range(2):
+                p_out(2, x_spot(k, xs[2], j, m, q), j, m, q).start()
 
     def z_forward(m, q):
         @pl.when(inner)
@@ -291,7 +286,7 @@
     fourths = (shard // 4, (shard - DIRECT) // 4)
     bases = (0, DIRECT)
 
-    def t_copy(u, w, j):
+    def t_copy(u, w):
         return remote(
             wf.at[
                 lax.div(u, 2),
@@ -299,33 +294,31 @@
                 pl.ds(lax.rem(u, 2) * shard + bases[w] + y * fourths[w], fourths[w]),
             ],
             tw.at[me, w, pl.ds(bases[w] + y * fourths[w], fourths[w])],
-            t_send.at[w, j],
-            t_recv.at[w, j],
+            t_send,
+            t_recv,
             (f, l * 8 + u),
         )
 
     def t_out(w, j):
-        return t_copy(lax.rem(me + j, 8), w, j)
-
-    def t_in(w, j):
-        u = lax.rem(me + 8 - j, 8)
-        spot = tw.at[u, w, pl.ds(bases[w] + y * fourths[w], fourths[w])]
-        return remote(spot, spot, t_send.at[w, j], t_recv.at[w, j], (f, l * 8 + u))
+        return t_copy(lax.rem(me + j, 8), w)
+
+    def t_all():
+        here = tw.at[pl.ds(0, 7), 0, pl.ds(0, fourths[0] + fourths[1])]
+        return remote(here, here, t_send, t_recv, mate)
 
     def g_out(j):
         u = lax.rem(me + j, 8)
         return remote(
             wf.at[lax.div(u, 2), 1, pl.ds(lax.rem(u, 2) * shard, DIRECT)],
             tw.at[me, 1, pl.ds(0, DIRECT)],
-            g_send.at[j],
-            g_recv.at[j],
+            g_send,
+            g_recv,
             (f, l * 8 + u),
         )
 
-    def g_in(j):
-        u = lax.rem(me + 8 - j, 8)
-        spot = tw.at[u, 1, pl.ds(0, DIRECT)]
-        return remote(spot, spot, g_send.at[j], g_recv.at[j], (f, l * 8 + u))
+    def g_all():
+        here = tw.at[pl.ds(0, 7), 1, pl.ds(0, DIRECT)]
+        return remote(here, here, g_send, g_recv, mate)
 
     def u_spot(o, w, q):
         return tw.at[pl.ds(q * 4, 4), w, pl.ds(bases[w] + o * fourths[w], fourths[w])]
@@ -333,16 +326,15 @@
     def u_out(way, w, q):
         here = u_spot(y, w, q)
         return remote(
-            here, here, u_send.at[way, w, q], u_recv.at[way, w, q], (north, south)[way]
+            here, here, u_send, u_recv.at[q if way == q else 2], (north, south)[way]
         )
 
     def u_on(w, q):
         here = u_spot(ys[q], w, q)
-        return remote(here, here, u_send.at[2, w, q], u_recv.at[2, w, q], (north, south)[q])
-
-    def u_in(d, w, q):
-        here = u_spot(ys[d], w, q)
-        return remote(here, here, u_send.at[2, w, q], u_recv.at[d, w, q], north)
+        return remote(here, here, u_send, u_recv.at[2], (north, south)[q])
+
+    def u_wait(e, here):
+        remote(here, here, u_send, u_recv.at[e], north).wait_recv()
 
     def v_spot(o, q):
         return xg.at[k * 4 + o, 0, home, pl.ds(first + q * xpart, xpart)]
@@ -350,16 +342,15 @@
     def v_out(way, q):
         here = v_spot(x, q)
         return remote(
-            here, here, v_send.at[way, q], v_recv.at[way, q], (right, left)[way]
+            here, here, v_send, v_recv.at[q if way == q else 2], (right, left)[way]
         )
 
     def v_on(q):
         here = v_spot(xs[q], q)
-        return remote(here, here, v_send.at[2, q], v_recv.at[2, q], (right, left)[q])
-
-    def v_in(d, q):
-        here = v_spot(xs[d], q)
-        return remote(here, here, v_send.at[2, q], v_recv.at[d, q], right)
+        return remote(here, here, v_send, v_recv.at[3], (right, left)[q])
+
+    def v_wait(e, here):
+        remote(here, here, v_send, v_recv.at[e], right).wait_recv()
 
     def zx_spot(p, d, at_s):
         return xg.at[p * 4 + places[d], 0, at_s, pl.ds(first, XFIRST)]
@@ -368,26 +359,22 @@
         return remote(
             zx_spot(k, d, home),
             zx_spot(k, d, h),
-            zx_send.at[0, d],
-            zx_recv.at[j, d],
+            zx_send.at[0],
+            zx_recv.at[j + (j * d == 2)],
             device,
         )
 
     def zx_on(d):
         here = zx_spot(k, d, 1 - h)
-        return remote(here, here, zx_send.at[1, d], zx_recv.at[1, d], flip)
-
-    def zx_in(j, d):
-        here = zx_spot(k, d, slot[j])
-        return remote(here, here, zx_send.at[0, d], zx_recv.at[j, d], flip)
+        return remote(here, here, zx_send.at[1], zx_recv.at[1 + (d == 2)], flip)
+
+    def zx_wait(e, count):
+        here = xg.at[pl.ds(0, count), 0, 0, pl.ds(first, XFIRST)]
+        remote(here, here, zx_send.at[0], zx_recv.at[e], flip).wait_recv()
 
     def px_out(d, j):
         here = zx_spot(k, d, slot[j])
-        return remote(here, here, px_send.at[d, j], px_recv.at[d, j], mate)
-
-    def px_in(d, j):
-        here = zx_spot(1 - k, d, slot[j])
-        return remote(here, here, px_send.at[d, j], px_recv.at[d, j], mate)
+        return remote(here, here, p_send, p_recv.at[d, 0], mate)
 
     def v_start():
         for q in range(2):
@@ -396,14 +383,12 @@
 
     def v_near():
         for q in range(2):
-            v_in(q, q).wait_recv()
+            v_wait(q, v_spot(xs[q], q))
             v_on(q).start()
-        for q in range(2):
-            v_in(1 - q, q).wait_recv()
+        v_wait(2, zx_spot(k, 0, home))
 
     def v_far():
-        for q in range(2):
-            v_in(2, q).wait_recv()
+        v_wait(3, zx_spot(k, 2, home))
 
     def zx_start(ds):
         for d in ds:
@@ -417,26 +402,26 @@
             def _(d=d):
                 zx_out(d, across, 1).start()
 
-    def zx_pass(ds):
-        for d in ds:
-
-            @pl.when(inner)
-            def _(d=d):
-                zx_in(1, d).wait_recv()
+    def zx_pass(e, ds):
+        @pl.when(inner)
+        def _():
+            zx_wait(e, len(ds))
+            for d in ds:
                 zx_on(d).start()
 
-    def zx_take(ds):
-        for d in ds:
-
-            @pl.when(inner)
-            def _(d=d):
-                zx_in(0, d).wait_recv()
+    def zx_take():
+        @pl.when(inner)
+        def _():
+            zx_wait(0, 4)
+            for d in range(4):
                 px_out(d, 0).start()
 
-            @pl.when(outer)
-            def _(d=d):
-                zx_in(1, d).wait_recv()
-
+        @pl.when(outer)
+        def _():
+            zx_wait(1, 3)
+            zx_wait(2, 1)
+
+        for d in range(4):
             px_out(d, 1).start()
 
     def z_start(m):
@@ -483,9 +468,9 @@
         passed(1, j, 0, 1)
         passed(0, j, 0, 1)
     z_forward(1, 0)
-    zx_pass((3, 0, 1))
+    zx_pass(1, (3, 0, 1))
     z_forward(1, 1)
-    zx_pass((2,))
+    zx_pass(2, (2,))
     z_near(1, 0)
     z_near(1, 1)
     w_rest(0)
@@ -499,7 +484,7 @@
     z_far(1, 0)
     z_far(1, 1)
     w_forward(2)
-    zx_take((3, 0, 1, 2))
+    zx_take()
     tall = 2 * rows
 
     def block(m, o):
@@ -508,12 +493,8 @@
         )
 
     def pair_in(d, m):
-        for q in range(2):
-            for j in range(2):
-                p_in(d, j, m, q).wait_recv()
-        if m == 0:
-            for j in range(2):
-                px_in(d, j).wait_recv()
+        here = xg.at[(1 - k) * 4 + places[d], m, pl.ds(0, 2)]
+        remote(here, here, p_send, p_recv.at[d, m], mate).wait_recv()
 
     def gate_up(d):
         o = places[d]
@@ -524,22 +505,22 @@
     for d in (3, 0, 1):
         pair_in(d, 0)
         gate_up(d)
-    for q in range(2):
-        for j in range(2):
-            passed(2, j, 0, q)
+    x_rest(0)
     pair_in(2, 0)
     gate_up(2)
     turn = (1 - l, l)
 
-    def swap(src, dst, send, recv):
+    def swap(src, dst, send, recvs):
         def copy(c):
             at_c = pl.ds(turn[c] * rows, rows)
-            return remote(src.at[at_c], dst.at[at_c], send.at[c], recv.at[c], opposite)
+            return remote(src.at[at_c], dst.at[at_c], send, recvs[c], opposite)
 
         return copy
 
-    a_swap = swap(sa, zla, a_send, a_recv)
-    b_swap = swap(sb, zlb, b_send, b_recv)
+    a_swap = swap(sa, zla, a_send, (a_recv, a_recv))
+    b_swap = swap(sb, zlb, b_send, (b_recv.at[0], b_recv.at[1]))
+    a_all = remote(sa, zla, a_send, a_recv, opposite)
+    b_all = remote(sb, zlb, b_send, b_recv.at[0], opposite)
 
     a_swap(0).start()
     for w in range(2):
@@ -547,10 +528,7 @@
         tw[me, w, mine_w] = wf[x, w, pl.ds(k * shard + bases[w] + y * fourths[w], fourths[w])]
     tw[me, 1, :DIRECT] = wf[x, 1, pl.ds(k * shard, DIRECT)]
     a_swap(1).start()
-    @pl.loop(1, 8)
-    def _(j):
-        for w in range(2):
-            t_in(w, j).wait_recv()
+    t_all().wait_recv()
 
     for w in range(2):
         for way, q in ((0, 0), (1, 1), (0, 1), (1, 0)):
@@ -573,19 +551,16 @@
     for d in (3, 0, 1):
         pair_in(d, 1)
         grad_in(d)
-    for q in range(2):
-        for j in range(2):
-            passed(2, j, 1, q)
+    x_rest(1)
     @pl.loop(1, 8)
     def _(j):
         g_out(j).start()
 
-    for w in range(2):
-        for q in range(2):
-            u_in(q, w, q).wait_recv()
+    for q in range(2):
+        u_wait(q, tw.at[pl.ds(q * 4, 4), 0, pl.ds(0, fourths[0] + fourths[1])])
+        for w in range(2):
             u_on(w, q).start()
-    for c in range(2):
-        a_swap(c).wait_recv()
+    a_all.wait_recv()
     sums = sa[...] + zla[...]
     gate, up = sums[:, :width], sums[:, width:]
     squashed = jax.nn.sigmoid(gate)
@@ -630,7 +605,7 @@
         return remote(
             twos[i].at[halves(i, q)],
             mids[i].at[q],
-            two_send.at[i, q],
+            two_send.at[i],
             two_recv.at[i, q],
             (north, south)[q],
         )
@@ -639,8 +614,8 @@
         return remote(
             ones[i].at[way, halves(i, q)],
             lands[i].at[way, halves(i, q)],
-            one_send.at[i, way, q],
-            one_recv.at[i, way, q],
+            one_send.at[i],
+            one_recv.at[i],
             (north, south)[way],
         )
 
@@ -660,9 +635,7 @@
             ).astype(BF16)
 
     def finals(i):
-        for way in range(2):
-            for q in range(2):
-                one_out(i, way, q).wait_recv()
+        remote(ones[i], lands[i], one_send.at[i], one_recv.at[i], north).wait_recv()
         return lands[i][0].astype(F32) + lands[i][1].astype(F32)
 
     dtwo[...] = down_part(ys[2]).astype(BF16)
@@ -679,24 +652,29 @@
     def dx_out(way, e, q):
         here = d_spot(k, x, e, q)
         return remote(
-            here, here, dx_send.at[way, e, q], dx_recv.at[way, e, q], (right, left)[way]
+            here, here, dx_send, dx_recv.at[way, e, q], (right, left)[way]
         )
 
     def dx_on(e, q):
         here = d_spot(k, xs[q], e, q)
-        return remote(here, here, dx_send.at[2, e, q], dx_recv.at[2, e, q], (right, left)[q])
+        return remote(here, here, dx_send, dx_recv.at[2, e, 0], (right, left)[q])
 
     def dx_in(d, e, q):
         here = d_spot(k, xs[d], e, q)
-        return remote(here, here, dx_send.at[2, e, q], dx_recv.at[d, e, q], right)
+        return remote(here, here, dx_send, dx_recv.at[d, e, q], right)
 
     def dp_out(d, e, q):
         here = d_spot(k, places[d], e, q)
-        return remote(here, here, dp_send.at[d, e, q], dp_recv.at[d, e, q], mate)
-
-    def dp_in(d, e, q):
-        here = d_spot(1 - k, places[d], e, q)
-        return remote(here, here, dp_send.at[d, e, q], dp_recv.at[d, e, q], mate)
+        return remote(here, here, dp_send, dp_recv.at[d, e], mate)
+
+    def d_half(c, d, e):
+        return dg.at[places[d] * 2 + c, pl.ds(turn[e] * rows, rows)]
+
+    def d_far(e):
+        here = d_half(k, 2, e)
+        remote(here, here, dx_send, dx_recv.at[2, e, 0], right).wait_recv()
+        for q in range(2):
+            dp_out(2, e, q).start()
 
     def d_start(e):
         for q in range(2):
@@ -730,19 +708,19 @@
 
     def gathers(e, ds):
         for d in ds:
-            for q in range(2):
-                dp_in(d, e, q).wait_recv()
+            here = d_half(1 - k, d, e)
+            remote(here, here, dp_send, dp_recv.at[d, e], mate).wait_recv()
             gather(d, e)
 
     piece = rows // 4
 
     def f_out(c):
         at_c = pl.ds(c * piece, piece)
-        return remote(total.at[0, at_c], near.at[at_c], f_send.at[c], f_recv.at[c], flip)
+        return remote(total.at[0, at_c], near.at[at_c], f_send, f_recv.at[c], flip)
 
     def r_out(c):
         at_c = pl.ds(c * piece, piece)
-        return remote(rounded.at[at_c], result.at[at_c], r_send.at[c], r_recv.at[c], across)
+        return remote(rounded.at[at_c], result.at[at_c], r_send, r_recv, across)
 
     def delta(e):
         b_swap(e).wait_recv()
@@ -767,17 +745,11 @@
     for way in range(2):
         one_out(1, way, 1 - way).start()
     gown[...] = gate_part(y)
-    for q in range(2):
-        for w in range(2):
-            u_in(1 - q, w, q).wait_recv()
-            u_in(2, w, q).wait_recv()
-    @pl.loop(1, 8)
-    def _(j):
-        g_in(j).wait_recv()
+    u_wait(2, tw.at[:, :, pl.ds(0, fourths[0] + fourths[1])])
+    g_all().wait_recv()
 
     gathers(0, (3, 0, 1))
-    for q in range(2):
-        d_passed(2, 0, q)
+    d_far(0)
     gathers(0, (2,))
     for c in range(2):
         f_out(c).start()
@@ -789,8 +761,7 @@
     for way in range(2):
         one_out(1, way, way).start()
     gathers(1, (0, 1))
-    for q in range(2):
-        d_passed(2, 1, q)
+    d_far(1)
     gathers(1, (2,))
     keeps = [
         pltpu.make_async_copy(src, dst, keep.at[i])
@@ -824,66 +795,35 @@
     for copy in keeps[:3]:
         copy.start()
 
-    for d in range(4):
-        zx_in(0, d).wait_send()
-        for j in range(2):
-            px_out(d, j).wait_send()
-
-        @pl.when(inner)
-        def _(d=d):
-            zx_on(d).wait_send()
-
-    for q in range(2):
-        for way in range(2):
-            v_out(way, q).wait_send()
-        v_on(q).wait_send()
-    for m in range(2):
-        for q in range(2):
-            z_in(0, m, q).wait_send()
-
-            @pl.when(inner)
-            def _(m=m, q=q):
-                z_on(m, q).wait_send()
-
-            for j in range(2):
-                for way in range(2):
-                    x_out(way, x_own(m, q), j, m, q).wait_send()
-                x_on(j, m, q).wait_send()
-                for d in range(4):
-                    p_out(d, x_own(m, q), j, m, q).wait_send()
-    for w in range(3):
-        for q in range(2):
-            for way in range(2):
-                w_out(way, w, q).wait_send()
-            w_on(w, q).wait_send()
-    for c in range(2):
-        for copy in (a_swap(c), b_swap(c), f_out(c), f_out(2 + c)):
-            copy.wait_send()
-        for i in range(2):
-            two_out(i, c).wait_send()
-            for q in range(2):
-                one_out(i, c, q).wait_send()
-        for w in range(2):
-            for way in range(2):
-                u_out(way, w, c).wait_send()
-            u_on(w, c).wait_send()
-        for e in range(2):
-            for way in range(2):
-                dx_out(way, e, c).wait_send()
-            dx_on(e, c).wait_send()
-            for d in range(4):
-                dp_out(d, e, c).wait_send()
-
-    @pl.loop(1, 8)
-    def _(j):
-        for w in range(2):
-            t_out(w, j).wait_send()
-        g_out(j).wait_send()
+    sent = [
+        (xg.at[0, :, 0, pl.ds(0, 240)], z_send.at[0]),
+        (xg.at[pl.ds(0, 4), 0, 0, pl.ds(0, XFIRST)], zx_send.at[0]),
+        (xg.at[pl.ds(0, 3), 0, 0, pl.ds(0, XFIRST)], v_send),
+        (xg.at[pl.ds(0, 4), 0, :, pl.ds(0, 240)], x_send),
+        (xg.at[:, :, 0], p_send),
+        (xg.at[pl.ds(0, 3), 0], y_send),
+        (tw.at[:, :, pl.ds(0, 3 * (fourths[0] + fourths[1]) // 2)], u_send),
+        (dg.at[pl.ds(0, 3)], dx_send),
+        (dg.at[pl.ds(0, 4)], dp_send),
+        (total.at[0], f_send),
+        (dtwo, two_send.at[0]),
+        (gtwo, two_send.at[1]),
+        (done, one_send.at[0]),
+        (gone, one_send.at[1]),
+    ]
+    for here, sem in sent:
+        remote(here, here, sem, load, mate).wait_send()
+    for copy in (a_all, b_all, t_all(), g_all()):
+        copy.wait_send()
 
     @pl.when(inner)
     def _():
-        for c in range(4):
-            r_out(c).wait()
+        for here, sem in (
+            (xg.at[0, :, 0, pl.ds(0, 240)], z_send.at[1]),
+            (xg.at[pl.ds(0, 4), 0, 0, pl.ds(0, XFIRST)], zx_send.at[1]),
+        ):
+            remote(here, here, sem, load, mate).wait_send()
+        remote(rounded, result, r_send, r_recv, across).wait()
 
     @pl.when(outer)
     def _():
@@ -960,44 +900,42 @@
                 pltpu.VMEM((2, rows, shard), F32),
                 pltpu.VMEM((rows, shard), F32),
                 pltpu.VMEM((rows, shard), BF16),
-                DMA((5,)),
+                DMA(()),
                 DMA((4,)),
+                DMA((2,)),
                 DMA((2, 2, 2)),
-                DMA((2, 2, 2)),
-                DMA((3, 2, 2, 2)),
-                DMA((3, 2, 2, 2)),
-                DMA((4, 2, 2, 2)),
-                DMA((4, 2, 2, 2)),
-                DMA((3, 2)),
-                DMA((3, 2)),
-                DMA((2, 4)),
-                DMA((2, 4)),
+                DMA(()),
+                DMA((2, 2, 5)),
+                DMA(()),
                 DMA((4, 2)),
+                DMA(()),
+                DMA((4,)),
+                DMA((2,)),
+                DMA((3,)),
+                DMA(()),
+                DMA((3, 3)),
+                DMA(()),
+                DMA(()),
+                DMA(()),
+                DMA((2,)),
+                DMA(()),
+                DMA(()),
+                DMA(()),
+                DMA((3,)),
+                DMA(()),
+                DMA(()),
+                DMA(()),
+                DMA((4,)),
+                DMA(()),
+                DMA((3, 2, 2)),
+                DMA(()),
                 DMA((4, 2)),
-                DMA((3, 3, 2)),
-                DMA((3, 3, 2)),
+                DMA((2,)),
+                DMA((2, 2)),
                 DMA((2,)),
                 DMA((2,)),
-                DMA((2,)),
-                DMA((2,)),
-                DMA((2, 8)),
-                DMA((2, 8)),
-                DMA((3, 2, 2)),
-                DMA((3, 2, 2)),
-                DMA((8,)),
-                DMA((8,)),
-                DMA((4,)),
-                DMA((4,)),
-                DMA((3, 2, 2)),
-                DMA((3, 2, 2)),
-                DMA((4, 2, 2)),
-                DMA((4, 2, 2)),
-                DMA((2, 2)),
-                DMA((2, 2)),
-                DMA((2, 2, 2)),
-                DMA((2, 2, 2)),
-                DMA((4,)),
-                DMA((4,)),
+                DMA(()),
+                DMA(()),
             ],
             compiler_params=pltpu.CompilerParams(
                 collective_id=0, has_side_effects=True, vmem_limit_bytes=VMEM_LIMIT

time: 90.4 us -> 87 us (0.962)
  Pallas kernels: 89.2 us -> 85.2 us
    pallas_call x1, Pallas kernels: 86.8 us -> 82.9 us  [body(): pl.pallas_call(functools.partial(kernel, factor), out_shape=shapes, in_sp...]
where the time goes in v8:
time: 87 us; the launch traced here: 85.8 us
  Pallas kernels  85.2 us (98%)
    pallas_call x1, Pallas kernels, body(): pl.pallas_call(functools.partial(kernel, factor), out_shape=shapes, in_sp...  82.9 us
    pallas_call x1, Pallas kernels, body(): pl.pallas_call(store_kernel, out_shape=shapes, in_specs=[HBM] * 4, out_sp...  2.33 us

profile of v8, /device:TPU:32, one launch (start us, length us, event | category | flops | bytes accessed | tf_op | source)
XLA Modules:
  0.0 85.8 jit_solution(6590053836160254446)
XLA Ops:
  0.6 82.9 %block.1 = (bf16[256,512]{1,0:T(8,128)(2,1)}, f32[1024,128]{1,0:T(8,128)}, f32[1024,128]{1,0:T(8,128)}, f32[128,1024]{1,0:T(8,128)}) custom-call(bf16[256,512]{1,0:T(8,128)(2,1)} %tokens.1, bf16[256,512]{1,0:T(8,128)(2,1)} %grads.1, bf16[1024,128]{1,0:T(8,128)(2,1)} %gate_weight.1, bf16[1024,128]{1,0:T(8,128)(2,1)} %up_weight.1, bf16[128,1024]{1,0:T(8,128)(2,1)} %down_weight.1), custom_call_target="tpu_custom_call" | custom-call | tf_op jit(solution)/shard_map/block/pallas_call | solution.py:869
  83.5 2.3 %store.1 = (bf16[256,512]{1,0:T(8,128)(2,1)}, f32[1024,128]{1,0:T(8,128)}, f32[1024,128]{1,0:T(8,128)}, f32[128,1024]{1,0:T(8,128)}) custom-call(bf16[256,512]{1,0:T(8,128)(2,1)} %get-tuple-element.8.refs_0_, f32[1024,128]{1,0:T(8,128)} %get-tuple-element.9.refs_1_, f32[1024,128]{1,0:T(8,128)} %get-tuple-element.10.refs_2_, ...), custom_call_target="tpu_custom_call" | custom-call | tf_op jit(solution)/shard_map/store/pallas_call | solution.py:947

commit v9 on v8

--- a/solution.py
+++ b/solution.py
@@ -13,6 +13,7 @@
 BF16 = jnp.bfloat16
 VMEM_LIMIT = 60 * 1024 * 1024
 XFIRST = 32
+PIECES = 8
 DIRECT = 384
 ROWS = ((0,), (0,))
 COLS = ((1,), (1,))
@@ -584,6 +585,15 @@
             hidden[...], block(1, o), (ROWS, ((), ())), preferred_element_type=F32
         )
 
+    def down_mine(q):
+        at_q = pl.ds(q * (width // 2), width // 2)
+        down_own[at_q] = lax.dot_general(
+            hidden[:, q * (width // 2) : (q + 1) * (width // 2)],
+            block(1, y),
+            (ROWS, ((), ())),
+            preferred_element_type=F32,
+        )
+
     def gate_part(o):
         return lax.dot_general(
             block(0, o), dg[me], (ROWS, ((), ())), preferred_element_type=F32
@@ -619,13 +629,12 @@
             (north, south)[way],
         )
 
-    def one_parts(i, fn):
-        for way in range(2):
-            q = way
-            term = fn(ys[1 - way])
-            size = term.shape[0] // 2
-            parts[i][way] = term[q * size : (q + 1) * size]
-            ones[i][way, halves(i, 1 - q)] = term[(1 - q) * size : (2 - q) * size].astype(BF16)
+    def one_part(i, fn, way):
+        q = way
+        term = fn(ys[1 - way])
+        size = term.shape[0] // 2
+        parts[i][way] = term[q * size : (q + 1) * size]
+        ones[i][way, halves(i, 1 - q)] = term[(1 - q) * size : (2 - q) * size].astype(BF16)
 
     def one_merge(i):
         for way in range(2):
@@ -640,9 +649,10 @@
 
     dtwo[...] = down_part(ys[2]).astype(BF16)
     b_swap(1).start()
-    one_parts(0, down_part)
+    one_part(0, down_part, 0)
     for q in range(2):
         two_out(0, q).start()
+    one_part(0, down_part, 1)
     for way in range(2):
         one_out(0, way, 1 - way).start()
 
@@ -712,7 +722,7 @@
             remote(here, here, dp_send, dp_recv.at[d, e], mate).wait_recv()
             gather(d, e)
 
-    piece = rows // 4
+    piece = rows // PIECES
 
     def f_out(c):
         at_c = pl.ds(c * piece, piece)
@@ -730,20 +740,22 @@
         dg[me, at_s, width:] = (hidden_grad * acts[at_s, width:]).astype(BF16)
 
     delta(0)
-    down_own[...] = down_part(y)
+    down_mine(0)
     d_start(0)
-    delta(1)
     one_merge(0)
-    gtwo[...] = gate_part(ys[2]).astype(BF16)
+    down_mine(1)
     for way in range(2):
         one_out(0, way, way).start()
-    d_near(0)
-    d_start(1)
+    delta(1)
+    gtwo[...] = gate_part(ys[2]).astype(BF16)
+    one_part(1, gate_part, 0)
     for q in range(2):
         two_out(1, q).start()
-    one_parts(1, gate_part)
-    for way in range(2):
-        one_out(1, way, 1 - way).start()
+    one_part(1, gate_part, 1)
+    one_out(1, 0, 1).start()
+    d_near(0)
+    one_out(1, 1, 0).start()
+    d_start(1)
     gown[...] = gate_part(y)
     u_wait(2, tw.at[:, :, pl.ds(0, fourths[0] + fourths[1])])
     g_all().wait_recv()
@@ -751,10 +763,10 @@
     gathers(0, (3, 0, 1))
     d_far(0)
     gathers(0, (2,))
-    for c in range(2):
+    for c in range(PIECES // 2):
         f_out(c).start()
     d_near(1)
-    for c in range(2, 4):
+    for c in range(PIECES // 2, PIECES):
         f_out(c).start()
     one_merge(1)
     gathers(1, (3,))
@@ -769,7 +781,7 @@
             ((down_own, down_out), (gate_own, gate_out), (up_own, up_out), (rounded, result))
         )
     ]
-    for c in range(4):
+    for c in range(PIECES):
         f_out(c).wait_recv()
         at_c = pl.ds(c * piece, piece)
         rounded[at_c] = (total[1, at_c] + near[at_c]).astype(BF16)
@@ -783,7 +795,7 @@
     down_own[...] = factor * (down_own[...] + finals(0))
     @pl.when(inner)
     def _():
-        r_out(3).start()
+        r_out(PIECES - 1).start()
 
     @pl.when(outer)
     def _():
@@ -925,7 +937,7 @@
                 DMA(()),
                 DMA(()),
                 DMA(()),
-                DMA((4,)),
+                DMA((PIECES,)),
                 DMA(()),
                 DMA((3, 2, 2)),
                 DMA(()),

time: 87 us -> 85.7 us (0.985)
  no operation moved by 1% of the time
where the time goes in v9:
time: 85.7 us; the launch traced here: 85.3 us
  Pallas kernels  84.6 us (99%)
    pallas_call x1, Pallas kernels, body(): pl.pallas_call(functools.partial(kernel, factor), out_shape=shapes, in_sp...  82.3 us
    pallas_call x1, Pallas kernels, body(): pl.pallas_call(store_kernel, out_shape=shapes, in_specs=[HBM] * 4, out_sp...  2.33 us

profile of v9, /device:TPU:32, one launch (start us, length us, event | category | flops | bytes accessed | tf_op | source)
XLA Modules:
  0.0 85.3 jit_solution(15872598617392054232)
XLA Ops:
  0.6 82.3 %block.1 = (bf16[256,512]{1,0:T(8,128)(2,1)}, f32[1024,128]{1,0:T(8,128)}, f32[1024,128]{1,0:T(8,128)}, f32[128,1024]{1,0:T(8,128)}) custom-call(bf16[256,512]{1,0:T(8,128)(2,1)} %tokens.1, bf16[256,512]{1,0:T(8,128)(2,1)} %grads.1, bf16[1024,128]{1,0:T(8,128)(2,1)} %gate_weight.1, bf16[1024,128]{1,0:T(8,128)(2,1)} %up_weight.1, bf16[128,1024]{1,0:T(8,128)(2,1)} %down_weight.1), custom_call_target="tpu_custom_call" | custom-call | tf_op jit(solution)/shard_map/block/pallas_call | solution.py:881
  82.9 2.3 %store.1 = (bf16[256,512]{1,0:T(8,128)(2,1)}, f32[1024,128]{1,0:T(8,128)}, f32[1024,128]{1,0:T(8,128)}, f32[128,1024]{1,0:T(8,128)}) custom-call(bf16[256,512]{1,0:T(8,128)(2,1)} %get-tuple-element.8.refs_0_, f32[1024,128]{1,0:T(8,128)} %get-tuple-element.9.refs_1_, f32[1024,128]{1,0:T(8,128)} %get-tuple-element.10.refs_2_, ...), custom_call_target="tpu_custom_call" | custom-call | tf_op jit(solution)/shard_map/store/pallas_call | solution.py:959

commit v10 on v9

--- a/solution.py
+++ b/solution.py
@@ -57,6 +57,8 @@
     gown,
     total,
     near,
+    slim,
+    slim_near,
     rounded,
     load,
     keep,
@@ -572,14 +574,6 @@
     hidden[...] = (activated * up).astype(BF16)
 
     pair_in(2, 1)
-    for c in range(2):
-        at_s = pl.ds(turn[c] * rows, rows)
-        last = jnp.concatenate([xg[p * 4 + xs[2], 1, turn[c]] for p in range(2)], axis=1)
-        sb[at_s] += lax.dot_general(
-            last, df[xs[2]], (COLS, ((), ())), preferred_element_type=F32
-        )
-        if c:
-            b_swap(0).start()
     def down_part(o):
         return lax.dot_general(
             hidden[...], block(1, o), (ROWS, ((), ())), preferred_element_type=F32
@@ -647,15 +641,25 @@
         remote(ones[i], lands[i], one_send.at[i], one_recv.at[i], north).wait_recv()
         return lands[i][0].astype(F32) + lands[i][1].astype(F32)
 
+    def grad_last(c):
+        at_s = pl.ds(turn[c] * rows, rows)
+        last = jnp.concatenate([xg[p * 4 + xs[2], 1, turn[c]] for p in range(2)], axis=1)
+        sb[at_s] += lax.dot_general(
+            last, df[xs[2]], (COLS, ((), ())), preferred_element_type=F32
+        )
+
     dtwo[...] = down_part(ys[2]).astype(BF16)
-    b_swap(1).start()
-    one_part(0, down_part, 0)
+    grad_last(0)
     for q in range(2):
         two_out(0, q).start()
+    grad_last(1)
+    b_swap(0).start()
+    one_part(0, down_part, 0)
+    b_swap(1).start()
     one_part(0, down_part, 1)
     for way in range(2):
         one_out(0, way, 1 - way).start()
-
+    one_merge(0)
     def d_spot(c, o, e, q):
         return dg.at[o * 2 + c, pl.ds(turn[e] * rows + q * part, part)]
 
@@ -726,7 +730,19 @@
 
     def f_out(c):
         at_c = pl.ds(c * piece, piece)
-        return remote(total.at[0, at_c], near.at[at_c], f_send, f_recv.at[c], flip)
+        return (
+            remote(total.at[0, at_c, pl.ds(0, wide)], near.at[at_c], f_send, f_recv.at[c], flip),
+            remote(slim.at[at_c], slim_near.at[at_c], f_send, f_recv.at[c], flip),
+        )
+
+    def f_start(cs):
+        for c in cs:
+            for copy in f_out(c):
+                copy.start()
+
+    def f_wait(c):
+        here = near.at[pl.ds(0, 3 * piece // 2)]
+        remote(here, here, f_send, f_recv.at[c], flip).wait_recv()
 
     def r_out(c):
         at_c = pl.ds(c * piece, piece)
@@ -740,12 +756,11 @@
         dg[me, at_s, width:] = (hidden_grad * acts[at_s, width:]).astype(BF16)
 
     delta(0)
+    for way in range(2):
+        one_out(0, way, way).start()
     down_mine(0)
     d_start(0)
-    one_merge(0)
     down_mine(1)
-    for way in range(2):
-        one_out(0, way, way).start()
     delta(1)
     gtwo[...] = gate_part(ys[2]).astype(BF16)
     one_part(1, gate_part, 0)
@@ -763,11 +778,10 @@
     gathers(0, (3, 0, 1))
     d_far(0)
     gathers(0, (2,))
-    for c in range(PIECES // 2):
-        f_out(c).start()
+    slim[...] = total[0, :, wide:].astype(BF16)
+    f_start(range(PIECES // 2))
     d_near(1)
-    for c in range(PIECES // 2, PIECES):
-        f_out(c).start()
+    f_start(range(PIECES // 2, PIECES))
     one_merge(1)
     gathers(1, (3,))
     for way in range(2):
@@ -782,9 +796,10 @@
         )
     ]
     for c in range(PIECES):
-        f_out(c).wait_recv()
+        f_wait(c)
         at_c = pl.ds(c * piece, piece)
-        rounded[at_c] = (total[1, at_c] + near[at_c]).astype(BF16)
+        rounded[at_c, :wide] = (total[1, at_c, :wide] + near[at_c]).astype(BF16)
+        rounded[at_c, wide:] = (total[1, at_c, wide:] + slim_near[at_c].astype(F32)).astype(BF16)
 
         if c:
 
@@ -817,7 +832,7 @@
         (tw.at[:, :, pl.ds(0, 3 * (fourths[0] + fourths[1]) // 2)], u_send),
         (dg.at[pl.ds(0, 3)], dx_send),
         (dg.at[pl.ds(0, 4)], dp_send),
-        (total.at[0], f_send),
+        (total.at[0, pl.ds(0, 3 * rows // 4)], f_send),
         (dtwo, two_send.at[0]),
         (gtwo, two_send.at[1]),
         (done, one_send.at[0]),
@@ -910,7 +925,9 @@
                 pltpu.VMEM((2, deep, wide), BF16),
                 pltpu.VMEM((deep, wide), F32),
                 pltpu.VMEM((2, rows, shard), F32),
-                pltpu.VMEM((rows, shard), F32),
+                pltpu.VMEM((rows, wide), F32),
+                pltpu.VMEM((rows, wide), BF16),
+                pltpu.VMEM((rows, wide), BF16),
                 pltpu.VMEM((rows, shard), BF16),
                 DMA(()),
                 DMA((4,)),

time: 85.7 us -> 84.6 us (0.987); the launches traced: 85.3 us -> 83.2 us
  Pallas kernels: 84.6 us -> 82.5 us
    pallas_call x1, Pallas kernels: 82.3 us -> 80.2 us  [body(): pl.pallas_call(functools.partial(kernel, factor), out_shape=shapes, in_sp...]
where the time goes in v10:
time: 84.6 us; the launch traced here: 83.2 us
  Pallas kernels  82.5 us (98%)
    pallas_call x1, Pallas kernels, body(): pl.pallas_call(functools.partial(kernel, factor), out_shape=shapes, in_sp...  80.2 us
    pallas_call x1, Pallas kernels, body(): pl.pallas_call(store_kernel, out_shape=shapes, in_specs=[HBM] * 4, out_sp...  2.33 us

profile of v10, /device:TPU:32, one launch (start us, length us, event | category | flops | bytes accessed | tf_op | source)
XLA Modules:
  0.0 83.2 jit_solution(9082909513685796321)
XLA Ops:
  0.6 80.2 %block.1 = (bf16[256,512]{1,0:T(8,128)(2,1)}, f32[1024,128]{1,0:T(8,128)}, f32[1024,128]{1,0:T(8,128)}, f32[128,1024]{1,0:T(8,128)}) custom-call(bf16[256,512]{1,0:T(8,128)(2,1)} %tokens.1, bf16[256,512]{1,0:T(8,128)(2,1)} %grads.1, bf16[1024,128]{1,0:T(8,128)(2,1)} %gate_weight.1, bf16[1024,128]{1,0:T(8,128)(2,1)} %up_weight.1, bf16[128,1024]{1,0:T(8,128)(2,1)} %down_weight.1), custom_call_target="tpu_custom_call" | custom-call | tf_op jit(solution)/shard_map/block/pallas_call | solution.py:896
  80.8 2.3 %store.1 = (bf16[256,512]{1,0:T(8,128)(2,1)}, f32[1024,128]{1,0:T(8,128)}, f32[1024,128]{1,0:T(8,128)}, f32[128,1024]{1,0:T(8,128)}) custom-call(bf16[256,512]{1,0:T(8,128)(2,1)} %get-tuple-element.8.refs_0_, f32[1024,128]{1,0:T(8,128)} %get-tuple-element.9.refs_1_, f32[1024,128]{1,0:T(8,128)} %get-tuple-element.10.refs_2_, ...), custom_call_target="tpu_custom_call" | custom-call | tf_op jit(solution)/shard_map/store/pallas_call | solution.py:976

commit v11 on v10

--- a/solution.py
+++ b/solution.py
@@ -474,8 +474,6 @@
     zx_pass(1, (3, 0, 1))
     z_forward(1, 1)
     zx_pass(2, (2,))
-    z_near(1, 0)
-    z_near(1, 1)
     w_rest(0)
     w_rest(1)
 
@@ -484,6 +482,8 @@
         for w in range(2):
             t_out(w, j).start()
 
+    z_near(1, 0)
+    z_near(1, 1)
     z_far(1, 0)
     z_far(1, 1)
     w_forward(2)
@@ -554,15 +554,83 @@
     for d in (3, 0, 1):
         pair_in(d, 1)
         grad_in(d)
+    def down_half(o, p):
+        return lax.dot_general(
+            hidden[...],
+            xg[p * 4 + o, 1, :2].reshape(tall, shard),
+            (ROWS, ((), ())),
+            preferred_element_type=F32,
+        )
+
+    def gate_part(o):
+        return lax.dot_general(
+            block(0, o), dg[me], (ROWS, ((), ())), preferred_element_type=F32
+        )
+
+    twos, mids, parts, ones, lands = (
+        (dtwo, gtwo),
+        (dmid, gmid),
+        (dpart, gpart),
+        (done, gone),
+        (dland, gland),
+    )
+
+    def halves(i, q):
+        return q if i == 0 else pl.ds(q * shard, shard)
+
+    def beside(way):
+        return lax.rem(y + 1 + 2 * way, 4)
+
+    def two_out(i, q):
+        return remote(
+            twos[i].at[halves(i, q)],
+            mids[i].at[q],
+            two_send.at[i],
+            two_recv.at[i, q],
+            at(x, beside(q), h, l, k),
+        )
+
+    def one_out(i, way, q):
+        return remote(
+            ones[i].at[way, halves(i, q)],
+            lands[i].at[way, halves(i, q)],
+            one_send.at[i],
+            one_recv.at[i],
+            at(x, beside(way), h, l, k),
+        )
+
+    def one_part(way):
+        term = gate_part(beside(way))
+        gpart[way] = term[way * shard : (way + 1) * shard]
+        gone[way, halves(1, 1 - way)] = term[(1 - way) * shard : (2 - way) * shard].astype(BF16)
+
+    def one_merge(i):
+        for way in range(2):
+            two_out(i, way).wait_recv()
+            ones[i][way, halves(i, way)] = (
+                parts[i][way] + mids[i][way].astype(F32)
+            ).astype(BF16)
+
+    def finals(i):
+        remote(ones[i], lands[i], one_send.at[i], one_recv.at[i], north).wait_recv()
+        return lands[i][0].astype(F32) + lands[i][1].astype(F32)
+
+    def grad_last(c):
+        at_s = pl.ds(turn[c] * rows, rows)
+        last = jnp.concatenate([xg[p * 4 + xs[2], 1, turn[c]] for p in range(2)], axis=1)
+        sb[at_s] += lax.dot_general(
+            last, df[xs[2]], (COLS, ((), ())), preferred_element_type=F32
+        )
+
+    for q in range(2):
+        u_wait(q, tw.at[pl.ds(q * 4, 4), 0, pl.ds(0, fourths[0] + fourths[1])])
+        for w in range(2):
+            u_on(w, q).start()
     x_rest(1)
     @pl.loop(1, 8)
     def _(j):
         g_out(j).start()
 
-    for q in range(2):
-        u_wait(q, tw.at[pl.ds(q * 4, 4), 0, pl.ds(0, fourths[0] + fourths[1])])
-        for w in range(2):
-            u_on(w, q).start()
     a_all.wait_recv()
     sums = sa[...] + zla[...]
     gate, up = sums[:, :width], sums[:, width:]
@@ -573,92 +641,21 @@
     acts[:, width:] = activated
     hidden[...] = (activated * up).astype(BF16)
 
+    dtwo[k] = down_half(ys[2], k).astype(BF16)
+    done[1 - k, k] = down_half(beside(1 - k), k).astype(BF16)
+    two_out(0, k).start()
     pair_in(2, 1)
-    def down_part(o):
-        return lax.dot_general(
-            hidden[...], block(1, o), (ROWS, ((), ())), preferred_element_type=F32
-        )
-
-    def down_mine(q):
-        at_q = pl.ds(q * (width // 2), width // 2)
-        down_own[at_q] = lax.dot_general(
-            hidden[:, q * (width // 2) : (q + 1) * (width // 2)],
-            block(1, y),
-            (ROWS, ((), ())),
-            preferred_element_type=F32,
-        )
-
-    def gate_part(o):
-        return lax.dot_general(
-            block(0, o), dg[me], (ROWS, ((), ())), preferred_element_type=F32
-        )
-
-    twos, mids, parts, ones, lands = (
-        (dtwo, gtwo),
-        (dmid, gmid),
-        (dpart, gpart),
-        (done, gone),
-        (dland, gland),
-    )
-
-    def halves(i, q):
-        size = twos[i].shape[0] // 2
-        return pl.ds(q * size, size)
-
-    def two_out(i, q):
-        return remote(
-            twos[i].at[halves(i, q)],
-            mids[i].at[q],
-            two_send.at[i],
-            two_recv.at[i, q],
-            (north, south)[q],
-        )
-
-    def one_out(i, way, q):
-        return remote(
-            ones[i].at[way, halves(i, q)],
-            lands[i].at[way, halves(i, q)],
-            one_send.at[i],
-            one_recv.at[i],
-            (north, south)[way],
-        )
-
-    def one_part(i, fn, way):
-        q = way
-        term = fn(ys[1 - way])
-        size = term.shape[0] // 2
-        parts[i][way] = term[q * size : (q + 1) * size]
-        ones[i][way, halves(i, 1 - q)] = term[(1 - q) * size : (2 - q) * size].astype(BF16)
-
-    def one_merge(i):
-        for way in range(2):
-            two_out(i, way).wait_recv()
-            ones[i][way, halves(i, way)] = (
-                parts[i][way] + mids[i][way].astype(F32)
-            ).astype(BF16)
-
-    def finals(i):
-        remote(ones[i], lands[i], one_send.at[i], one_recv.at[i], north).wait_recv()
-        return lands[i][0].astype(F32) + lands[i][1].astype(F32)
-
-    def grad_last(c):
-        at_s = pl.ds(turn[c] * rows, rows)
-        last = jnp.concatenate([xg[p * 4 + xs[2], 1, turn[c]] for p in range(2)], axis=1)
-        sb[at_s] += lax.dot_general(
-            last, df[xs[2]], (COLS, ((), ())), preferred_element_type=F32
-        )
-
-    dtwo[...] = down_part(ys[2]).astype(BF16)
     grad_last(0)
-    for q in range(2):
-        two_out(0, q).start()
     grad_last(1)
     b_swap(0).start()
-    one_part(0, down_part, 0)
+    dtwo[1 - k] = down_half(ys[2], 1 - k).astype(BF16)
     b_swap(1).start()
-    one_part(0, down_part, 1)
-    for way in range(2):
-        one_out(0, way, 1 - way).start()
+    done[k, 1 - k] = down_half(beside(k), 1 - k).astype(BF16)
+    two_out(0, 1 - k).start()
+    one_out(0, 1 - k, k).start()
+    dpart[k] = down_half(beside(k), k)
+    one_out(0, k, 1 - k).start()
+    dpart[1 - k] = down_half(beside(1 - k), 1 - k)
     one_merge(0)
     def d_spot(c, o, e, q):
         return dg.at[o * 2 + c, pl.ds(turn[e] * rows + q * part, part)]
@@ -758,15 +755,15 @@
     delta(0)
     for way in range(2):
         one_out(0, way, way).start()
-    down_mine(0)
+    down_own[:, :shard] = down_half(y, 0)
     d_start(0)
-    down_mine(1)
+    down_own[:, shard:] = down_half(y, 1)
     delta(1)
     gtwo[...] = gate_part(ys[2]).astype(BF16)
-    one_part(1, gate_part, 0)
+    one_part(0)
     for q in range(2):
         two_out(1, q).start()
-    one_part(1, gate_part, 1)
+    one_part(1)
     one_out(1, 0, 1).start()
     d_near(0)
     one_out(1, 1, 0).start()
@@ -807,7 +804,10 @@
             def _(c=c):
                 r_out(c - 1).start()
 
-    down_own[...] = factor * (down_own[...] + finals(0))
+    both = finals(0)
+    for p in range(2):
+        at_p = slice(p * shard, (p + 1) * shard)
+        down_own[:, at_p] = factor * (down_own[:, at_p] + both[p])
     @pl.when(inner)
     def _():
         r_out(PIECES - 1).start()
@@ -913,15 +913,15 @@
                 pltpu.VMEM((tall, width), BF16),
                 pltpu.VMEM((8, tall, wide), BF16),
                 pltpu.VMEM((8, 2, shard, width), BF16),
-                pltpu.VMEM((2, width // 2, deep), F32),
+                pltpu.VMEM((2, width, shard), F32),
                 pltpu.VMEM((2, deep // 2, wide), F32),
-                pltpu.VMEM((width, deep), BF16),
+                pltpu.VMEM((2, width, shard), BF16),
                 pltpu.VMEM((deep, wide), BF16),
-                pltpu.VMEM((2, width, deep), BF16),
+                pltpu.VMEM((2, 2, width, shard), BF16),
                 pltpu.VMEM((2, deep, wide), BF16),
-                pltpu.VMEM((2, width // 2, deep), BF16),
+                pltpu.VMEM((2, width, shard), BF16),
                 pltpu.VMEM((2, deep // 2, wide), BF16),
-                pltpu.VMEM((2, width, deep), BF16),
+                pltpu.VMEM((2, 2, width, shard), BF16),
                 pltpu.VMEM((2, deep, wide), BF16),
                 pltpu.VMEM((deep, wide), F32),
                 pltpu.VMEM((2, rows, shard), F32),

time: 84.6 us -> 84.5 us (level)
  no operation moved by 1% of the time
where the time goes in v11:
time: 84.5 us; the launch traced here: 83.4 us
  Pallas kernels  82.8 us (98%)
    pallas_call x1, Pallas kernels, body(): pl.pallas_call(functools.partial(kernel, factor), out_shape=shapes, in_sp...  80.5 us
    pallas_call x1, Pallas kernels, body(): pl.pallas_call(store_kernel, out_shape=shapes, in_specs=[HBM] * 4, out_sp...  2.33 us

profile of v11, /device:TPU:32, one launch (start us, length us, event | category | flops | bytes accessed | tf_op | source)
XLA Modules:
  0.0 83.4 jit_solution(1372858845958399948)
XLA Ops:
  0.6 80.5 %block.1 = (bf16[256,512]{1,0:T(8,128)(2,1)}, f32[1024,128]{1,0:T(8,128)}, f32[1024,128]{1,0:T(8,128)}, f32[128,1024]{1,0:T(8,128)}) custom-call(bf16[256,512]{1,0:T(8,128)(2,1)} %tokens.1, bf16[256,512]{1,0:T(8,128)(2,1)} %grads.1, bf16[1024,128]{1,0:T(8,128)(2,1)} %gate_weight.1, bf16[1024,128]{1,0:T(8,128)(2,1)} %up_weight.1, bf16[128,1024]{1,0:T(8,128)(2,1)} %down_weight.1), custom_call_target="tpu_custom_call" | custom-call | tf_op jit(solution)/shard_map/block/pallas_call | solution.py:896
  81.1 2.3 %store.1 = (bf16[256,512]{1,0:T(8,128)(2,1)}, f32[1024,128]{1,0:T(8,128)}, f32[1024,128]{1,0:T(8,128)}, f32[128,1024]{1,0:T(8,128)}) custom-call(bf16[256,512]{1,0:T(8,128)(2,1)} %get-tuple-element.8.refs_0_, f32[1024,128]{1,0:T(8,128)} %get-tuple-element.9.refs_1_, f32[1024,128]{1,0:T(8,128)} %get-tuple-element.10.refs_2_, ...), custom_call_target="tpu_custom_call" | custom-call | tf_op jit(solution)/shard_map/store/pallas_call | solution.py:976

commit v12 on v11

--- a/solution.py
+++ b/solution.py
@@ -599,10 +599,21 @@
             at(x, beside(way), h, l, k),
         )
 
-    def one_part(way):
-        term = gate_part(beside(way))
-        gpart[way] = term[way * shard : (way + 1) * shard]
-        gone[way, halves(1, 1 - way)] = term[(1 - way) * shard : (2 - way) * shard].astype(BF16)
+    def gate_half(o, p):
+        return lax.dot_general(
+            xg[p * 4 + o, 0, :2].reshape(tall, shard),
+            dg[me],
+            (ROWS, ((), ())),
+            preferred_element_type=F32,
+        )
+
+    def gate_rows(o, p, e):
+        return lax.dot_general(
+            xg[p * 4 + o, 0, turn[e]],
+            dg[me, pl.ds(turn[e] * rows, rows)],
+            (ROWS, ((), ())),
+            preferred_element_type=F32,
+        )
 
     def one_merge(i):
         for way in range(2):
@@ -758,15 +769,19 @@
     down_own[:, :shard] = down_half(y, 0)
     d_start(0)
     down_own[:, shard:] = down_half(y, 1)
+    gown[...] = jnp.concatenate([gate_rows(ys[2], p, 0) for p in range(2)], axis=0)
     delta(1)
-    gtwo[...] = gate_part(ys[2]).astype(BF16)
-    one_part(0)
-    for q in range(2):
-        two_out(1, q).start()
-    one_part(1)
+    for p in range(2):
+        gtwo[halves(1, p)] = (gown[halves(1, p)] + gate_rows(ys[2], p, 1)).astype(BF16)
+    two_out(1, 0).start()
+    gone[0, halves(1, 1)] = gate_half(beside(0), 1).astype(BF16)
+    two_out(1, 1).start()
+    gone[1, halves(1, 0)] = gate_half(beside(1), 0).astype(BF16)
     one_out(1, 0, 1).start()
+    gpart[0] = gate_half(beside(0), 0)
+    one_out(1, 1, 0).start()
+    gpart[1] = gate_half(beside(1), 1)
     d_near(0)
-    one_out(1, 1, 0).start()
     d_start(1)
     gown[...] = gate_part(y)
     u_wait(2, tw.at[:, :, pl.ds(0, fourths[0] + fourths[1])])

time: 84.5 us -> 84.1 us (level)
  no operation moved by 1% of the time
where the time goes in v12:
time: 84.1 us; the launch traced here: 83.7 us
  Pallas kernels  83 us (99%)
    pallas_call x1, Pallas kernels, body(): pl.pallas_call(functools.partial(kernel, factor), out_shape=shapes, in_sp...  80.7 us
    pallas_call x1, Pallas kernels, body(): pl.pallas_call(store_kernel, out_shape=shapes, in_specs=[HBM] * 4, out_sp...  2.33 us

profile of v12, /device:TPU:32, one launch (start us, length us, event | category | flops | bytes accessed | tf_op | source)
XLA Modules:
  0.0 83.7 jit_solution(13610679635922922371)
XLA Ops:
  0.6 80.7 %block.1 = (bf16[256,512]{1,0:T(8,128)(2,1)}, f32[1024,128]{1,0:T(8,128)}, f32[1024,128]{1,0:T(8,128)}, f32[128,1024]{1,0:T(8,128)}) custom-call(bf16[256,512]{1,0:T(8,128)(2,1)} %tokens.1, bf16[256,512]{1,0:T(8,128)(2,1)} %grads.1, bf16[1024,128]{1,0:T(8,128)(2,1)} %gate_weight.1, bf16[1024,128]{1,0:T(8,128)(2,1)} %up_weight.1, bf16[128,1024]{1,0:T(8,128)(2,1)} %down_weight.1), custom_call_target="tpu_custom_call" | custom-call | tf_op jit(solution)/shard_map/block/pallas_call | solution.py:911
  81.4 2.3 %store.1 = (bf16[256,512]{1,0:T(8,128)(2,1)}, f32[1024,128]{1,0:T(8,128)}, f32[1024,128]{1,0:T(8,128)}, f32[128,1024]{1,0:T(8,128)}) custom-call(bf16[256,512]{1,0:T(8,128)(2,1)} %get-tuple-element.8.refs_0_, f32[1024,128]{1,0:T(8,128)} %get-tuple-element.9.refs_1_, f32[1024,128]{1,0:T(8,128)} %get-tuple-element.10.refs_2_, ...), custom_call_target="tpu_custom_call" | custom-call | tf_op jit(solution)/shard_map/store/pallas_call | solution.py:991

commit v13 on v12

--- a/solution.py
+++ b/solution.py
@@ -586,7 +586,7 @@
             twos[i].at[halves(i, q)],
             mids[i].at[q],
             two_send.at[i],
-            two_recv.at[i, q],
+            two_recv.at[i],
             at(x, beside(q), h, l, k),
         )
 
@@ -616,8 +616,8 @@
         )
 
     def one_merge(i):
+        remote(mids[i], mids[i], two_send.at[i], two_recv.at[i], north).wait_recv()
         for way in range(2):
-            two_out(i, way).wait_recv()
             ones[i][way, halves(i, way)] = (
                 parts[i][way] + mids[i][way].astype(F32)
             ).astype(BF16)
@@ -831,10 +831,11 @@
     def _():
         keeps[3].start()
 
-    both = factor * (gown[...] + finals(1))
-    gate_own[...] = both[:, :width]
-    up_own[...] = both[:, width:]
-    for copy in keeps[:3]:
+    keeps[0].start()
+    last = finals(1)
+    gate_own[...] = factor * (gown[:, :width] + last[:, :width])
+    up_own[...] = factor * (gown[:, width:] + last[:, width:])
+    for copy in keeps[1:3]:
         copy.start()
 
     sent = [
@@ -975,7 +976,7 @@
                 DMA(()),
                 DMA((4, 2)),
                 DMA((2,)),
-                DMA((2, 2)),
+                DMA((2,)),
                 DMA((2,)),
                 DMA((2,)),
                 DMA(()),

time: 84.1 us -> 84 us (level)
  no operation moved by 1% of the time
where the time goes in v13:
time: 84 us; the launch traced here: 83.7 us
  Pallas kernels  83 us (99%)
    pallas_call x1, Pallas kernels, body(): pl.pallas_call(functools.partial(kernel, factor), out_shape=shapes, in_sp...  80.7 us
    pallas_call x1, Pallas kernels, body(): pl.pallas_call(store_kernel, out_shape=shapes, in_specs=[HBM] * 4, out_sp...  2.33 us

profile of v13, /device:TPU:32, one launch (start us, length us, event | category | flops | bytes accessed | tf_op | source)
XLA Modules:
  0.0 83.7 jit_solution(8409855896633280227)
XLA Ops:
  0.6 80.7 %block.1 = (bf16[256,512]{1,0:T(8,128)(2,1)}, f32[1024,128]{1,0:T(8,128)}, f32[1024,128]{1,0:T(8,128)}, f32[128,1024]{1,0:T(8,128)}) custom-call(bf16[256,512]{1,0:T(8,128)(2,1)} %tokens.1, bf16[256,512]{1,0:T(8,128)(2,1)} %grads.1, bf16[1024,128]{1,0:T(8,128)(2,1)} %gate_weight.1, bf16[1024,128]{1,0:T(8,128)(2,1)} %up_weight.1, bf16[128,1024]{1,0:T(8,128)(2,1)} %down_weight.1), custom_call_target="tpu_custom_call" | custom-call | tf_op jit(solution)/shard_map/block/pallas_call | solution.py:912
  81.3 2.3 %store.1 = (bf16[256,512]{1,0:T(8,128)(2,1)}, f32[1024,128]{1,0:T(8,128)}, f32[1024,128]{1,0:T(8,128)}, f32[128,1024]{1,0:T(8,128)}) custom-call(bf16[256,512]{1,0:T(8,128)(2,1)} %get-tuple-element.8.refs_0_, f32[1024,128]{1,0:T(8,128)} %get-tuple-element.9.refs_1_, f32[1024,128]{1,0:T(8,128)} %get-tuple-element.10.refs_2_, ...), custom_call_target="tpu_custom_call" | custom-call | tf_op jit(solution)/shard_map/store/pallas_call | solution.py:992

commit v14 on v13

--- a/solution.py
+++ b/solution.py
@@ -657,13 +657,13 @@
     two_out(0, k).start()
     pair_in(2, 1)
     grad_last(0)
+    dtwo[1 - k] = down_half(ys[2], 1 - k).astype(BF16)
+    b_swap(0).start()
     grad_last(1)
-    b_swap(0).start()
-    dtwo[1 - k] = down_half(ys[2], 1 - k).astype(BF16)
-    b_swap(1).start()
-    done[k, 1 - k] = down_half(beside(k), 1 - k).astype(BF16)
     two_out(0, 1 - k).start()
     one_out(0, 1 - k, k).start()
+    done[k, 1 - k] = down_half(beside(k), 1 - k).astype(BF16)
+    b_swap(1).start()
     dpart[k] = down_half(beside(k), k)
     one_out(0, k, 1 - k).start()
     dpart[1 - k] = down_half(beside(1 - k), 1 - k)

time: 84 us -> 83.9 us (level)
  no operation moved by 1% of the time
where the time goes in v14:
time: 83.9 us; the launch traced here: 83 us
  Pallas kernels  82.4 us (98%)
    pallas_call x1, Pallas kernels, body(): pl.pallas_call(functools.partial(kernel, factor), out_shape=shapes, in_sp...  80 us
    pallas_call x1, Pallas kernels, body(): pl.pallas_call(store_kernel, out_shape=shapes, in_specs=[HBM] * 4, out_sp...  2.33 us

profile of v14, /device:TPU:32, one launch (start us, length us, event | category | flops | bytes accessed | tf_op | source)
XLA Modules:
  0.0 83.0 jit_solution(9257856537730366936)
XLA Ops:
  0.6 80.0 %block.1 = (bf16[256,512]{1,0:T(8,128)(2,1)}, f32[1024,128]{1,0:T(8,128)}, f32[1024,128]{1,0:T(8,128)}, f32[128,1024]{1,0:T(8,128)}) custom-call(bf16[256,512]{1,0:T(8,128)(2,1)} %tokens.1, bf16[256,512]{1,0:T(8,128)(2,1)} %grads.1, bf16[1024,128]{1,0:T(8,128)(2,1)} %gate_weight.1, bf16[1024,128]{1,0:T(8,128)(2,1)} %up_weight.1, bf16[128,1024]{1,0:T(8,128)(2,1)} %down_weight.1), custom_call_target="tpu_custom_call" | custom-call | tf_op jit(solution)/shard_map/block/pallas_call | solution.py:912
  80.7 2.3 %store.1 = (bf16[256,512]{1,0:T(8,128)(2,1)}, f32[1024,128]{1,0:T(8,128)}, f32[1024,128]{1,0:T(8,128)}, f32[128,1024]{1,0:T(8,128)}) custom-call(bf16[256,512]{1,0:T(8,128)(2,1)} %get-tuple-element.8.refs_0_, f32[1024,128]{1,0:T(8,128)} %get-tuple-element.9.refs_1_, f32[1024,128]{1,0:T(8,128)} %get-tuple-element.10.refs_2_, ...), custom_call_target="tpu_custom_call" | custom-call | tf_op jit(solution)/shard_map/store/pallas_call | solution.py:992

commit v15 on v14

--- a/solution.py
+++ b/solution.py
@@ -505,10 +505,12 @@
         term = jnp.dot(block(0, o), weights, preferred_element_type=F32)
         sa[...] = term if d == 3 else sa[...] + term
 
-    for d in (3, 0, 1):
+    for d in (3, 0):
         pair_in(d, 0)
         gate_up(d)
     x_rest(0)
+    pair_in(1, 0)
+    gate_up(1)
     pair_in(2, 0)
     gate_up(2)
     turn = (1 - l, l)

time: 83.9 us -> 83.9 us (level)
  no operation moved by 1% of the time
where the time goes in v15:
time: 83.9 us; the launch traced here: 83.5 us
  Pallas kernels  82.9 us (99%)
    pallas_call x1, Pallas kernels, body(): pl.pallas_call(functools.partial(kernel, factor), out_shape=shapes, in_sp...  80.5 us
    pallas_call x1, Pallas kernels, body(): pl.pallas_call(store_kernel, out_shape=shapes, in_specs=[HBM] * 4, out_sp...  2.33 us

profile of v15, /device:TPU:32, one launch (start us, length us, event | category | flops | bytes accessed | tf_op | source)
XLA Modules:
  0.0 83.5 jit_solution(17012091787283743781)
XLA Ops:
  0.6 80.5 %block.1 = (bf16[256,512]{1,0:T(8,128)(2,1)}, f32[1024,128]{1,0:T(8,128)}, f32[1024,128]{1,0:T(8,128)}, f32[128,1024]{1,0:T(8,128)}) custom-call(bf16[256,512]{1,0:T(8,128)(2,1)} %tokens.1, bf16[256,512]{1,0:T(8,128)(2,1)} %grads.1, bf16[1024,128]{1,0:T(8,128)(2,1)} %gate_weight.1, bf16[1024,128]{1,0:T(8,128)(2,1)} %up_weight.1, bf16[128,1024]{1,0:T(8,128)(2,1)} %down_weight.1), custom_call_target="tpu_custom_call" | custom-call | tf_op jit(solution)/shard_map/block/pallas_call | solution.py:914
  81.2 2.3 %store.1 = (bf16[256,512]{1,0:T(8,128)(2,1)}, f32[1024,128]{1,0:T(8,128)}, f32[1024,128]{1,0:T(8,128)}, f32[128,1024]{1,0:T(8,128)}) custom-call(bf16[256,512]{1,0:T(8,128)(2,1)} %get-tuple-element.8.refs_0_, f32[1024,128]{1,0:T(8,128)} %get-tuple-element.9.refs_1_, f32[1024,128]{1,0:T(8,128)} %get-tuple-element.10.refs_2_, ...), custom_call_target="tpu_custom_call" | custom-call | tf_op jit(solution)/shard_map/store/pallas_call | solution.py:994
